TPU v7x, 32 devices: a whole 2x2x4 slice. The times are simulated.
32 devices in a mesh: gx: 4 (over y, x), gy: 8 (over z, core).
Axes of the slice: x: 2, y: 2, z: 4, core: 2. Of those that a mesh axis runs over, the one named last changes fastest.
Arguments:
- density: float32 [16, 256, 1024], P(None, 'gx', 'gy'), may hold values from 0.1 to 1
- cotangent: float32 [16, 256, 1024], P(None, 'gx', 'gy'), may hold values from -6 to 6
Outputs:
- printed: float32 [16, 256, 1024], P(None, 'gx', 'gy')
- gradient: float32 [16, 256, 1024], P(None, 'gx', 'gy')
All inputs are finite; a program needn't handle non-finite values.
Results may differ from a plain program's by a relative error of at most 0.0003.
Values sent between devices are 32-bit elements; how exact they have to be, the bound alone decides.
No kernel may reach another device: no remote copies, remote signals or barrier semaphores. Data moves between devices by JAX's collectives and lax.ppermute only.
A program may use at most 64 MiB of HBM per device.

v0:
```python
import math

import jax
import jax.numpy as jnp
from jax import lax
from jax.sharding import PartitionSpec as P

power_p = 20.0
root_q = 20.0 + math.log(5.0) / math.log(0.1)
smooth_eps = 0.0001


def with_halo(block, sides, width):
    for axis, dim in sides:
        count = lax.axis_size(axis)
        forward = [(i, i + 1) for i in range(count - 1)]
        forward.append((count - 1, 0))
        backward = [(target, source) for source, target in forward]
        low = lax.ppermute(
            lax.slice_in_dim(block, block.shape[dim] - width, None, axis=dim), axis, forward
        )
        high = lax.ppermute(lax.slice_in_dim(block, 0, width, axis=dim), axis, backward)
        block = jnp.concatenate([low, block, high], axis=dim)
    return block


def cross(plane):
    return (
        plane[1:-1, 1:-1] + plane[2:, 1:-1] + plane[:-2, 1:-1] + plane[1:-1, 2:] + plane[1:-1, :-2]
    )


def trim(plane, cells):
    if cells == 0:
        return plane
    return plane[cells : plane.shape[0] - cells, cells : plane.shape[1] - cells]


def forward_block(dens_pad, prev_pad, first, depth):
    prev = prev_pad
    layers = []
    for step in range(depth):
        total = cross(prev**power_p)
        level = jnp.where(first + step == 0, jnp.float32(1.0), total ** (1.0 / root_q))
        plane = trim(dens_pad[step], step + 1)
        diff = plane - level
        printed_layer = 0.5 * (
            plane + level - jnp.sqrt(diff * diff + smooth_eps) + math.sqrt(smooth_eps)
        )
        layers.append(trim(printed_layer, depth - step - 1))
        prev = printed_layer
    return (jnp.stack(layers), prev)


def backward_block(grad_pad, dens_pad, print_pad, state_pad, first, depth):
    carried = state_pad
    grads = [None] * depth
    for step in range(depth):
        local = depth - 1 - step
        width = depth - 1 - step
        spread = cross(carried)
        here = trim(print_pad[local + 1], depth - width)
        adjoint = (
            trim(grad_pad[local], depth - width)
            + power_p / root_q * here ** (power_p - 1.0) * spread
        )
        under = trim(print_pad[local], depth - width - 1)
        total = cross(under**power_p)
        level = jnp.where(first + local == 0, jnp.float32(1.0), total ** (1.0 / root_q))
        diff = trim(dens_pad[local], depth - width) - level
        root = jnp.sqrt(diff * diff + smooth_eps)
        grads[local] = trim(adjoint * 0.5 * (1.0 - diff / root), width)
        carried = adjoint * 0.5 * (1.0 + diff / root) * level / total
    return (jnp.stack(grads), carried)


def shards(density, cotangent):
    depth = 8
    layers_all = density.shape[0]
    blocks = layers_all // depth
    plane_shape = density.shape[1:]
    ones_layer = jnp.ones(plane_shape, jnp.float32)

    def forward_step(index, carry):
        printed_all, prev = carry
        first = index * depth
        dens_block = lax.dynamic_slice_in_dim(density, first, depth, 0)
        dens_pad, prev_wide = (
            with_halo(dens_block, (("gx", 1), ("gy", 2)), depth),
            with_halo(prev[None], (("gx", 1), ("gy", 2)), depth),
        )
        prev_pad = prev_wide[0]
        block, last = forward_block(dens_pad, prev_pad, first, depth)
        printed_all = lax.dynamic_update_slice_in_dim(printed_all, block, first, 0)
        return (printed_all, last)

    printed, final_layer = lax.fori_loop(
        0, blocks, forward_step, (jnp.zeros_like(density), ones_layer)
    )
    print_ext = jnp.concatenate([ones_layer[None], printed], 0)

    def backward_step(index, carry):
        gradient_all, carried = carry
        first = (blocks - 1 - index) * depth
        grad_block = lax.dynamic_slice_in_dim(cotangent, first, depth, 0)
        dens_block = lax.dynamic_slice_in_dim(density, first, depth, 0)
        print_block = lax.dynamic_slice_in_dim(print_ext, first, depth + 1, 0)
        grad_pad, dens_pad, print_pad, state_wide = (
            with_halo(grad_block, (("gx", 1), ("gy", 2)), depth),
            with_halo(dens_block, (("gx", 1), ("gy", 2)), depth),
            with_halo(print_block, (("gx", 1), ("gy", 2)), depth),
            with_halo(carried[None], (("gx", 1), ("gy", 2)), depth),
        )
        state_pad = state_wide[0]
        block, carried_next = backward_block(grad_pad, dens_pad, print_pad, state_pad, first, depth)
        gradient_all = lax.dynamic_update_slice_in_dim(gradient_all, block, first, 0)
        return (gradient_all, carried_next)

    gradient, final_state = lax.fori_loop(
        0, blocks, backward_step, (jnp.zeros_like(density), jnp.zeros(plane_shape, jnp.float32))
    )
    return (printed, gradient)


def solution(mesh):
    placed = (P(None, "gx", "gy"), P(None, "gx", "gy"))
    return jax.shard_map(
        shards,
        mesh=mesh,
        in_specs=placed,
        out_specs=(P(None, "gx", "gy"), P(None, "gx", "gy")),
        check_vma=False,
    )
```

profile of v0, /device:TPU:0, one launch (start us, length us, event | category | flops | bytes accessed | tf_op | source)
XLA Modules:
  0.0 147.3 jit_solution(10353710206916408079)
XLA Ops:
  1.7 51.4 %while.32 = (s32[]{:T(128)}, f32[16,64,128]{2,1,0:T(8,128)S(1)}, f32[64,128]{1,0:T(8,128)S(1)}, f32[16,64,128]{2,1,0:T(8,128)S(1)}, s32[]{:T(128)}, /*index=5*/s...) while((s32[]{:T(128)}, f32[16,64,128]{2,1,0:T(8,128)S(1)}, ...), condition=%wide.region_1.2_spmd.clone, body=%wide.region_0.1_spmd.clone.sunk | while | flops 1529431 | bytes 7055557 | solution.py:97
  1.7 4.0 %collective-permute-start.4 = (f32[8,8,128]{2,1,0:T(8,128)S(1)}, f32[8,8,128]{2,1,0:T(8,128)S(1)}, u32[]{:S(2)}, u32[]{:S(2)}) collective-permute-start(f32[8,8,128]{2,1,0:T(8,128)S(1)} %get-tuple-element.520), channel_id=1, source_target_pairs={{8,0},{16,8},{24,16},{0,24},{9,1},{17,9},{25,17},{1,25},{10,2},{18... | collective-permute-start | bytes 98312 | tf_op jit(solution)/shard_map/while/body/eval_jaxpr/ppermute | solution.py:22
  5.7 3.0 %collective-permute-start = (f32[1,8,128]{2,1,0:T(8,128)S(1)}, f32[1,8,128]{2,1,0:T(8,128)S(1)}, u32[]{:S(2)}, u32[]{:S(2)}) collective-permute-start(f32[1,8,128]{2,1,0:T(8,128)S(1)} %get-tuple-element.516), channel_id=1, source_target_pairs={{8,0},{16,8},{24,16},{0,24},{9,1},{17,9},{25,17},{1,25},{10,2},{18... | collective-permute-start | bytes 12296 | tf_op jit(solution)/shard_map/while/body/eval_jaxpr/ppermute | solution.py:22
  8.7 1.3 collective-permute-done
  10.0 3.2 %collective-permute-done.1 = f32[1,8,128]{2,1,0:T(8,128)S(1)} collective-permute-done((f32[1,8,128]{2,1,0:T(8,128)S(1)}, f32[1,8,128]{2,1,0:T(8,128)S(1)}, u32[]{:S(2)}, u32[]{:S(2)}) %collective-permute-start.1) | collective-permute-done | bytes 4128 | tf_op jit(solution)/shard_map/while/body/eval_jaxpr/ppermute | solution.py:19
  14.5 3.6 %collective-permute-start.6 = (f32[8,80,8]{2,1,0:T(8,128)S(1)}, f32[8,80,8]{2,1,0:T(8,128)S(1)}, u32[]{:S(2)}, u32[]{:S(2)}) collective-permute-start(f32[8,80,8]{2,1,0:T(8,128)S(1)} %get-tuple-element.522), channel_id=1, source_target_pairs={{1,0},{2,1},{3,2},{4,3},{5,4},{6,5},{7,6},{0,7},{9,8},{10,9},{11,1... | collective-permute-start | bytes 61448 | tf_op jit(solution)/shard_map/while/body/eval_jaxpr/ppermute | solution.py:22
  18.1 1.5 %collective-permute-done.3 = f32[1,80,8]{2,1,0:T(8,128)S(1)} collective-permute-done((f32[1,80,8]{2,1,0:T(8,128)S(1)}, f32[1,80,8]{2,1,0:T(8,128)S(1)}, u32[]{:S(2)}, u32[]{:S(2)}) %collective-permute-start.3) | collective-permute-done | bytes 2592 | tf_op jit(solution)/shard_map/while/body/eval_jaxpr/ppermute | solution.py:19
  19.7 4.7 %collective-permute-done.6 = f32[8,80,8]{2,1,0:T(8,128)S(1)} collective-permute-done((f32[8,80,8]{2,1,0:T(8,128)S(1)}, f32[8,80,8]{2,1,0:T(8,128)S(1)}, u32[]{:S(2)}, u32[]{:S(2)}) %collective-permute-start.6) | collective-permute-done | bytes 20512 | tf_op jit(solution)/shard_map/while/body/eval_jaxpr/ppermute | solution.py:22
  24.4 3.0 %collective-permute-done.7 = f32[8,80,8]{2,1,0:T(8,128)S(1)} collective-permute-done((f32[8,80,8]{2,1,0:T(8,128)S(1)}, f32[8,80,8]{2,1,0:T(8,128)S(1)}, u32[]{:S(2)}, u32[]{:S(2)}) %collective-permute-start.7) | collective-permute-done | bytes 20512 | tf_op jit(solution)/shard_map/while/body/eval_jaxpr/ppermute | solution.py:19
  30.3 2.0 %collective-permute-start.5 = (f32[8,8,128]{2,1,0:T(8,128)S(1)}, f32[8,8,128]{2,1,0:T(8,128)S(1)}, u32[]{:S(2)}, u32[]{:S(2)}) collective-permute-start(f32[8,8,128]{2,1,0:T(8,128)S(1)} %get-tuple-element.521), channel_id=1, source_target_pairs={{0,8},{8,16},{16,24},{24,0},{1,9},{9,17},{17,25},{25,1},{2,10},{10... | collective-permute-start | bytes 98312 | tf_op jit(solution)/shard_map/while/body/eval_jaxpr/ppermute | solution.py:19
  33.4 1.1 collective-permute-start.1
  34.5 1.5 %collective-permute-done = f32[1,8,128]{2,1,0:T(8,128)S(1)} collective-permute-done((f32[1,8,128]{2,1,0:T(8,128)S(1)}, f32[1,8,128]{2,1,0:T(8,128)S(1)}, u32[]{:S(2)}, u32[]{:S(2)}) %collective-permute-start) | collective-permute-done | bytes 4128 | tf_op jit(solution)/shard_map/while/body/eval_jaxpr/ppermute | solution.py:22
  36.0 1.9 %collective-permute-done.1 = f32[1,8,128]{2,1,0:T(8,128)S(1)} collective-permute-done((f32[1,8,128]{2,1,0:T(8,128)S(1)}, f32[1,8,128]{2,1,0:T(8,128)S(1)}, u32[]{:S(2)}, u32[]{:S(2)}) %collective-permute-start.1) | collective-permute-done | bytes 4128 | tf_op jit(solution)/shard_map/while/body/eval_jaxpr/ppermute | solution.py:19
  38.7 3.1 %collective-permute-start.6 = (f32[8,80,8]{2,1,0:T(8,128)S(1)}, f32[8,80,8]{2,1,0:T(8,128)S(1)}, u32[]{:S(2)}, u32[]{:S(2)}) collective-permute-start(f32[8,80,8]{2,1,0:T(8,128)S(1)} %get-tuple-element.522), channel_id=1, source_target_pairs={{1,0},{2,1},{3,2},{4,3},{5,4},{6,5},{7,6},{0,7},{9,8},{10,9},{11,1... | collective-permute-start | bytes 61448 | tf_op jit(solution)/shard_map/while/body/eval_jaxpr/ppermute | solution.py:22
  41.8 1.7 %collective-permute-done.3 = f32[1,80,8]{2,1,0:T(8,128)S(1)} collective-permute-done((f32[1,80,8]{2,1,0:T(8,128)S(1)}, f32[1,80,8]{2,1,0:T(8,128)S(1)}, u32[]{:S(2)}, u32[]{:S(2)}) %collective-permute-start.3) | collective-permute-done | bytes 2592 | tf_op jit(solution)/shard_map/while/body/eval_jaxpr/ppermute | solution.py:19
  43.6 4.3 %collective-permute-done.6 = f32[8,80,8]{2,1,0:T(8,128)S(1)} collective-permute-done((f32[8,80,8]{2,1,0:T(8,128)S(1)}, f32[8,80,8]{2,1,0:T(8,128)S(1)}, u32[]{:S(2)}, u32[]{:S(2)}) %collective-permute-start.6) | collective-permute-done | bytes 20512 | tf_op jit(solution)/shard_map/while/body/eval_jaxpr/ppermute | solution.py:22
  47.9 2.4 %collective-permute-done.7 = f32[8,80,8]{2,1,0:T(8,128)S(1)} collective-permute-done((f32[8,80,8]{2,1,0:T(8,128)S(1)}, f32[8,80,8]{2,1,0:T(8,128)S(1)}, u32[]{:S(2)}, u32[]{:S(2)}) %collective-permute-start.7) | collective-permute-done | bytes 20512 | tf_op jit(solution)/shard_map/while/body/eval_jaxpr/ppermute | solution.py:19
  54.9 91.6 %while.33 = (s32[]{:T(128)}, f32[16,64,128]{2,1,0:T(8,128)S(1)}, f32[64,128]{1,0:T(8,128)S(1)}, f32[16,64,128]{2,1,0:T(8,128)S(1)}, f32[17,64,128]{2,1,0:T(8,128...) while((s32[]{:T(128)}, f32[16,64,128]{2,1,0:T(8,128)S(1)}, ...), condition=%wide.region_3.4_spmd.clone, body=%wide.region_2.3_spmd.clone.sunk | while | flops 3867897 | bytes 18338844 | solution.py:119
  55.1 1.9 %collective-permute-start.13 = (f32[9,8,128]{2,1,0:T(8,128)S(1)}, f32[9,8,128]{2,1,0:T(8,128)S(1)}, u32[]{:S(2)}, u32[]{:S(2)}) collective-permute-start(f32[9,8,128]{2,1,0:T(8,128)S(1)} %get-tuple-element.561), channel_id=1, source_target_pairs={{0,8},{8,16},{16,24},{24,0},{1,9},{9,17},{17,25},{25,1},{2,10},{10... | collective-permute-start | bytes 110600 | tf_op jit(solution)/shard_map/while/body/eval_jaxpr/ppermute | solution.py:19
  60.2 1.5 %collective-permute-done.16 = f32[1,8,128]{2,1,0:T(8,128)S(1)} collective-permute-done((f32[1,8,128]{2,1,0:T(8,128)S(1)}, f32[1,8,128]{2,1,0:T(8,128)S(1)}, u32[]{:S(2)}, u32[]{:S(2)}) %collective-permute-start.16) | collective-permute-done | bytes 4128 | tf_op jit(solution)/shard_map/while/body/eval_jaxpr/ppermute | solution.py:22
  61.7 1.9 %collective-permute-done.17 = f32[1,8,128]{2,1,0:T(8,128)S(1)} collective-permute-done((f32[1,8,128]{2,1,0:T(8,128)S(1)}, f32[1,8,128]{2,1,0:T(8,128)S(1)}, u32[]{:S(2)}, u32[]{:S(2)}) %collective-permute-start.17) | collective-permute-done | bytes 4128 | tf_op jit(solution)/shard_map/while/body/eval_jaxpr/ppermute | solution.py:19
  64.2 1.2 collective-permute-done.18
  65.6 3.4 %collective-permute-done.19 = f32[1,80,8]{2,1,0:T(8,128)S(1)} collective-permute-done((f32[1,80,8]{2,1,0:T(8,128)S(1)}, f32[1,80,8]{2,1,0:T(8,128)S(1)}, u32[]{:S(2)}, u32[]{:S(2)}) %collective-permute-start.19) | collective-permute-done | bytes 2592 | tf_op jit(solution)/shard_map/while/body/eval_jaxpr/ppermute | solution.py:19
  69.0 1.1 collective-permute-start.20
  71.4 1.7 %collective-permute-start.10 = (f32[8,80,8]{2,1,0:T(8,128)S(1)}, f32[8,80,8]{2,1,0:T(8,128)S(1)}, u32[]{:S(2)}, u32[]{:S(2)}) collective-permute-start(f32[8,80,8]{2,1,0:T(8,128)S(1)} %get-tuple-element.557), channel_id=1, source_target_pairs={{1,0},{2,1},{3,2},{4,3},{5,4},{6,5},{7,6},{0,7},{9,8},{10,9},{11,1... | collective-permute-start | bytes 61448 | tf_op jit(solution)/shard_map/while/body/eval_jaxpr/ppermute | solution.py:22
  73.1 1.9 %collective-permute-done.21 = f32[8,8,128]{2,1,0:T(8,128)S(1)} collective-permute-done((f32[8,8,128]{2,1,0:T(8,128)S(1)}, f32[8,8,128]{2,1,0:T(8,128)S(1)}, u32[]{:S(2)}, u32[]{:S(2)}) %collective-permute-start.21) | collective-permute-done | bytes 32800 | tf_op jit(solution)/shard_map/while/body/eval_jaxpr/ppermute | solution.py:19
  75.2 1.7 %collective-permute-start.22 = (f32[8,80,8]{2,1,0:T(8,128)S(1)}, f32[8,80,8]{2,1,0:T(8,128)S(1)}, u32[]{:S(2)}, u32[]{:S(2)}) collective-permute-start(f32[8,80,8]{2,1,0:T(8,128)S(1)} %get-tuple-element.593), channel_id=1, source_target_pairs={{1,0},{2,1},{3,2},{4,3},{5,4},{6,5},{7,6},{0,7},{9,8},{10,9},{11,1... | collective-permute-start | bytes 61448 | tf_op jit(solution)/shard_map/while/body/eval_jaxpr/ppermute | solution.py:22
  77.1 3.6 %collective-permute-start.14 = (f32[9,80,8]{2,1,0:T(8,128)S(1)}, f32[9,80,8]{2,1,0:T(8,128)S(1)}, u32[]{:S(2)}, u32[]{:S(2)}) collective-permute-start(f32[9,80,8]{2,1,0:T(8,128)S(1)} %get-tuple-element.562), channel_id=1, source_target_pairs={{1,0},{2,1},{3,2},{4,3},{5,4},{6,5},{7,6},{0,7},{9,8},{10,9},{11,1... | collective-permute-start | bytes 69128 | tf_op jit(solution)/shard_map/while/body/eval_jaxpr/ppermute | solution.py:22
  81.2 3.7 %collective-permute-done.11 = f32[8,80,8]{2,1,0:T(8,128)S(1)} collective-permute-done((f32[8,80,8]{2,1,0:T(8,128)S(1)}, f32[8,80,8]{2,1,0:T(8,128)S(1)}, u32[]{:S(2)}, u32[]{:S(2)}) %collective-permute-start.11) | collective-permute-done | bytes 20512 | tf_op jit(solution)/shard_map/while/body/eval_jaxpr/ppermute | solution.py:19
  85.3 2.9 %collective-permute-done.22 = f32[8,80,8]{2,1,0:T(8,128)S(1)} collective-permute-done((f32[8,80,8]{2,1,0:T(8,128)S(1)}, f32[8,80,8]{2,1,0:T(8,128)S(1)}, u32[]{:S(2)}, u32[]{:S(2)}) %collective-permute-start.22) | collective-permute-done | bytes 20512 | tf_op jit(solution)/shard_map/while/body/eval_jaxpr/ppermute | solution.py:22
  88.2 2.1 %collective-permute-done.23 = f32[8,80,8]{2,1,0:T(8,128)S(1)} collective-permute-done((f32[8,80,8]{2,1,0:T(8,128)S(1)}, f32[8,80,8]{2,1,0:T(8,128)S(1)}, u32[]{:S(2)}, u32[]{:S(2)}) %collective-permute-start.23) | collective-permute-done | bytes 20512 | tf_op jit(solution)/shard_map/while/body/eval_jaxpr/ppermute | solution.py:19
  90.7 3.6 %collective-permute-done.14 = f32[9,80,8]{2,1,0:T(8,128)S(1)} collective-permute-done((f32[9,80,8]{2,1,0:T(8,128)S(1)}, f32[9,80,8]{2,1,0:T(8,128)S(1)}, u32[]{:S(2)}, u32[]{:S(2)}) %collective-permute-start.14) | collective-permute-done | bytes 23072 | tf_op jit(solution)/shard_map/while/body/eval_jaxpr/ppermute | solution.py:22
  99.4 2.0 %collective-permute-start.12 = (f32[9,8,128]{2,1,0:T(8,128)S(1)}, f32[9,8,128]{2,1,0:T(8,128)S(1)}, u32[]{:S(2)}, u32[]{:S(2)}) collective-permute-start(f32[9,8,128]{2,1,0:T(8,128)S(1)} %get-tuple-element.560), channel_id=1, source_target_pairs={{8,0},{16,8},{24,16},{0,24},{9,1},{17,9},{25,17},{1,25},{10,2},{18... | collective-permute-start | bytes 110600 | tf_op jit(solution)/shard_map/while/body/eval_jaxpr/ppermute | solution.py:22
  101.5 2.9 %collective-permute-start.8 = (f32[8,8,128]{2,1,0:T(8,128)S(1)}, f32[8,8,128]{2,1,0:T(8,128)S(1)}, u32[]{:S(2)}, u32[]{:S(2)}) collective-permute-start(f32[8,8,128]{2,1,0:T(8,128)S(1)} %get-tuple-element.554), channel_id=1, source_target_pairs={{8,0},{16,8},{24,16},{0,24},{9,1},{17,9},{25,17},{1,25},{10,2},{18... | collective-permute-start | bytes 98312 | tf_op jit(solution)/shard_map/while/body/eval_jaxpr/ppermute | solution.py:22
  104.6 2.0 %collective-permute-start.17 = (f32[1,8,128]{2,1,0:T(8,128)S(1)}, f32[1,8,128]{2,1,0:T(8,128)S(1)}, u32[]{:S(2)}, u32[]{:S(2)}) collective-permute-start(f32[1,8,128]{2,1,0:T(8,128)S(1)} %get-tuple-element.586), channel_id=1, source_target_pairs={{0,8},{8,16},{16,24},{24,0},{1,9},{9,17},{17,25},{25,1},{2,10},{10... | collective-permute-start | bytes 12296 | tf_op jit(solution)/shard_map/while/body/eval_jaxpr/ppermute | solution.py:19
  106.6 1.5 %collective-permute-done.16 = f32[1,8,128]{2,1,0:T(8,128)S(1)} collective-permute-done((f32[1,8,128]{2,1,0:T(8,128)S(1)}, f32[1,8,128]{2,1,0:T(8,128)S(1)}, u32[]{:S(2)}, u32[]{:S(2)}) %collective-permute-start.16) | collective-permute-done | bytes 4128 | tf_op jit(solution)/shard_map/while/body/eval_jaxpr/ppermute | solution.py:22
  109.2 1.7 %collective-permute-start.18 = (f32[1,80,8]{2,1,0:T(8,128)S(1)}, f32[1,80,8]{2,1,0:T(8,128)S(1)}, u32[]{:S(2)}, u32[]{:S(2)}) collective-permute-start(f32[1,80,8]{2,1,0:T(8,128)S(1)} %get-tuple-element.587), channel_id=1, source_target_pairs={{1,0},{2,1},{3,2},{4,3},{5,4},{6,5},{7,6},{0,7},{9,8},{10,9},{11,1... | collective-permute-start | bytes 7688 | tf_op jit(solution)/shard_map/while/body/eval_jaxpr/ppermute | solution.py:22
  110.9 1.6 %collective-permute-done.18 = f32[1,80,8]{2,1,0:T(8,128)S(1)} collective-permute-done((f32[1,80,8]{2,1,0:T(8,128)S(1)}, f32[1,80,8]{2,1,0:T(8,128)S(1)}, u32[]{:S(2)}, u32[]{:S(2)}) %collective-permute-start.18) | collective-permute-done | bytes 2592 | tf_op jit(solution)/shard_map/while/body/eval_jaxpr/ppermute | solution.py:22
  113.3 2.8 %collective-permute-done.19 = f32[1,80,8]{2,1,0:T(8,128)S(1)} collective-permute-done((f32[1,80,8]{2,1,0:T(8,128)S(1)}, f32[1,80,8]{2,1,0:T(8,128)S(1)}, u32[]{:S(2)}, u32[]{:S(2)}) %collective-permute-start.19) | collective-permute-done | bytes 2592 | tf_op jit(solution)/shard_map/while/body/eval_jaxpr/ppermute | solution.py:19
  116.9 1.4 collective-permute-start.21
  118.5 1.5 %collective-permute-start.10 = (f32[8,80,8]{2,1,0:T(8,128)S(1)}, f32[8,80,8]{2,1,0:T(8,128)S(1)}, u32[]{:S(2)}, u32[]{:S(2)}) collective-permute-start(f32[8,80,8]{2,1,0:T(8,128)S(1)} %get-tuple-element.557), channel_id=1, source_target_pairs={{1,0},{2,1},{3,2},{4,3},{5,4},{6,5},{7,6},{0,7},{9,8},{10,9},{11,1... | collective-permute-start | bytes 61448 | tf_op jit(solution)/shard_map/while/body/eval_jaxpr/ppermute | solution.py:22
  120.0 1.8 %collective-permute-done.21 = f32[8,8,128]{2,1,0:T(8,128)S(1)} collective-permute-done((f32[8,8,128]{2,1,0:T(8,128)S(1)}, f32[8,8,128]{2,1,0:T(8,128)S(1)}, u32[]{:S(2)}, u32[]{:S(2)}) %collective-permute-start.21) | collective-permute-done | bytes 32800 | tf_op jit(solution)/shard_map/while/body/eval_jaxpr/ppermute | solution.py:19
  122.0 1.8 %collective-permute-start.22 = (f32[8,80,8]{2,1,0:T(8,128)S(1)}, f32[8,80,8]{2,1,0:T(8,128)S(1)}, u32[]{:S(2)}, u32[]{:S(2)}) collective-permute-start(f32[8,80,8]{2,1,0:T(8,128)S(1)} %get-tuple-element.593), channel_id=1, source_target_pairs={{1,0},{2,1},{3,2},{4,3},{5,4},{6,5},{7,6},{0,7},{9,8},{10,9},{11,1... | collective-permute-start | bytes 61448 | tf_op jit(solution)/shard_map/while/body/eval_jaxpr/ppermute | solution.py:22
  124.0 3.6 %collective-permute-start.14 = (f32[9,80,8]{2,1,0:T(8,128)S(1)}, f32[9,80,8]{2,1,0:T(8,128)S(1)}, u32[]{:S(2)}, u32[]{:S(2)}) collective-permute-start(f32[9,80,8]{2,1,0:T(8,128)S(1)} %get-tuple-element.562), channel_id=1, source_target_pairs={{1,0},{2,1},{3,2},{4,3},{5,4},{6,5},{7,6},{0,7},{9,8},{10,9},{11,1... | collective-permute-start | bytes 69128 | tf_op jit(solution)/shard_map/while/body/eval_jaxpr/ppermute | solution.py:22
  128.1 3.7 %collective-permute-done.11 = f32[8,80,8]{2,1,0:T(8,128)S(1)} collective-permute-done((f32[8,80,8]{2,1,0:T(8,128)S(1)}, f32[8,80,8]{2,1,0:T(8,128)S(1)}, u32[]{:S(2)}, u32[]{:S(2)}) %collective-permute-start.11) | collective-permute-done | bytes 20512 | tf_op jit(solution)/shard_map/while/body/eval_jaxpr/ppermute | solution.py:19
  132.2 2.9 %collective-permute-done.22 = f32[8,80,8]{2,1,0:T(8,128)S(1)} collective-permute-done((f32[8,80,8]{2,1,0:T(8,128)S(1)}, f32[8,80,8]{2,1,0:T(8,128)S(1)}, u32[]{:S(2)}, u32[]{:S(2)}) %collective-permute-start.22) | collective-permute-done | bytes 20512 | tf_op jit(solution)/shard_map/while/body/eval_jaxpr/ppermute | solution.py:22
  135.1 1.7 %collective-permute-done.23 = f32[8,80,8]{2,1,0:T(8,128)S(1)} collective-permute-done((f32[8,80,8]{2,1,0:T(8,128)S(1)}, f32[8,80,8]{2,1,0:T(8,128)S(1)}, u32[]{:S(2)}, u32[]{:S(2)}) %collective-permute-start.23) | collective-permute-done | bytes 20512 | tf_op jit(solution)/shard_map/while/body/eval_jaxpr/ppermute | solution.py:19
  137.2 4.2 %collective-permute-done.14 = f32[9,80,8]{2,1,0:T(8,128)S(1)} collective-permute-done((f32[9,80,8]{2,1,0:T(8,128)S(1)}, f32[9,80,8]{2,1,0:T(8,128)S(1)}, u32[]{:S(2)}, u32[]{:S(2)}) %collective-permute-start.14) | collective-permute-done | bytes 23072 | tf_op jit(solution)/shard_map/while/body/eval_jaxpr/ppermute | solution.py:22
  (225 shorter events, 34.0 us)
Async XLA Ops:
  1.7 12.6 %collective-permute-start.4 = (f32[8,8,128]{2,1,0:T(8,128)S(1)}, f32[8,8,128]{2,1,0:T(8,128)S(1)}, u32[]{:S(2)}, u32[]{:S(2)}) collective-permute-start(f32[8,8,128]{2,1,0:T(8,128)S(1)} %get-tuple-element.520), channel_id=1, source_target_pairs={{8,0},{16,8},{24,16},{0,24},{9,1},{17,9},{25,17},{1,25},{10,2},{18... | collective-permute-start | bytes 98312 | tf_op jit(solution)/shard_map/while/body/eval_jaxpr/ppermute | solution.py:22
  5.7 8.6 %collective-permute-start.5 = (f32[8,8,128]{2,1,0:T(8,128)S(1)}, f32[8,8,128]{2,1,0:T(8,128)S(1)}, u32[]{:S(2)}, u32[]{:S(2)}) collective-permute-start(f32[8,8,128]{2,1,0:T(8,128)S(1)} %get-tuple-element.521), channel_id=1, source_target_pairs={{0,8},{8,16},{16,24},{24,0},{1,9},{9,17},{17,25},{25,1},{2,10},{10... | collective-permute-start | bytes 98312 | tf_op jit(solution)/shard_map/while/body/eval_jaxpr/ppermute | solution.py:19
  5.7 4.3 %collective-permute-start = (f32[1,8,128]{2,1,0:T(8,128)S(1)}, f32[1,8,128]{2,1,0:T(8,128)S(1)}, u32[]{:S(2)}, u32[]{:S(2)}) collective-permute-start(f32[1,8,128]{2,1,0:T(8,128)S(1)} %get-tuple-element.516), channel_id=1, source_target_pairs={{8,0},{16,8},{24,16},{0,24},{9,1},{17,9},{25,17},{1,25},{10,2},{18... | collective-permute-start | bytes 12296 | tf_op jit(solution)/shard_map/while/body/eval_jaxpr/ppermute | solution.py:22
  8.6 4.5 %collective-permute-start.1 = (f32[1,8,128]{2,1,0:T(8,128)S(1)}, f32[1,8,128]{2,1,0:T(8,128)S(1)}, u32[]{:S(2)}, u32[]{:S(2)}) collective-permute-start(f32[1,8,128]{2,1,0:T(8,128)S(1)} %get-tuple-element.517), channel_id=1, source_target_pairs={{0,8},{8,16},{16,24},{24,0},{1,9},{9,17},{17,25},{25,1},{2,10},{10... | collective-permute-start | bytes 12296 | tf_op jit(solution)/shard_map/while/body/eval_jaxpr/ppermute | solution.py:19
  13.2 4.9 %collective-permute-start.2 = (f32[1,80,8]{2,1,0:T(8,128)S(1)}, f32[1,80,8]{2,1,0:T(8,128)S(1)}, u32[]{:S(2)}, u32[]{:S(2)}) collective-permute-start(f32[1,80,8]{2,1,0:T(8,128)S(1)} %get-tuple-element.518), channel_id=1, source_target_pairs={{1,0},{2,1},{3,2},{4,3},{5,4},{6,5},{7,6},{0,7},{9,8},{10,9},{11,1... | collective-permute-start | bytes 7688 | tf_op jit(solution)/shard_map/while/body/eval_jaxpr/ppermute | solution.py:22
  14.3 5.3 %collective-permute-start.3 = (f32[1,80,8]{2,1,0:T(8,128)S(1)}, f32[1,80,8]{2,1,0:T(8,128)S(1)}, u32[]{:S(2)}, u32[]{:S(2)}) collective-permute-start(f32[1,80,8]{2,1,0:T(8,128)S(1)} %get-tuple-element.519), channel_id=1, source_target_pairs={{0,1},{1,2},{2,3},{3,4},{4,5},{5,6},{6,7},{7,0},{8,9},{9,10},{10,1... | collective-permute-start | bytes 7688 | tf_op jit(solution)/shard_map/while/body/eval_jaxpr/ppermute | solution.py:19
  14.5 9.9 %collective-permute-start.6 = (f32[8,80,8]{2,1,0:T(8,128)S(1)}, f32[8,80,8]{2,1,0:T(8,128)S(1)}, u32[]{:S(2)}, u32[]{:S(2)}) collective-permute-start(f32[8,80,8]{2,1,0:T(8,128)S(1)} %get-tuple-element.522), channel_id=1, source_target_pairs={{1,0},{2,1},{3,2},{4,3},{5,4},{6,5},{7,6},{0,7},{9,8},{10,9},{11,1... | collective-permute-start | bytes 61448 | tf_op jit(solution)/shard_map/while/body/eval_jaxpr/ppermute | solution.py:22
  18.1 9.4 %collective-permute-start.7 = (f32[8,80,8]{2,1,0:T(8,128)S(1)}, f32[8,80,8]{2,1,0:T(8,128)S(1)}, u32[]{:S(2)}, u32[]{:S(2)}) collective-permute-start(f32[8,80,8]{2,1,0:T(8,128)S(1)} %get-tuple-element.523), channel_id=1, source_target_pairs={{0,1},{1,2},{2,3},{3,4},{4,5},{5,6},{6,7},{7,0},{8,9},{9,10},{10,1... | collective-permute-start | bytes 61448 | tf_op jit(solution)/shard_map/while/body/eval_jaxpr/ppermute | solution.py:19
  30.3 8.2 %collective-permute-start.4 = (f32[8,8,128]{2,1,0:T(8,128)S(1)}, f32[8,8,128]{2,1,0:T(8,128)S(1)}, u32[]{:S(2)}, u32[]{:S(2)}) collective-permute-start(f32[8,8,128]{2,1,0:T(8,128)S(1)} %get-tuple-element.520), channel_id=1, source_target_pairs={{8,0},{16,8},{24,16},{0,24},{9,1},{17,9},{25,17},{1,25},{10,2},{18... | collective-permute-start | bytes 98312 | tf_op jit(solution)/shard_map/while/body/eval_jaxpr/ppermute | solution.py:22
  30.3 8.1 %collective-permute-start.5 = (f32[8,8,128]{2,1,0:T(8,128)S(1)}, f32[8,8,128]{2,1,0:T(8,128)S(1)}, u32[]{:S(2)}, u32[]{:S(2)}) collective-permute-start(f32[8,8,128]{2,1,0:T(8,128)S(1)} %get-tuple-element.521), channel_id=1, source_target_pairs={{0,8},{8,16},{16,24},{24,0},{1,9},{9,17},{17,25},{25,1},{2,10},{10... | collective-permute-start | bytes 98312 | tf_op jit(solution)/shard_map/while/body/eval_jaxpr/ppermute | solution.py:19
  32.4 3.7 %collective-permute-start = (f32[1,8,128]{2,1,0:T(8,128)S(1)}, f32[1,8,128]{2,1,0:T(8,128)S(1)}, u32[]{:S(2)}, u32[]{:S(2)}) collective-permute-start(f32[1,8,128]{2,1,0:T(8,128)S(1)} %get-tuple-element.516), channel_id=1, source_target_pairs={{8,0},{16,8},{24,16},{0,24},{9,1},{17,9},{25,17},{1,25},{10,2},{18... | collective-permute-start | bytes 12296 | tf_op jit(solution)/shard_map/while/body/eval_jaxpr/ppermute | solution.py:22
  33.4 4.5 %collective-permute-start.1 = (f32[1,8,128]{2,1,0:T(8,128)S(1)}, f32[1,8,128]{2,1,0:T(8,128)S(1)}, u32[]{:S(2)}, u32[]{:S(2)}) collective-permute-start(f32[1,8,128]{2,1,0:T(8,128)S(1)} %get-tuple-element.517), channel_id=1, source_target_pairs={{0,8},{8,16},{16,24},{24,0},{1,9},{9,17},{17,25},{25,1},{2,10},{10... | collective-permute-start | bytes 12296 | tf_op jit(solution)/shard_map/while/body/eval_jaxpr/ppermute | solution.py:19
  38.0 3.9 %collective-permute-start.2 = (f32[1,80,8]{2,1,0:T(8,128)S(1)}, f32[1,80,8]{2,1,0:T(8,128)S(1)}, u32[]{:S(2)}, u32[]{:S(2)}) collective-permute-start(f32[1,80,8]{2,1,0:T(8,128)S(1)} %get-tuple-element.518), channel_id=1, source_target_pairs={{1,0},{2,1},{3,2},{4,3},{5,4},{6,5},{7,6},{0,7},{9,8},{10,9},{11,1... | collective-permute-start | bytes 7688 | tf_op jit(solution)/shard_map/while/body/eval_jaxpr/ppermute | solution.py:22
  38.0 5.5 %collective-permute-start.3 = (f32[1,80,8]{2,1,0:T(8,128)S(1)}, f32[1,80,8]{2,1,0:T(8,128)S(1)}, u32[]{:S(2)}, u32[]{:S(2)}) collective-permute-start(f32[1,80,8]{2,1,0:T(8,128)S(1)} %get-tuple-element.519), channel_id=1, source_target_pairs={{0,1},{1,2},{2,3},{3,4},{4,5},{5,6},{6,7},{7,0},{8,9},{9,10},{10,1... | collective-permute-start | bytes 7688 | tf_op jit(solution)/shard_map/while/body/eval_jaxpr/ppermute | solution.py:19
  38.7 9.2 %collective-permute-start.6 = (f32[8,80,8]{2,1,0:T(8,128)S(1)}, f32[8,80,8]{2,1,0:T(8,128)S(1)}, u32[]{:S(2)}, u32[]{:S(2)}) collective-permute-start(f32[8,80,8]{2,1,0:T(8,128)S(1)} %get-tuple-element.522), channel_id=1, source_target_pairs={{1,0},{2,1},{3,2},{4,3},{5,4},{6,5},{7,6},{0,7},{9,8},{10,9},{11,1... | collective-permute-start | bytes 61448 | tf_op jit(solution)/shard_map/while/body/eval_jaxpr/ppermute | solution.py:22
  41.8 8.5 %collective-permute-start.7 = (f32[8,80,8]{2,1,0:T(8,128)S(1)}, f32[8,80,8]{2,1,0:T(8,128)S(1)}, u32[]{:S(2)}, u32[]{:S(2)}) collective-permute-start(f32[8,80,8]{2,1,0:T(8,128)S(1)} %get-tuple-element.523), channel_id=1, source_target_pairs={{0,1},{1,2},{2,3},{3,4},{4,5},{5,6},{6,7},{7,0},{8,9},{9,10},{10,1... | collective-permute-start | bytes 61448 | tf_op jit(solution)/shard_map/while/body/eval_jaxpr/ppermute | solution.py:19
  54.9 22.0 %collective-permute-start.12 = (f32[9,8,128]{2,1,0:T(8,128)S(1)}, f32[9,8,128]{2,1,0:T(8,128)S(1)}, u32[]{:S(2)}, u32[]{:S(2)}) collective-permute-start(f32[9,8,128]{2,1,0:T(8,128)S(1)} %get-tuple-element.560), channel_id=1, source_target_pairs={{8,0},{16,8},{24,16},{0,24},{9,1},{17,9},{25,17},{1,25},{10,2},{18... | collective-permute-start | bytes 110600 | tf_op jit(solution)/shard_map/while/body/eval_jaxpr/ppermute | solution.py:22
  55.1 21.8 %collective-permute-start.13 = (f32[9,8,128]{2,1,0:T(8,128)S(1)}, f32[9,8,128]{2,1,0:T(8,128)S(1)}, u32[]{:S(2)}, u32[]{:S(2)}) collective-permute-start(f32[9,8,128]{2,1,0:T(8,128)S(1)} %get-tuple-element.561), channel_id=1, source_target_pairs={{0,8},{8,16},{16,24},{24,0},{1,9},{9,17},{17,25},{25,1},{2,10},{10... | collective-permute-start | bytes 110600 | tf_op jit(solution)/shard_map/while/body/eval_jaxpr/ppermute | solution.py:19
  57.0 13.2 %collective-permute-start.8 = (f32[8,8,128]{2,1,0:T(8,128)S(1)}, f32[8,8,128]{2,1,0:T(8,128)S(1)}, u32[]{:S(2)}, u32[]{:S(2)}) collective-permute-start(f32[8,8,128]{2,1,0:T(8,128)S(1)} %get-tuple-element.554), channel_id=1, source_target_pairs={{8,0},{16,8},{24,16},{0,24},{9,1},{17,9},{25,17},{1,25},{10,2},{18... | collective-permute-start | bytes 98312 | tf_op jit(solution)/shard_map/while/body/eval_jaxpr/ppermute | solution.py:22
  58.1 3.7 %collective-permute-start.16 = (f32[1,8,128]{2,1,0:T(8,128)S(1)}, f32[1,8,128]{2,1,0:T(8,128)S(1)}, u32[]{:S(2)}, u32[]{:S(2)}) collective-permute-start(f32[1,8,128]{2,1,0:T(8,128)S(1)} %get-tuple-element.585), channel_id=1, source_target_pairs={{8,0},{16,8},{24,16},{0,24},{9,1},{17,9},{25,17},{1,25},{10,2},{18... | collective-permute-start | bytes 12296 | tf_op jit(solution)/shard_map/while/body/eval_jaxpr/ppermute | solution.py:22
  59.1 4.5 %collective-permute-start.17 = (f32[1,8,128]{2,1,0:T(8,128)S(1)}, f32[1,8,128]{2,1,0:T(8,128)S(1)}, u32[]{:S(2)}, u32[]{:S(2)}) collective-permute-start(f32[1,8,128]{2,1,0:T(8,128)S(1)} %get-tuple-element.586), channel_id=1, source_target_pairs={{0,8},{8,16},{16,24},{24,0},{1,9},{9,17},{17,25},{25,1},{2,10},{10... | collective-permute-start | bytes 12296 | tf_op jit(solution)/shard_map/while/body/eval_jaxpr/ppermute | solution.py:19
  63.7 1.8 %collective-permute-start.18 = (f32[1,80,8]{2,1,0:T(8,128)S(1)}, f32[1,80,8]{2,1,0:T(8,128)S(1)}, u32[]{:S(2)}, u32[]{:S(2)}) collective-permute-start(f32[1,80,8]{2,1,0:T(8,128)S(1)} %get-tuple-element.587), channel_id=1, source_target_pairs={{1,0},{2,1},{3,2},{4,3},{5,4},{6,5},{7,6},{0,7},{9,8},{10,9},{11,1... | collective-permute-start | bytes 7688 | tf_op jit(solution)/shard_map/while/body/eval_jaxpr/ppermute | solution.py:22
  63.7 5.3 %collective-permute-start.19 = (f32[1,80,8]{2,1,0:T(8,128)S(1)}, f32[1,80,8]{2,1,0:T(8,128)S(1)}, u32[]{:S(2)}, u32[]{:S(2)}) collective-permute-start(f32[1,80,8]{2,1,0:T(8,128)S(1)} %get-tuple-element.588), channel_id=1, source_target_pairs={{0,1},{1,2},{2,3},{3,4},{4,5},{5,6},{6,7},{7,0},{8,9},{9,10},{10,1... | collective-permute-start | bytes 7688 | tf_op jit(solution)/shard_map/while/body/eval_jaxpr/ppermute | solution.py:19
  65.5 5.7 %collective-permute-start.9 = (f32[8,8,128]{2,1,0:T(8,128)S(1)}, f32[8,8,128]{2,1,0:T(8,128)S(1)}, u32[]{:S(2)}, u32[]{:S(2)}) collective-permute-start(f32[8,8,128]{2,1,0:T(8,128)S(1)} %get-tuple-element.556), channel_id=1, source_target_pairs={{0,8},{8,16},{16,24},{24,0},{1,9},{9,17},{17,25},{25,1},{2,10},{10... | collective-permute-start | bytes 98312 | tf_op jit(solution)/shard_map/while/body/eval_jaxpr/ppermute | solution.py:19
  69.0 4.1 %collective-permute-start.20 = (f32[8,8,128]{2,1,0:T(8,128)S(1)}, f32[8,8,128]{2,1,0:T(8,128)S(1)}, u32[]{:S(2)}, u32[]{:S(2)}) collective-permute-start(f32[8,8,128]{2,1,0:T(8,128)S(1)} %get-tuple-element.590), channel_id=1, source_target_pairs={{8,0},{16,8},{24,16},{0,24},{9,1},{17,9},{25,17},{1,25},{10,2},{18... | collective-permute-start | bytes 98312 | tf_op jit(solution)/shard_map/while/body/eval_jaxpr/ppermute | solution.py:22
  70.2 4.9 %collective-permute-start.21 = (f32[8,8,128]{2,1,0:T(8,128)S(1)}, f32[8,8,128]{2,1,0:T(8,128)S(1)}, u32[]{:S(2)}, u32[]{:S(2)}) collective-permute-start(f32[8,8,128]{2,1,0:T(8,128)S(1)} %get-tuple-element.592), channel_id=1, source_target_pairs={{0,8},{8,16},{16,24},{24,0},{1,9},{9,17},{17,25},{25,1},{2,10},{10... | collective-permute-start | bytes 98312 | tf_op jit(solution)/shard_map/while/body/eval_jaxpr/ppermute | solution.py:19
  71.4 9.8 %collective-permute-start.10 = (f32[8,80,8]{2,1,0:T(8,128)S(1)}, f32[8,80,8]{2,1,0:T(8,128)S(1)}, u32[]{:S(2)}, u32[]{:S(2)}) collective-permute-start(f32[8,80,8]{2,1,0:T(8,128)S(1)} %get-tuple-element.557), channel_id=1, source_target_pairs={{1,0},{2,1},{3,2},{4,3},{5,4},{6,5},{7,6},{0,7},{9,8},{10,9},{11,1... | collective-permute-start | bytes 61448 | tf_op jit(solution)/shard_map/while/body/eval_jaxpr/ppermute | solution.py:22
  73.1 11.8 %collective-permute-start.11 = (f32[8,80,8]{2,1,0:T(8,128)S(1)}, f32[8,80,8]{2,1,0:T(8,128)S(1)}, u32[]{:S(2)}, u32[]{:S(2)}) collective-permute-start(f32[8,80,8]{2,1,0:T(8,128)S(1)} %get-tuple-element.558), channel_id=1, source_target_pairs={{0,1},{1,2},{2,3},{3,4},{4,5},{5,6},{6,7},{7,0},{8,9},{9,10},{10,1... | collective-permute-start | bytes 61448 | tf_op jit(solution)/shard_map/while/body/eval_jaxpr/ppermute | solution.py:19
  75.2 13.0 %collective-permute-start.22 = (f32[8,80,8]{2,1,0:T(8,128)S(1)}, f32[8,80,8]{2,1,0:T(8,128)S(1)}, u32[]{:S(2)}, u32[]{:S(2)}) collective-permute-start(f32[8,80,8]{2,1,0:T(8,128)S(1)} %get-tuple-element.593), channel_id=1, source_target_pairs={{1,0},{2,1},{3,2},{4,3},{5,4},{6,5},{7,6},{0,7},{9,8},{10,9},{11,1... | collective-permute-start | bytes 61448 | tf_op jit(solution)/shard_map/while/body/eval_jaxpr/ppermute | solution.py:22
  76.9 13.4 %collective-permute-start.23 = (f32[8,80,8]{2,1,0:T(8,128)S(1)}, f32[8,80,8]{2,1,0:T(8,128)S(1)}, u32[]{:S(2)}, u32[]{:S(2)}) collective-permute-start(f32[8,80,8]{2,1,0:T(8,128)S(1)} %get-tuple-element.594), channel_id=1, source_target_pairs={{0,1},{1,2},{2,3},{3,4},{4,5},{5,6},{6,7},{7,0},{8,9},{9,10},{10,1... | collective-permute-start | bytes 61448 | tf_op jit(solution)/shard_map/while/body/eval_jaxpr/ppermute | solution.py:19
  77.1 17.2 %collective-permute-start.14 = (f32[9,80,8]{2,1,0:T(8,128)S(1)}, f32[9,80,8]{2,1,0:T(8,128)S(1)}, u32[]{:S(2)}, u32[]{:S(2)}) collective-permute-start(f32[9,80,8]{2,1,0:T(8,128)S(1)} %get-tuple-element.562), channel_id=1, source_target_pairs={{1,0},{2,1},{3,2},{4,3},{5,4},{6,5},{7,6},{0,7},{9,8},{10,9},{11,1... | collective-permute-start | bytes 69128 | tf_op jit(solution)/shard_map/while/body/eval_jaxpr/ppermute | solution.py:22
  81.2 13.1 %collective-permute-start.15 = (f32[9,80,8]{2,1,0:T(8,128)S(1)}, f32[9,80,8]{2,1,0:T(8,128)S(1)}, u32[]{:S(2)}, u32[]{:S(2)}) collective-permute-start(f32[9,80,8]{2,1,0:T(8,128)S(1)} %get-tuple-element.563), channel_id=1, source_target_pairs={{0,1},{1,2},{2,3},{3,4},{4,5},{5,6},{6,7},{7,0},{8,9},{9,10},{10,1... | collective-permute-start | bytes 69128 | tf_op jit(solution)/shard_map/while/body/eval_jaxpr/ppermute | solution.py:19
  99.4 24.4 %collective-permute-start.12 = (f32[9,8,128]{2,1,0:T(8,128)S(1)}, f32[9,8,128]{2,1,0:T(8,128)S(1)}, u32[]{:S(2)}, u32[]{:S(2)}) collective-permute-start(f32[9,8,128]{2,1,0:T(8,128)S(1)} %get-tuple-element.560), channel_id=1, source_target_pairs={{8,0},{16,8},{24,16},{0,24},{9,1},{17,9},{25,17},{1,25},{10,2},{18... | collective-permute-start | bytes 110600 | tf_op jit(solution)/shard_map/while/body/eval_jaxpr/ppermute | solution.py:22
  101.5 22.4 %collective-permute-start.13 = (f32[9,8,128]{2,1,0:T(8,128)S(1)}, f32[9,8,128]{2,1,0:T(8,128)S(1)}, u32[]{:S(2)}, u32[]{:S(2)}) collective-permute-start(f32[9,8,128]{2,1,0:T(8,128)S(1)} %get-tuple-element.561), channel_id=1, source_target_pairs={{0,8},{8,16},{16,24},{24,0},{1,9},{9,17},{17,25},{25,1},{2,10},{10... | collective-permute-start | bytes 110600 | tf_op jit(solution)/shard_map/while/body/eval_jaxpr/ppermute | solution.py:19
  101.5 15.4 %collective-permute-start.8 = (f32[8,8,128]{2,1,0:T(8,128)S(1)}, f32[8,8,128]{2,1,0:T(8,128)S(1)}, u32[]{:S(2)}, u32[]{:S(2)}) collective-permute-start(f32[8,8,128]{2,1,0:T(8,128)S(1)} %get-tuple-element.554), channel_id=1, source_target_pairs={{8,0},{16,8},{24,16},{0,24},{9,1},{17,9},{25,17},{1,25},{10,2},{18... | collective-permute-start | bytes 98312 | tf_op jit(solution)/shard_map/while/body/eval_jaxpr/ppermute | solution.py:22
  104.5 3.7 %collective-permute-start.16 = (f32[1,8,128]{2,1,0:T(8,128)S(1)}, f32[1,8,128]{2,1,0:T(8,128)S(1)}, u32[]{:S(2)}, u32[]{:S(2)}) collective-permute-start(f32[1,8,128]{2,1,0:T(8,128)S(1)} %get-tuple-element.585), channel_id=1, source_target_pairs={{8,0},{16,8},{24,16},{0,24},{9,1},{17,9},{25,17},{1,25},{10,2},{18... | collective-permute-start | bytes 12296 | tf_op jit(solution)/shard_map/while/body/eval_jaxpr/ppermute | solution.py:22
  104.6 4.5 %collective-permute-start.17 = (f32[1,8,128]{2,1,0:T(8,128)S(1)}, f32[1,8,128]{2,1,0:T(8,128)S(1)}, u32[]{:S(2)}, u32[]{:S(2)}) collective-permute-start(f32[1,8,128]{2,1,0:T(8,128)S(1)} %get-tuple-element.586), channel_id=1, source_target_pairs={{0,8},{8,16},{16,24},{24,0},{1,9},{9,17},{17,25},{25,1},{2,10},{10... | collective-permute-start | bytes 12296 | tf_op jit(solution)/shard_map/while/body/eval_jaxpr/ppermute | solution.py:19
  109.2 3.4 %collective-permute-start.18 = (f32[1,80,8]{2,1,0:T(8,128)S(1)}, f32[1,80,8]{2,1,0:T(8,128)S(1)}, u32[]{:S(2)}, u32[]{:S(2)}) collective-permute-start(f32[1,80,8]{2,1,0:T(8,128)S(1)} %get-tuple-element.587), channel_id=1, source_target_pairs={{1,0},{2,1},{3,2},{4,3},{5,4},{6,5},{7,6},{0,7},{9,8},{10,9},{11,1... | collective-permute-start | bytes 7688 | tf_op jit(solution)/shard_map/while/body/eval_jaxpr/ppermute | solution.py:22
  110.9 5.2 %collective-permute-start.19 = (f32[1,80,8]{2,1,0:T(8,128)S(1)}, f32[1,80,8]{2,1,0:T(8,128)S(1)}, u32[]{:S(2)}, u32[]{:S(2)}) collective-permute-start(f32[1,80,8]{2,1,0:T(8,128)S(1)} %get-tuple-element.588), channel_id=1, source_target_pairs={{0,1},{1,2},{2,3},{3,4},{4,5},{5,6},{6,7},{7,0},{8,9},{9,10},{10,1... | collective-permute-start | bytes 7688 | tf_op jit(solution)/shard_map/while/body/eval_jaxpr/ppermute | solution.py:19
  112.6 5.7 %collective-permute-start.9 = (f32[8,8,128]{2,1,0:T(8,128)S(1)}, f32[8,8,128]{2,1,0:T(8,128)S(1)}, u32[]{:S(2)}, u32[]{:S(2)}) collective-permute-start(f32[8,8,128]{2,1,0:T(8,128)S(1)} %get-tuple-element.556), channel_id=1, source_target_pairs={{0,8},{8,16},{16,24},{24,0},{1,9},{9,17},{17,25},{25,1},{2,10},{10... | collective-permute-start | bytes 98312 | tf_op jit(solution)/shard_map/while/body/eval_jaxpr/ppermute | solution.py:19
  116.1 3.9 %collective-permute-start.20 = (f32[8,8,128]{2,1,0:T(8,128)S(1)}, f32[8,8,128]{2,1,0:T(8,128)S(1)}, u32[]{:S(2)}, u32[]{:S(2)}) collective-permute-start(f32[8,8,128]{2,1,0:T(8,128)S(1)} %get-tuple-element.590), channel_id=1, source_target_pairs={{8,0},{16,8},{24,16},{0,24},{9,1},{17,9},{25,17},{1,25},{10,2},{18... | collective-permute-start | bytes 98312 | tf_op jit(solution)/shard_map/while/body/eval_jaxpr/ppermute | solution.py:22
  116.9 4.9 %collective-permute-start.21 = (f32[8,8,128]{2,1,0:T(8,128)S(1)}, f32[8,8,128]{2,1,0:T(8,128)S(1)}, u32[]{:S(2)}, u32[]{:S(2)}) collective-permute-start(f32[8,8,128]{2,1,0:T(8,128)S(1)} %get-tuple-element.592), channel_id=1, source_target_pairs={{0,8},{8,16},{16,24},{24,0},{1,9},{9,17},{17,25},{25,1},{2,10},{10... | collective-permute-start | bytes 98312 | tf_op jit(solution)/shard_map/while/body/eval_jaxpr/ppermute | solution.py:19
  118.5 9.6 %collective-permute-start.10 = (f32[8,80,8]{2,1,0:T(8,128)S(1)}, f32[8,80,8]{2,1,0:T(8,128)S(1)}, u32[]{:S(2)}, u32[]{:S(2)}) collective-permute-start(f32[8,80,8]{2,1,0:T(8,128)S(1)} %get-tuple-element.557), channel_id=1, source_target_pairs={{1,0},{2,1},{3,2},{4,3},{5,4},{6,5},{7,6},{0,7},{9,8},{10,9},{11,1... | collective-permute-start | bytes 61448 | tf_op jit(solution)/shard_map/while/body/eval_jaxpr/ppermute | solution.py:22
  120.0 11.8 %collective-permute-start.11 = (f32[8,80,8]{2,1,0:T(8,128)S(1)}, f32[8,80,8]{2,1,0:T(8,128)S(1)}, u32[]{:S(2)}, u32[]{:S(2)}) collective-permute-start(f32[8,80,8]{2,1,0:T(8,128)S(1)} %get-tuple-element.558), channel_id=1, source_target_pairs={{0,1},{1,2},{2,3},{3,4},{4,5},{5,6},{6,7},{7,0},{8,9},{9,10},{10,1... | collective-permute-start | bytes 61448 | tf_op jit(solution)/shard_map/while/body/eval_jaxpr/ppermute | solution.py:19
  122.0 13.1 %collective-permute-start.22 = (f32[8,80,8]{2,1,0:T(8,128)S(1)}, f32[8,80,8]{2,1,0:T(8,128)S(1)}, u32[]{:S(2)}, u32[]{:S(2)}) collective-permute-start(f32[8,80,8]{2,1,0:T(8,128)S(1)} %get-tuple-element.593), channel_id=1, source_target_pairs={{1,0},{2,1},{3,2},{4,3},{5,4},{6,5},{7,6},{0,7},{9,8},{10,9},{11,1... | collective-permute-start | bytes 61448 | tf_op jit(solution)/shard_map/while/body/eval_jaxpr/ppermute | solution.py:22
  123.8 13.0 %collective-permute-start.23 = (f32[8,80,8]{2,1,0:T(8,128)S(1)}, f32[8,80,8]{2,1,0:T(8,128)S(1)}, u32[]{:S(2)}, u32[]{:S(2)}) collective-permute-start(f32[8,80,8]{2,1,0:T(8,128)S(1)} %get-tuple-element.594), channel_id=1, source_target_pairs={{0,1},{1,2},{2,3},{3,4},{4,5},{5,6},{6,7},{7,0},{8,9},{9,10},{10,1... | collective-permute-start | bytes 61448 | tf_op jit(solution)/shard_map/while/body/eval_jaxpr/ppermute | solution.py:19
  124.0 17.4 %collective-permute-start.14 = (f32[9,80,8]{2,1,0:T(8,128)S(1)}, f32[9,80,8]{2,1,0:T(8,128)S(1)}, u32[]{:S(2)}, u32[]{:S(2)}) collective-permute-start(f32[9,80,8]{2,1,0:T(8,128)S(1)} %get-tuple-element.562), channel_id=1, source_target_pairs={{1,0},{2,1},{3,2},{4,3},{5,4},{6,5},{7,6},{0,7},{9,8},{10,9},{11,1... | collective-permute-start | bytes 69128 | tf_op jit(solution)/shard_map/while/body/eval_jaxpr/ppermute | solution.py:22
  128.1 13.3 %collective-permute-start.15 = (f32[9,80,8]{2,1,0:T(8,128)S(1)}, f32[9,80,8]{2,1,0:T(8,128)S(1)}, u32[]{:S(2)}, u32[]{:S(2)}) collective-permute-start(f32[9,80,8]{2,1,0:T(8,128)S(1)} %get-tuple-element.563), channel_id=1, source_target_pairs={{0,1},{1,2},{2,3},{3,4},{4,5},{5,6},{6,7},{7,0},{8,9},{9,10},{10,1... | collective-permute-start | bytes 69128 | tf_op jit(solution)/shard_map/while/body/eval_jaxpr/ppermute | solution.py:19
  (4 other events, 3.7 us)
where the time goes:
time: 148 us; the launch traced here: 147 us
  waiting for transfers between devices  69.9 us (47%)
  starting transfers between devices  52.9 us (36%)
  other arithmetic  14.3 us (10%)
  local copies, waits for them, and re-layouts  8.43 us (6%)
    ppermute x24, starting transfers between devices, with_halo(): lax.ppermute(lax.slice_in_dim(block, 0, width, axis=dim), axis, backward)  40.5 us
    ppermute x24, waiting for transfers between devices, with_halo(): lax.ppermute(lax.slice_in_dim(block, block.shape[dim] - width, None, axis...  37.6 us
    ppermute x24, waiting for transfers between devices, with_halo(): lax.ppermute(lax.slice_in_dim(block, 0, width, axis=dim), axis, backward)  32.3 us
    ppermute x24, starting transfers between devices, with_halo(): lax.ppermute(lax.slice_in_dim(block, block.shape[dim] - width, None, axis...  12.3 us
    div x30, other arithmetic, backward_block(): carried = adjoint * 0.5 * (1.0 + diff / root) * level / total  6.18 us
    unnamed x8, local copies, waits for them, and re-layouts  3.48 us
    pow x16, other arithmetic, forward_block(): total = cross(prev ** power_p)  3.42 us
  transfers between devices with their start and end apart: 48, of which 30 were waited for; matrix products, arithmetic and copies ran while one was open for 3% of the time, Pallas kernels for 0%

commit v1 on v0

v1 whole, which is shorter than its diff:
```python
import functools
import math

import jax
import jax.numpy as jnp
from jax import lax
from jax.experimental import pallas as pl
from jax.experimental.pallas import tpu as pltpu
from jax.sharding import PartitionSpec as P

power_p = 20.0
root_q = 20.0 + math.log(5.0) / math.log(0.1)
smooth_eps = 0.0001
SUB = 8

VMEM = pl.BlockSpec(memory_space=pltpu.VMEM)


def up8(n):
    return -(-n // SUB) * SUB


class Plan:
    def __init__(self, layers, rows, cols):
        self.nz, self.rows, self.cols = layers, rows, cols
        self.fields = [(0, z, 2 * (layers - 1) - z) for z in range(layers)]
        self.fields += [(1, z, z) for z in range(layers - 1, 0, -1)]
        far = 2 * (layers - 1)
        self.halo = up8(far)
        self.row_at = {}
        at = SUB
        for arr, z, d in self.fields:
            self.row_at[arr, z] = at
            at += d
        self.row_len = up8(at) + SUB
        self.col_at, self.col_tiles = self.fit([((arr, z), d) for arr, z, d in self.fields])
        items = []
        for arr, z, d in self.fields:
            for k in range(-(-(d - 1) // SUB)):
                items.append(((arr, z, k), 2 * (d - 1 - SUB * k)))
        self.corner_at, self.corner_tiles = self.fit(items)

    def fit(self, items):
        room, where = [], {}
        for key, width in sorted(items, key=lambda item: -item[1]):
            for tile, used in enumerate(room):
                if used + width <= self.cols:
                    break
            else:
                tile = len(room)
                room.append(0)
            where[key] = (tile, room[tile])
            room[tile] += width
        return where, len(room)


def shift(x, amount):
    amount %= x.shape[1]
    return x if amount == 0 else pltpu.roll(x, amount, 1)


def lanes_of(shape):
    return lax.broadcasted_iota(jnp.int32, shape, 1)


def pack_rows(plan, dens, cot, first, last):
    for arr, z, d in plan.fields:
        src = (dens, cot)[arr]
        at = plan.row_at[arr, z]
        first[at : at + d, :] = src[z, :d, :]
        last[at : at + d, :] = src[z, plan.rows - d :, :]
    end = plan.row_at[1, 1] + 1
    for ref in (first, last):
        ref[:SUB, :] = jnp.zeros((SUB, plan.cols), jnp.float32)
        ref[end:, :] = jnp.zeros((plan.row_len - end, plan.cols), jnp.float32)


def pack_columns(plan, dens, cot, first, last):
    n = plan.cols
    lane = lanes_of((SUB, n))
    for tile in range(plan.col_tiles):
        inside = [f for f in plan.fields if plan.col_at[f[0], f[1]][0] == tile]
        inside.sort(key=lambda f: plan.col_at[f[0], f[1]][1])
        for r in range(0, plan.rows, SUB):
            one, two = None, None
            for arr, z, d in inside:
                at = plan.col_at[arr, z][1]
                x = (dens, cot)[arr][z, r : r + SUB, :]
                a, b = shift(x, at), shift(x, at + d)
                if one is None:
                    one, two = a, b
                else:
                    here = lane >= at
                    one, two = jnp.where(here, a, one), jnp.where(here, b, two)
            first[tile, r : r + SUB, :] = one
            last[tile, r : r + SUB, :] = two


def pack_corners(plan, left, right, first, last):
    lane = lanes_of((SUB, plan.cols))
    out = [[None] * plan.corner_tiles, [None] * plan.corner_tiles]
    order = sorted(plan.corner_at.items(), key=lambda item: item[1][1])
    reach = {(arr, z): d for arr, z, d in plan.fields}
    for (arr, z, k), (tile, at) in order:
        d = reach[arr, z]
        w = d - 1 - SUB * k
        ctile, cat = plan.col_at[arr, z]
        for way in range(2):
            r = SUB * k if way == 0 else plan.rows - SUB * (k + 1)
            a = shift(left[ctile, r : r + SUB, :], at - (cat + d - w))
            b = shift(right[ctile, r : r + SUB, :], at + w - cat)
            both = jnp.where(lane >= at + w, b, a)
            prev = out[way][tile]
            out[way][tile] = both if prev is None else jnp.where(lane >= at, both, prev)
    for tile in range(plan.corner_tiles):
        first[tile] = out[0][tile]
        last[tile] = out[1][tile]


def assemble(plan, arr, src, above, below, left, right, cabove, cbelow, main, side):
    n, top = plan.cols, plan.halo
    lane = lanes_of((SUB, n))
    low = lane < n // 2
    for a, z, d in plan.fields:
        if a != arr:
            continue
        at = plan.row_at[arr, z]
        ctile, cat = plan.col_at[arr, z]
        for r in range(0, plan.rows, SUB):
            main[z, top + r : top + r + SUB, :] = src[z, r : r + SUB, :]
            x = shift(left[ctile, r : r + SUB, :], -(cat + d))
            y = shift(right[ctile, r : r + SUB, :], -cat)
            side[z, top + r : top + r + SUB, :] = jnp.where(low, y, x)
        for k in range(-(-d // SUB)):
            lo, hi = top - SUB * (k + 1), top + plan.rows + SUB * k
            main[z, lo : lo + SUB, :] = above[at + d - SUB * (k + 1) : at + d - SUB * k, :]
            main[z, hi : hi + SUB, :] = below[at + SUB * k : at + SUB * (k + 1), :]
            w = d - 1 - SUB * k
            if w > 0:
                tile, cor = plan.corner_at[arr, z, k]
                side[z, lo : lo + SUB, :] = shift(cabove[tile], -(cor + w))
                side[z, hi : hi + SUB, :] = shift(cbelow[tile], -(cor + w))


def cross(ref, now, r, lane):
    n = lane.shape[1]
    b = SUB + r
    m, s = ref[now, 0, b : b + SUB, :], ref[now, 1, b : b + SUB, :]
    vm = ref[now, 0, b - 1 : b + SUB - 1, :] + ref[now, 0, b + 1 : b + SUB + 1, :]
    vs = ref[now, 1, b - 1 : b + SUB - 1, :] + ref[now, 1, b + 1 : b + SUB + 1, :]
    m1, s1 = pltpu.roll(m, 1, 1), pltpu.roll(s, 1, 1)
    m2, s2 = pltpu.roll(m, n - 1, 1), pltpu.roll(s, n - 1, 1)
    start, end = lane == 0, lane == n - 1
    hm = jnp.where(start, s1, m1) + jnp.where(end, s2, m2)
    hs = jnp.where(start, m1, s1) + jnp.where(end, m2, s2)
    return m + vm + hm, s + vs + hs


def filter_body(
    plan, dens, cot, above, below, left, right, cabove, cbelow,
    printed, gradient, dm, ds, cm, cs, work, slope, weight, da,
):
    nz, rows, n, top = plan.nz, plan.rows, plan.cols, plan.halo
    lane = lanes_of((SUB, n))
    full = top + rows + top
    args = (above, below, left, right, cabove, cbelow)
    assemble(plan, 0, dens, *args, dm, ds)
    assemble(plan, 1, cot, *args, cm, cs)

    margin = jnp.ones((SUB, n), jnp.float32)
    for now in range(2):
        for half in range(2):
            work[now, half, :SUB, :] = margin
            work[now, half, SUB + full :, :] = margin

    def tiles(reach):
        depth = up8(max(reach, 0))
        return range(top - depth, top + rows + depth, SUB)

    coef_rows = up8(nz - 1)

    def layer(z, now, r, half, density, total):
        if total is None:
            level = jnp.ones_like(density)
        else:
            lg = jnp.log(total)
            level = jnp.exp2(lg * jnp.float32(1.0 / (root_q * math.log(2.0))))
            ratio = jnp.exp2(lg * jnp.float32((1.0 / root_q - 1.0) / math.log(2.0)))
        diff = density - level
        square = diff * diff + smooth_eps
        inv = lax.rsqrt(square)
        u = diff * inv
        out = 0.5 * (density + level - square * inv + math.sqrt(smooth_eps))
        p2 = out * out
        p4 = p2 * p2
        p16 = (p4 * p4) * (p4 * p4)
        work[now, half, SUB + r : SUB + r + SUB, :] = p16 * p4
        if top - coef_rows <= r < top + rows + coef_rows:
            slope[z, half, r : r + SUB, :] = jnp.float32(power_p / root_q) * (p16 * (p2 * out))
            if total is not None:
                weight[z, half, r : r + SUB, :] = (0.5 + 0.5 * u) * ratio
        if half == 0 and top <= r < top + rows:
            printed[z, r - top : r - top + SUB, :] = out
            da[z, r - top : r - top + SUB, :] = 0.5 - 0.5 * u

    for r in tiles(2 * (nz - 1)):
        layer(0, 0, r, 0, dm[0, r : r + SUB, :], None)
        layer(0, 0, r, 1, ds[0, r : r + SUB, :], None)

    def forward(reach):
        def step(z, carry):
            now = lax.rem(z, 2)
            for r in tiles(reach):
                tm, ts = cross(work, 1 - now, r, lane)
                layer(z, now, r, 0, dm[z, r : r + SUB, :], tm)
                layer(z, now, r, 1, ds[z, r : r + SUB, :], ts)
            return carry

        return step

    def ranges(reach_of, zs):
        runs = []
        for z in zs:
            if runs and up8(reach_of(z)) == up8(reach_of(runs[-1][0])):
                runs[-1][1] = z
            else:
                runs.append([z, z])
        return runs

    for lo, hi in ranges(lambda z: 2 * (nz - 1) - z, range(1, nz)):
        lax.fori_loop(lo, hi + 1, forward(2 * (nz - 1) - lo), 0)

    def back(z, now, r, total):
        inside = top <= r < top + rows
        for half, spread in enumerate(total):
            adjoint = (cm, cs)[half][z, r : r + SUB, :]
            if spread is not None:
                adjoint = adjoint + slope[z, half, r : r + SUB, :] * spread
            work[now, half, SUB + r : SUB + r + SUB, :] = adjoint * weight[z, half, r : r + SUB, :]
            if half == 0 and inside:
                k = r - top
                gradient[z, k : k + SUB, :] = adjoint * da[z, k : k + SUB, :]

    for r in tiles(nz - 1):
        back(nz - 1, (nz - 1) % 2, r, (None, None))

    def backward(reach):
        def step(i, carry):
            z = nz - 1 - i
            now = lax.rem(z, 2)
            for r in tiles(reach):
                back(z, now, r, cross(work, 1 - now, r, lane))
            return carry

        return step

    for lo, hi in ranges(lambda z: z, range(nz - 2, 0, -1)):
        lax.fori_loop(nz - 1 - lo, nz - hi, backward(lo), 0)

    for r in range(top, top + rows, SUB):
        spread, _ = cross(work, 1, r, lane)
        k = r - top
        adjoint = cot[0, k : k + SUB, :] + slope[0, 0, r : r + SUB, :] * spread
        gradient[0, k : k + SUB, :] = adjoint * da[0, k : k + SUB, :]


def call(body, outs, n_in, scratch=(), flops=1000):
    return pl.pallas_call(
        body,
        out_shape=[jax.ShapeDtypeStruct(s, jnp.float32) for s in outs],
        in_specs=[VMEM] * n_in,
        out_specs=[VMEM] * len(outs),
        scratch_shapes=[pltpu.VMEM(s, jnp.float32) for s in scratch],
        cost_estimate=pl.CostEstimate(flops=flops, bytes_accessed=flops, transcendentals=0),
    )


def swap(axis, first, last):
    count = lax.axis_size(axis)
    forward = [(i, (i + 1) % count) for i in range(count)]
    backward = [(i, (i - 1) % count) for i in range(count)]
    return lax.ppermute(last, axis, forward), lax.ppermute(first, axis, backward)


def shards(density, cotangent):
    nz, rows, cols = density.shape
    plan = Plan(nz, rows, cols)
    part = functools.partial
    first, last = call(part(pack_rows, plan), [(plan.row_len, cols)] * 2, 2)(density, cotangent)
    above, below = swap("gx", first, last)
    first, last = call(part(pack_columns, plan), [(plan.col_tiles, rows, cols)] * 2, 2)(density, cotangent)
    left, right = swap("gy", first, last)
    first, last = call(part(pack_corners, plan), [(plan.corner_tiles, SUB, cols)] * 2, 2)(left, right)
    cabove, cbelow = swap("gx", first, last)
    full = rows + 2 * plan.halo
    scratch = [(nz, full, cols)] * 4
    scratch += [(2, 2, full + 2 * SUB, cols), (nz, 2, full, cols), (nz, 2, full, cols), (nz, rows, cols)]
    body = call(part(filter_body, plan), [(nz, rows, cols)] * 2, 8, scratch)
    return tuple(body(density, cotangent, above, below, left, right, cabove, cbelow))


def solution(mesh):
    placed = P(None, "gx", "gy")
    return jax.shard_map(
        shards,
        mesh=mesh,
        in_specs=(placed, placed),
        out_specs=(placed, placed),
        check_vma=False,
    )
```

time: 148 us -> 42.4 us (0.29)
  waiting for transfers between devices: 69.9 us -> 7.33 us
  starting transfers between devices: 52.9 us -> 10.4 us
  Pallas kernels: 0 us -> 21.1 us
  other arithmetic: 14.3 us -> 0 us
  local copies, waits for them, and re-layouts: 8.43 us -> 2.69 us
    ppermute x48 -> x6, waiting for transfers between devices: 69.9 us -> 7.33 us  [the longest x3 5.84 us: swap(): lax.ppermute(last, axis, forward)]
    ppermute x48 -> x6, starting transfers between devices: 52.9 us -> 10.4 us  [the longest x3 6.35 us: swap(): lax.ppermute(first, axis, backward)]
    pallas_call x0 -> x4, Pallas kernels: none -> 21.1 us  [the longest x1 14.7 us: shards(): body(density, cotangent, above, below, left, right, cabove, cbelow)]
    div x30 -> x0, other arithmetic: 6.18 us -> none  [backward_block(): carried = adjoint * 0.5 * (1.0 + diff / root) * level / total]
    pow x16 -> x0, other arithmetic: 3.42 us -> none  [forward_block(): total = cross(prev ** power_p)]
    concatenate x20 -> x0, other arithmetic: 2.84 us -> none  [with_halo(): block = jnp.concatenate([low, block, high], axis=dim)]
    slice x24 -> x0, local copies, waits for them, and re-layouts: 1.72 us -> none  [with_halo(): lax.slice_in_dim(block, block.shape[dim] - width, None, axis=dim)]
    unnamed x8 -> x12, local copies, waits for them, and re-layouts: 3.48 us -> 2.69 us
  transfers between devices with their start and end apart: 48 -> 6, of which waited for: 30 -> 3; matrix products, arithmetic and copies ran while one was open for 3% -> 0% of each run, Pallas kernels for 0% -> 10%
where the time goes in v1:
time: 42.4 us; the launch traced here: 42.2 us
  Pallas kernels  21.1 us (50%)
  starting transfers between devices  10.4 us (25%)
  waiting for transfers between devices  7.33 us (17%)
  local copies, waits for them, and re-layouts  2.69 us (6%)
  between operations  0.65 us (2%)
    pallas_call x1, Pallas kernels, shards(): body(density, cotangent, above, below, left, right, cabove, cbelow)  14.7 us
    ppermute x3, starting transfers between devices, swap(): lax.ppermute(first, axis, backward)  6.35 us
    ppermute x3, waiting for transfers between devices, swap(): lax.ppermute(last, axis, forward)  5.84 us
    ppermute x3, starting transfers between devices, swap(): lax.ppermute(last, axis, forward)  4.04 us
    unnamed x12, local copies, waits for them, and re-layouts  2.69 us
    pallas_call x1, Pallas kernels, shards(): call(part(pack_columns, plan), [(plan.col_tiles, rows, cols)] * 2, 2)  2.42 us
    pallas_call x1, Pallas kernels, shards(): call(part(pack_rows, plan), [(plan.row_len, cols)] * 2, 2)  2.02 us
    pallas_call x1, Pallas kernels, shards(): call(part(pack_corners, plan), [(plan.corner_tiles, SUB, cols)] * 2, 2)  1.97 us
  transfers between devices with their start and end apart: 6, of which 3 were waited for; matrix products, arithmetic and copies ran while one was open for 0% of the time, Pallas kernels for 10%

profile of v1, /device:TPU:0, one launch (start us, length us, event | category | flops | bytes accessed | tf_op | source)
XLA Modules:
  0.0 42.2 jit_solution(15576232844195055238)
XLA Ops:
  0.6 2.0 %shard_map.41 = (f32[496,128]{1,0:T(8,128)}, f32[496,128]{1,0:T(8,128)}) custom-call(f32[16,64,128]{2,1,0:T(8,128)} %dens.5, f32[16,64,128]{2,1,0:T(8,128)} %cot.5), custom_call_target="tpu_custom_call" | custom-call | flops 1000 | bytes 1000 | tf_op jit(solution)/shard_map/pallas_call | solution.py:289
  2.7 3.0 %collective-permute-start = (f32[496,128]{1,0:T(8,128)}, f32[496,128]{1,0:T(8,128)S(1)}, u32[]{:S(2)}, u32[]{:S(2)}) collective-permute-start(f32[496,128]{1,0:T(8,128)} %get-tuple-element.8), channel_id=1, source_target_pairs={{0,8},{8,16},{16,24},{24,0},{1,9},{9,17},{17,25},{25,1},{2,10},{10... | collective-permute-start | bytes 761864 | tf_op jit(solution)/shard_map/ppermute | solution.py:282
  5.6 1.0 %collective-permute-start.1 = (f32[496,128]{1,0:T(8,128)}, f32[496,128]{1,0:T(8,128)S(1)}, u32[]{:S(2)}, u32[]{:S(2)}) collective-permute-start(f32[496,128]{1,0:T(8,128)} %get-tuple-element.9), channel_id=1, source_target_pairs={{0,24},{8,0},{16,8},{24,16},{1,25},{9,1},{17,9},{25,17},{2,26},{10... | collective-permute-start | bytes 761864 | tf_op jit(solution)/shard_map/ppermute | solution.py:282
  6.6 2.4 %shard_map.42 = (f32[4,64,128]{2,1,0:T(8,128)}, f32[4,64,128]{2,1,0:T(8,128)}) custom-call(f32[16,64,128]{2,1,0:T(8,128)} %dens.5, f32[16,64,128]{2,1,0:T(8,128)} %cot.5), custom_call_target="tpu_custom_call" | custom-call | flops 1000 | bytes 1000 | tf_op jit(solution)/shard_map/pallas_call | solution.py:291
  9.0 0.0 collective-permute-start.2
  9.0 3.5 %collective-permute-start.3 = (f32[4,64,128]{2,1,0:T(8,128)}, f32[4,64,128]{2,1,0:T(8,128)S(1)}, u32[]{:S(2)}, u32[]{:S(2)}) collective-permute-start(f32[4,64,128]{2,1,0:T(8,128)} %get-tuple-element.11), channel_id=1, source_target_pairs={{0,7},{1,0},{2,1},{3,2},{4,3},{5,4},{6,5},{7,6},{8,15},{9,8},{10,9... | collective-permute-start | bytes 393224 | tf_op jit(solution)/shard_map/ppermute | solution.py:282
  12.5 3.0 %collective-permute-done.2.left = f32[4,64,128]{2,1,0:T(8,128)S(1)} collective-permute-done((f32[4,64,128]{2,1,0:T(8,128)}, f32[4,64,128]{2,1,0:T(8,128)S(1)}, u32[]{:S(2)}, u32[]{:S(2)}) %collective-permute-start.2) | collective-permute-done | bytes 131104 | tf_op jit(solution)/shard_map/ppermute | solution.py:282
  15.5 0.0 copy-start
  15.5 0.0 collective-permute-done.3.right
  15.5 0.6 %copy-done = f32[4,64,128]{2,1,0:T(8,128)} copy-done((f32[4,64,128]{2,1,0:T(8,128)}, f32[4,64,128]{2,1,0:T(8,128)S(1)}, u32[]{:S(2)}) %copy-start) | copy-done | bytes 131096
  16.1 0.0 copy-start.1
  16.1 0.7 %copy-done.1 = f32[4,64,128]{2,1,0:T(8,128)} copy-done((f32[4,64,128]{2,1,0:T(8,128)}, f32[4,64,128]{2,1,0:T(8,128)S(1)}, u32[]{:S(2)}) %copy-start.1) | copy-done | bytes 131096
  16.8 2.0 %shard_map.43 = (f32[13,8,128]{2,1,0:T(8,128)}, f32[13,8,128]{2,1,0:T(8,128)}) custom-call(f32[4,64,128]{2,1,0:T(8,128)} %copy-done, f32[4,64,128]{2,1,0:T(8,128)} %copy-done.1), custom_call_target="tpu_custom_call" | custom-call | flops 1000 | bytes 1000 | tf_op jit(solution)/shard_map/pallas_call | solution.py:293
  18.8 1.1 %collective-permute-start.4 = (f32[13,8,128]{2,1,0:T(8,128)}, f32[13,8,128]{2,1,0:T(8,128)S(1)}, u32[]{:S(2)}, u32[]{:S(2)}) collective-permute-start(f32[13,8,128]{2,1,0:T(8,128)} %get-tuple-element.12), channel_id=1, source_target_pairs={{0,8},{8,16},{16,24},{24,0},{1,9},{9,17},{17,25},{25,1},{2,10},{10... | collective-permute-start | bytes 159752 | tf_op jit(solution)/shard_map/ppermute | solution.py:282
  19.8 1.9 %collective-permute-start.5 = (f32[13,8,128]{2,1,0:T(8,128)}, f32[13,8,128]{2,1,0:T(8,128)S(1)}, u32[]{:S(2)}, u32[]{:S(2)}) collective-permute-start(f32[13,8,128]{2,1,0:T(8,128)} %get-tuple-element.13), channel_id=1, source_target_pairs={{0,24},{8,0},{16,8},{24,16},{1,25},{9,1},{17,9},{25,17},{2,26},{10... | collective-permute-start | bytes 159752 | tf_op jit(solution)/shard_map/ppermute | solution.py:282
  21.7 2.9 %collective-permute-done.4.cabove = f32[13,8,128]{2,1,0:T(8,128)S(1)} collective-permute-done((f32[13,8,128]{2,1,0:T(8,128)}, f32[13,8,128]{2,1,0:T(8,128)S(1)}, u32[]{:S(2)}, u32[]{:S(2)}) %collective-permute-start.4) | collective-permute-done | bytes 53280 | tf_op jit(solution)/shard_map/ppermute | solution.py:282
  24.6 0.0 copy-start.4
  24.6 1.5 %collective-permute-done.5.cbelow = f32[13,8,128]{2,1,0:T(8,128)S(1)} collective-permute-done((f32[13,8,128]{2,1,0:T(8,128)}, f32[13,8,128]{2,1,0:T(8,128)S(1)}, u32[]{:S(2)}, u32[]{:S(2)}) %collective-permute-start.5) | collective-permute-done | bytes 53280 | tf_op jit(solution)/shard_map/ppermute | solution.py:282
  26.1 0.0 copy-start.5
  26.1 0.0 collective-permute-done.above
  26.1 0.0 copy-start.2
  26.1 0.0 collective-permute-done.1.below
  26.1 0.0 copy-done.4
  26.1 0.6 %copy-done.5 = f32[13,8,128]{2,1,0:T(8,128)} copy-done((f32[13,8,128]{2,1,0:T(8,128)}, f32[13,8,128]{2,1,0:T(8,128)S(1)}, u32[]{:S(2)}) %copy-start.5) | copy-done | bytes 53272
  26.7 0.1 copy-done.2
  26.8 0.0 copy-start.3
  26.8 0.7 %copy-done.3 = f32[496,128]{1,0:T(8,128)} copy-done((f32[496,128]{1,0:T(8,128)}, f32[496,128]{1,0:T(8,128)S(1)}, u32[]{:S(2)}) %copy-start.3) | copy-done | bytes 253976
  27.5 14.7 %shard_map.44 = (f32[16,64,128]{2,1,0:T(8,128)}, f32[16,64,128]{2,1,0:T(8,128)}) custom-call(f32[16,64,128]{2,1,0:T(8,128)} %dens.5, f32[16,64,128]{2,1,0:T(8,128)} %cot.5, f32[496,128]{1,0:T(8,128)} %copy-done.2, f32[496,128]{1,0:T(8,128)} %copy-done.3, f32[4,64,128]{2,1,0:T(8,128)} %copy-done, f32[4,64,128]{2,1,0:T(8,128)} %copy-done.1, ...), custom_call_target="tpu_custom_call" | custom-call | flops 1000 | bytes 1000 | tf_op jit(solution)/shard_map/pallas_call | solution.py:299
Async XLA Ops:
  2.7 23.4 %collective-permute-start = (f32[496,128]{1,0:T(8,128)}, f32[496,128]{1,0:T(8,128)S(1)}, u32[]{:S(2)}, u32[]{:S(2)}) collective-permute-start(f32[496,128]{1,0:T(8,128)} %get-tuple-element.8), channel_id=1, source_target_pairs={{0,8},{8,16},{16,24},{24,0},{1,9},{9,17},{17,25},{25,1},{2,10},{10... | collective-permute-start | bytes 761864 | tf_op jit(solution)/shard_map/ppermute | solution.py:282
  5.6 20.5 %collective-permute-start.1 = (f32[496,128]{1,0:T(8,128)}, f32[496,128]{1,0:T(8,128)S(1)}, u32[]{:S(2)}, u32[]{:S(2)}) collective-permute-start(f32[496,128]{1,0:T(8,128)} %get-tuple-element.9), channel_id=1, source_target_pairs={{0,24},{8,0},{16,8},{24,16},{1,25},{9,1},{17,9},{25,17},{2,26},{10... | collective-permute-start | bytes 761864 | tf_op jit(solution)/shard_map/ppermute | solution.py:282
  9.0 6.5 %collective-permute-start.2 = (f32[4,64,128]{2,1,0:T(8,128)}, f32[4,64,128]{2,1,0:T(8,128)S(1)}, u32[]{:S(2)}, u32[]{:S(2)}) collective-permute-start(f32[4,64,128]{2,1,0:T(8,128)} %get-tuple-element.10), channel_id=1, source_target_pairs={{0,1},{1,2},{2,3},{3,4},{4,5},{5,6},{6,7},{7,0},{8,9},{9,10},{10,1... | collective-permute-start | bytes 393224 | tf_op jit(solution)/shard_map/ppermute | solution.py:282
  9.0 6.5 %collective-permute-start.3 = (f32[4,64,128]{2,1,0:T(8,128)}, f32[4,64,128]{2,1,0:T(8,128)S(1)}, u32[]{:S(2)}, u32[]{:S(2)}) collective-permute-start(f32[4,64,128]{2,1,0:T(8,128)} %get-tuple-element.11), channel_id=1, source_target_pairs={{0,7},{1,0},{2,1},{3,2},{4,3},{5,4},{6,5},{7,6},{8,15},{9,8},{10,9... | collective-permute-start | bytes 393224 | tf_op jit(solution)/shard_map/ppermute | solution.py:282
  15.5 0.6 %copy-start = (f32[4,64,128]{2,1,0:T(8,128)}, f32[4,64,128]{2,1,0:T(8,128)S(1)}, u32[]{:S(2)}) copy-start(f32[4,64,128]{2,1,0:T(8,128)S(1)} %collective-permute-done.2.left) | copy-start | bytes 393220
  16.1 0.7 %copy-start.1 = (f32[4,64,128]{2,1,0:T(8,128)}, f32[4,64,128]{2,1,0:T(8,128)S(1)}, u32[]{:S(2)}) copy-start(f32[4,64,128]{2,1,0:T(8,128)S(1)} %collective-permute-done.3.right) | copy-start | bytes 393220
  18.8 5.8 %collective-permute-start.4 = (f32[13,8,128]{2,1,0:T(8,128)}, f32[13,8,128]{2,1,0:T(8,128)S(1)}, u32[]{:S(2)}, u32[]{:S(2)}) collective-permute-start(f32[13,8,128]{2,1,0:T(8,128)} %get-tuple-element.12), channel_id=1, source_target_pairs={{0,8},{8,16},{16,24},{24,0},{1,9},{9,17},{17,25},{25,1},{2,10},{10... | collective-permute-start | bytes 159752 | tf_op jit(solution)/shard_map/ppermute | solution.py:282
  19.8 6.2 %collective-permute-start.5 = (f32[13,8,128]{2,1,0:T(8,128)}, f32[13,8,128]{2,1,0:T(8,128)S(1)}, u32[]{:S(2)}, u32[]{:S(2)}) collective-permute-start(f32[13,8,128]{2,1,0:T(8,128)} %get-tuple-element.13), channel_id=1, source_target_pairs={{0,24},{8,0},{16,8},{24,16},{1,25},{9,1},{17,9},{25,17},{2,26},{10... | collective-permute-start | bytes 159752 | tf_op jit(solution)/shard_map/ppermute | solution.py:282
  24.6 1.5 %copy-start.4 = (f32[13,8,128]{2,1,0:T(8,128)}, f32[13,8,128]{2,1,0:T(8,128)S(1)}, u32[]{:S(2)}) copy-start(f32[13,8,128]{2,1,0:T(8,128)S(1)} %collective-permute-done.4.cabove) | copy-start | bytes 159748
  26.1 0.6 %copy-start.5 = (f32[13,8,128]{2,1,0:T(8,128)}, f32[13,8,128]{2,1,0:T(8,128)S(1)}, u32[]{:S(2)}) copy-start(f32[13,8,128]{2,1,0:T(8,128)S(1)} %collective-permute-done.5.cbelow) | copy-start | bytes 159748
  26.1 0.7 %copy-start.2 = (f32[496,128]{1,0:T(8,128)}, f32[496,128]{1,0:T(8,128)S(1)}, u32[]{:S(2)}) copy-start(f32[496,128]{1,0:T(8,128)S(1)} %collective-permute-done.above) | copy-start | bytes 761860
  26.8 0.7 %copy-start.3 = (f32[496,128]{1,0:T(8,128)}, f32[496,128]{1,0:T(8,128)S(1)}, u32[]{:S(2)}) copy-start(f32[496,128]{1,0:T(8,128)S(1)} %collective-permute-done.1.below) | copy-start | bytes 761860

commit v2 on v1

v2 whole, which is shorter than its diff:
```python
import functools
import math

import jax
import jax.numpy as jnp
from jax import lax
from jax.experimental import pallas as pl
from jax.experimental.pallas import tpu as pltpu
from jax.sharding import PartitionSpec as P

power_p = 20.0
root_q = 20.0 + math.log(5.0) / math.log(0.1)
smooth_eps = 0.0001
SUB = 8

VMEM = pl.BlockSpec(memory_space=pltpu.VMEM)


def up8(n):
    return -(-n // SUB) * SUB


class Plan:
    def __init__(self, layers, rows, cols):
        self.nz, self.rows, self.cols = layers, rows, cols
        self.fields = [(0, z, 2 * (layers - 1) - z) for z in range(layers)]
        self.fields += [(1, z, z) for z in range(layers - 1, 0, -1)]
        far = 2 * (layers - 1)
        self.halo = up8(far)
        self.row_at = {}
        at = SUB
        for arr, z, d in self.fields:
            self.row_at[arr, z] = at
            at += d
        self.row_len = up8(at) + SUB
        self.col_at, self.col_tiles = self.fit([((arr, z), d) for arr, z, d in self.fields])
        items = []
        for arr, z, d in self.fields:
            for k in range(-(-(d - 1) // SUB)):
                items.append(((arr, z, k), 2 * (d - 1 - SUB * k)))
        self.corner_at, self.corner_tiles = self.fit(items)

    def fit(self, items):
        room, where = [], {}
        for key, width in sorted(items, key=lambda item: -item[1]):
            for tile, used in enumerate(room):
                if used + width <= self.cols:
                    break
            else:
                tile = len(room)
                room.append(0)
            where[key] = (tile, room[tile])
            room[tile] += width
        return where, len(room)


def shift(x, amount):
    amount %= x.shape[1]
    return x if amount == 0 else pltpu.roll(x, amount, 1)


def lanes_of(shape):
    return lax.broadcasted_iota(jnp.int32, shape, 1)


def pack_rows(plan, dens, cot, first, last):
    for arr, z, d in plan.fields:
        src = (dens, cot)[arr]
        at = plan.row_at[arr, z]
        first[at : at + d, :] = src[z, :d, :]
        last[at : at + d, :] = src[z, plan.rows - d :, :]
    end = plan.row_at[1, 1] + 1
    for ref in (first, last):
        ref[:SUB, :] = jnp.zeros((SUB, plan.cols), jnp.float32)
        ref[end:, :] = jnp.zeros((plan.row_len - end, plan.cols), jnp.float32)


def pack_columns(plan, dens, cot, first, last):
    n = plan.cols
    lane = lanes_of((SUB, n))
    for tile in range(plan.col_tiles):
        inside = [f for f in plan.fields if plan.col_at[f[0], f[1]][0] == tile]
        inside.sort(key=lambda f: plan.col_at[f[0], f[1]][1])
        for r in range(0, plan.rows, SUB):
            one, two = None, None
            for arr, z, d in inside:
                at = plan.col_at[arr, z][1]
                x = (dens, cot)[arr][z, r : r + SUB, :]
                a, b = shift(x, at), shift(x, at + d)
                if one is None:
                    one, two = a, b
                else:
                    here = lane >= at
                    one, two = jnp.where(here, a, one), jnp.where(here, b, two)
            first[tile, r : r + SUB, :] = one
            last[tile, r : r + SUB, :] = two


def pack_corners(plan, left, right, first, last):
    lane = lanes_of((SUB, plan.cols))
    out = [[None] * plan.corner_tiles, [None] * plan.corner_tiles]
    order = sorted(plan.corner_at.items(), key=lambda item: item[1][1])
    reach = {(arr, z): d for arr, z, d in plan.fields}
    for (arr, z, k), (tile, at) in order:
        d = reach[arr, z]
        w = d - 1 - SUB * k
        ctile, cat = plan.col_at[arr, z]
        for way in range(2):
            r = SUB * k if way == 0 else plan.rows - SUB * (k + 1)
            a = shift(left[ctile, r : r + SUB, :], at - (cat + d - w))
            b = shift(right[ctile, r : r + SUB, :], at + w - cat)
            both = jnp.where(lane >= at + w, b, a)
            prev = out[way][tile]
            out[way][tile] = both if prev is None else jnp.where(lane >= at, both, prev)
    for tile in range(plan.corner_tiles):
        first[tile] = out[0][tile]
        last[tile] = out[1][tile]


def unpack_columns(plan, left, right, *sides):
    n = plan.cols
    low = lanes_of((SUB, n)) < n // 2
    for arr, z, d in plan.fields:
        tile, at = plan.col_at[arr, z]
        for r in range(0, plan.rows, SUB):
            x = shift(left[tile, r : r + SUB, :], -(at + d))
            y = shift(right[tile, r : r + SUB, :], -at)
            sides[arr][z, r : r + SUB, :] = jnp.where(low, y, x)


def unpack_halo(plan, arr, above, below, cabove, cbelow, main, side):
    top = plan.halo
    for a, z, d in plan.fields:
        if a != arr:
            continue
        at = plan.row_at[arr, z]
        for k in range(-(-d // SUB)):
            lo, hi = top - SUB * (k + 1), top + SUB * k
            main[z, lo : lo + SUB, :] = above[at + d - SUB * (k + 1) : at + d - SUB * k, :]
            main[z, hi : hi + SUB, :] = below[at + SUB * k : at + SUB * (k + 1), :]
            w = d - 1 - SUB * k
            if w > 0:
                tile, cor = plan.corner_at[arr, z, k]
                side[z, lo : lo + SUB, :] = shift(cabove[tile], -(cor + w))
                side[z, hi : hi + SUB, :] = shift(cbelow[tile], -(cor + w))


def cross(ref, r, lane):
    n = lane.shape[1]
    b = SUB + r
    m, s = ref[0, b : b + SUB, :], ref[1, b : b + SUB, :]
    m1, s1 = pltpu.roll(m, 1, 1), pltpu.roll(s, 1, 1)
    m2, s2 = pltpu.roll(m, n - 1, 1), pltpu.roll(s, n - 1, 1)
    vm = m + ref[0, b - 1 : b + SUB - 1, :] + ref[0, b + 1 : b + SUB + 1, :]
    vs = s + ref[1, b - 1 : b + SUB - 1, :] + ref[1, b + 1 : b + SUB + 1, :]
    start, end = lane == 0, lane == n - 1
    hm = jnp.where(start, s1, m1) + jnp.where(end, s2, m2)
    hs = jnp.where(start, m1, s1) + jnp.where(end, m2, s2)
    return vm + hm, vs + hs


def filter_body(
    plan, dens, cot, dens_side, cot_side, above, below, cabove, cbelow,
    printed_out, gradient_out, dmh, dsh, cmh, csh, even, odd, slope, weight, da, printed, gradient, sems,
):
    nz, rows, n, top = plan.nz, plan.rows, plan.cols, plan.halo
    lane = lanes_of((SUB, n))
    full = top + rows + top
    unpack_halo(plan, 0, above, below, cabove, cbelow, dmh, dsh)

    margin = jnp.ones((SUB, n), jnp.float32)
    for ref in (even, odd):
        for half in range(2):
            ref[half, :SUB, :] = margin
            ref[half, SUB + full :, :] = margin

    def tiles(reach):
        depth = up8(max(reach, 0))
        return range(top - depth, top + rows + depth, SUB)

    def inside(r):
        return top <= r < top + rows

    def field(blocks, halos, half, z, r):
        if inside(r):
            return blocks[half][z, r - top : r - top + SUB, :]
        at = r if r < top else r - rows
        return halos[half][z, at : at + SUB, :]

    coef = up8(nz - 1)

    def layer(z, out, r, half, total):
        density = field((dens, dens_side), (dmh, dsh), half, z, r)
        if total is None:
            level = jnp.ones_like(density)
        else:
            lg = jnp.log(total)
            level = jnp.exp2(lg * jnp.float32(1.0 / (root_q * math.log(2.0))))
        diff = density - level
        square = diff * diff + smooth_eps
        inv = lax.rsqrt(square)
        value = 0.5 * (density + level - square * inv + math.sqrt(smooth_eps))
        p2 = value * value
        p4 = p2 * p2
        p16 = (p4 * p4) * (p4 * p4)
        out[half, SUB + r : SUB + r + SUB, :] = p16 * p4
        if top - coef <= r < top + rows + coef:
            hu = 0.5 * (diff * inv)
            slope[z, half, r : r + SUB, :] = jnp.float32(power_p / root_q) * (p16 * (p2 * value))
            if total is not None:
                ratio = jnp.exp2(lg * jnp.float32((1.0 / root_q - 1.0) / math.log(2.0)))
                weight[z, half, r : r + SUB, :] = (0.5 + hu) * ratio
            if half == 0 and inside(r):
                printed[z, r - top : r - top + SUB, :] = value
                da[z, r - top : r - top + SUB, :] = 0.5 - hu

    for r in tiles(2 * (nz - 1)):
        for half in range(2):
            layer(0, even, r, half, None)

    refs = (even, odd)

    def forward(z, parity, reach):
        for r in tiles(reach):
            for half, total in enumerate(cross(refs[1 - parity], r, lane)):
                layer(z, refs[parity], r, half, total)

    def runs(reach_of, zs):
        found = []
        for z in zs[: len(zs) // 2 * 2 : 2]:
            if found and up8(reach_of(z)) == up8(reach_of(found[-1][0])):
                found[-1].append(z)
            else:
                found.append([z])
        return found

    def reach(z):
        return 2 * (nz - 1) - z

    later = list(range(1, nz))
    for run in runs(reach, later):

        def pair(i, carry, run=run):
            z = run[0] + 2 * i
            forward(z, run[0] % 2, reach(run[0]))
            forward(z + 1, (run[0] + 1) % 2, reach(run[0] + 1))
            return carry

        lax.fori_loop(0, len(run), pair, 0)
    if len(later) % 2:
        forward(later[-1], later[-1] % 2, reach(later[-1]))

    send = pltpu.make_async_copy(printed, printed_out, sems.at[0])
    send.start()
    unpack_halo(plan, 1, above, below, cabove, cbelow, cmh, csh)

    def back(z, out, r, spreads):
        for half, spread in enumerate(spreads):
            adjoint = field((cot, cot_side), (cmh, csh), half, z, r)
            if spread is not None:
                adjoint = adjoint + slope[z, half, r : r + SUB, :] * spread
            out[half, SUB + r : SUB + r + SUB, :] = adjoint * weight[z, half, r : r + SUB, :]
            if half == 0 and inside(r):
                k = r - top
                gradient[z, k : k + SUB, :] = adjoint * da[z, k : k + SUB, :]

    for r in tiles(nz - 1):
        back(nz - 1, refs[(nz - 1) % 2], r, (None, None))

    def backward(z, parity, reach):
        for r in tiles(reach):
            back(z, refs[parity], r, cross(refs[1 - parity], r, lane))

    later = list(range(nz - 2, 0, -1))
    for run in runs(lambda z: z, later):

        def pair(i, carry, run=run):
            z = run[0] - 2 * i
            backward(z, run[0] % 2, run[0])
            backward(z - 1, (run[0] + 1) % 2, run[0] - 1)
            return carry

        lax.fori_loop(0, len(run), pair, 0)
    if len(later) % 2:
        backward(later[-1], later[-1] % 2, later[-1])

    for r in range(top, top + rows, SUB):
        spread, _ = cross(odd, r, lane)
        k = r - top
        adjoint = cot[0, k : k + SUB, :] + slope[0, 0, r : r + SUB, :] * spread
        gradient[0, k : k + SUB, :] = adjoint * da[0, k : k + SUB, :]
    other = pltpu.make_async_copy(gradient, gradient_out, sems.at[1])
    other.start()
    send.wait()
    other.wait()


def near(x):
    return pltpu.with_memory_space_constraint(x, pltpu.VMEM)


def call(body, outs, *args, flops=100000):
    return pl.pallas_call(
        body,
        out_shape=[pltpu.VMEM(s, jnp.float32) for s in outs],
        in_specs=[VMEM] * len(args),
        out_specs=[VMEM] * len(outs),
        cost_estimate=pl.CostEstimate(flops=flops, bytes_accessed=flops, transcendentals=0),
        compiler_params=pltpu.CompilerParams(vmem_limit_bytes=4 << 20),
    )(*[near(x) for x in args])


def swap(axis, first, last):
    count = lax.axis_size(axis)
    forward = [(i, (i + 1) % count) for i in range(count)]
    backward = [(i, (i - 1) % count) for i in range(count)]
    return lax.ppermute(last, axis, forward), lax.ppermute(first, axis, backward)


def shards(density, cotangent):
    nz, rows, cols = density.shape
    plan = Plan(nz, rows, cols)
    part = functools.partial
    block = (nz, rows, cols)
    first, last = call(part(pack_rows, plan), [(plan.row_len, cols)] * 2, density, cotangent)
    above, below = swap("gx", first, last)
    first, last = call(part(pack_columns, plan), [(plan.col_tiles, rows, cols)] * 2, density, cotangent)
    left, right = swap("gy", first, last)
    first, last = call(part(pack_corners, plan), [(plan.corner_tiles, SUB, cols)] * 2, left, right)
    cabove, cbelow = swap("gx", first, last)
    sides = call(part(unpack_columns, plan), [block] * 2, left, right)
    full = rows + 2 * plan.halo
    halo = (nz, 2 * plan.halo, cols)
    work = (2, full + 2 * SUB, cols)
    scratch = [halo] * 4 + [work] * 2 + [(nz, 2, full, cols)] * 2 + [block] * 3
    args = (density, cotangent, *sides, above, below, cabove, cbelow)
    outs = pl.pallas_call(
        part(filter_body, plan),
        out_shape=[jax.ShapeDtypeStruct(block, jnp.float32)] * 2,
        in_specs=[VMEM] * len(args),
        out_specs=[pl.BlockSpec(memory_space=pltpu.HBM)] * 2,
        scratch_shapes=[pltpu.VMEM(s, jnp.float32) for s in scratch] + [pltpu.SemaphoreType.DMA((2,))],
        cost_estimate=pl.CostEstimate(flops=10000000, bytes_accessed=1000000, transcendentals=0),
        compiler_params=pltpu.CompilerParams(vmem_limit_bytes=24 << 20),
    )(*[near(x) for x in args])
    return tuple(outs)


def solution(mesh):
    placed = P(None, "gx", "gy")
    return jax.shard_map(
        shards,
        mesh=mesh,
        in_specs=(placed, placed),
        out_specs=(placed, placed),
        check_vma=False,
    )
```

time: 42.4 us -> 26.3 us (0.62)
  Pallas kernels: 21.1 us -> 6.62 us
  waiting for transfers between devices: 7.33 us -> 6.06 us
  local copies, waits for them, and re-layouts: 2.69 us -> 2.09 us
    pallas_call x4 -> x5, Pallas kernels: 21.1 us -> 6.62 us  [the longest x1 5.18 us: shards(): pl.pallas_call(part(filter_body, plan), out_shape=[jax.ShapeDtypeStruct(b...]
    ppermute x3, waiting for transfers between devices: 5.84 us -> 4.44 us  [swap(): lax.ppermute(last, axis, forward)]
    unnamed x12 -> x8, local copies, waits for them, and re-layouts: 2.69 us -> 2.09 us
  transfers between devices with their start and end apart: 6 -> 6, of which waited for: 3 -> 3; matrix products, arithmetic and copies ran while one was open for 0% -> 0% of each run, Pallas kernels for 10% -> 5%
where the time goes in v2:
time: 26.3 us; the launch traced here: 26.1 us
  starting transfers between devices  10.6 us (40%)
  Pallas kernels  6.62 us (25%)
  waiting for transfers between devices  6.06 us (23%)
  local copies, waits for them, and re-layouts  2.09 us (8%)
  between operations  0.7 us (3%)
    ppermute x3, starting transfers between devices, swap(): lax.ppermute(first, axis, backward)  6.47 us
    pallas_call x1, Pallas kernels, shards(): pl.pallas_call(part(filter_body, plan), out_shape=[jax.ShapeDtypeStruct(b...  5.18 us
    ppermute x3, waiting for transfers between devices, swap(): lax.ppermute(last, axis, forward)  4.44 us
    ppermute x3, starting transfers between devices, swap(): lax.ppermute(last, axis, forward)  4.13 us
    unnamed x8, local copies, waits for them, and re-layouts  2.09 us
    ppermute x3, waiting for transfers between devices, swap(): lax.ppermute(first, axis, backward)  1.62 us
    pallas_call x4, Pallas kernels, call(): pl.pallas_call(body, out_shape=[pltpu.VMEM(s, jnp.float32) for s in outs]...  1.44 us
  transfers between devices with their start and end apart: 6, of which 3 were waited for; matrix products, arithmetic and copies ran while one was open for 0% of the time, Pallas kernels for 5%

profile of v2, /device:TPU:0, one launch (start us, length us, event | category | flops | bytes accessed | tf_op | source)
XLA Modules:
  0.0 26.1 jit_solution(12290624574654039725)
XLA Ops:
  0.6 0.0 copy-start
  0.6 1.0 %copy-done = f32[16,64,128]{2,1,0:T(8,128)S(1)} copy-done((f32[16,64,128]{2,1,0:T(8,128)S(1)}, f32[16,64,128]{2,1,0:T(8,128)}, u32[]{:S(2)}) %copy-start) | copy-done | bytes 524312
  1.7 0.0 copy-start.2
  1.7 1.0 %copy-done.2 = f32[16,64,128]{2,1,0:T(8,128)S(1)} copy-done((f32[16,64,128]{2,1,0:T(8,128)S(1)}, f32[16,64,128]{2,1,0:T(8,128)}, u32[]{:S(2)}) %copy-start.2) | copy-done | bytes 524312
  2.8 3.0 %collective-permute-start.2 = (f32[496,128]{1,0:T(8,128)S(1)}, f32[496,128]{1,0:T(8,128)S(1)}, u32[]{:S(2)}, u32[]{:S(2)}) collective-permute-start(f32[496,128]{1,0:T(8,128)S(1)} %get-tuple-element.14), channel_id=1, source_target_pairs={{0,8},{8,16},{16,24},{24,0},{1,9},{9,17},{17,25},{25,1},{2,10},{10... | collective-permute-start | bytes 761864 | tf_op jit(solution)/shard_map/ppermute | solution.py:317
  5.8 1.0 %collective-permute-start.3 = (f32[496,128]{1,0:T(8,128)S(1)}, f32[496,128]{1,0:T(8,128)S(1)}, u32[]{:S(2)}, u32[]{:S(2)}) collective-permute-start(f32[496,128]{1,0:T(8,128)S(1)} %get-tuple-element.15), channel_id=1, source_target_pairs={{0,24},{8,0},{16,8},{24,16},{1,25},{9,1},{17,9},{25,17},{2,26},{10... | collective-permute-start | bytes 761864 | tf_op jit(solution)/shard_map/ppermute | solution.py:317
  6.8 0.0 copy-start.3
  6.8 0.5 %shard_map.41 = (f32[4,64,128]{2,1,0:T(8,128)S(1)}, f32[4,64,128]{2,1,0:T(8,128)S(1)}) custom-call(f32[16,64,128]{2,1,0:T(8,128)S(1)} %copy-done, f32[16,64,128]{2,1,0:T(8,128)S(1)} %copy-done.2), custom_call_target="tpu_custom_call" | custom-call | flops 100000 | bytes 100000 | tf_op jit(solution)/shard_map/pallas_call | solution.py:303
  7.3 0.0 copy-start.1
  7.3 0.1 collective-permute-start
  7.4 3.5 %collective-permute-start.1 = (f32[4,64,128]{2,1,0:T(8,128)S(1)}, f32[4,64,128]{2,1,0:T(8,128)S(1)}, u32[]{:S(2)}, u32[]{:S(2)}) collective-permute-start(f32[4,64,128]{2,1,0:T(8,128)S(1)} %get-tuple-element.11), channel_id=1, source_target_pairs={{0,7},{1,0},{2,1},{3,2},{4,3},{5,4},{6,5},{7,6},{8,15},{9,8},{10,9... | collective-permute-start | bytes 393224 | tf_op jit(solution)/shard_map/ppermute | solution.py:317
  10.9 2.7 %collective-permute-done.left = f32[4,64,128]{2,1,0:T(8,128)S(1)} collective-permute-done((f32[4,64,128]{2,1,0:T(8,128)S(1)}, f32[4,64,128]{2,1,0:T(8,128)S(1)}, u32[]{:S(2)}, u32[]{:S(2)}) %collective-permute-start) | collective-permute-done | bytes 131104 | tf_op jit(solution)/shard_map/ppermute | solution.py:317
  13.7 0.0 collective-permute-done.1.right
  13.7 0.4 %shard_map.44 = (f32[13,8,128]{2,1,0:T(8,128)S(1)}, f32[13,8,128]{2,1,0:T(8,128)S(1)}) custom-call(f32[4,64,128]{2,1,0:T(8,128)S(1)} %collective-permute-done.left, f32[4,64,128]{2,1,0:T(8,128)S(1)} %collective-permute-done.1.right), custom_call_target="tpu_custom_call" | custom-call | flops 100000 | bytes 100000 | tf_op jit(solution)/shard_map/pallas_call | solution.py:303
  14.1 1.1 %collective-permute-start.4 = (f32[13,8,128]{2,1,0:T(8,128)S(1)}, f32[13,8,128]{2,1,0:T(8,128)S(1)}, u32[]{:S(2)}, u32[]{:S(2)}) collective-permute-start(f32[13,8,128]{2,1,0:T(8,128)S(1)} %get-tuple-element.16), channel_id=1, source_target_pairs={{0,8},{8,16},{16,24},{24,0},{1,9},{9,17},{17,25},{25,1},{2,10},{10... | collective-permute-start | bytes 159752 | tf_op jit(solution)/shard_map/ppermute | solution.py:317
  15.1 1.9 %collective-permute-start.5 = (f32[13,8,128]{2,1,0:T(8,128)S(1)}, f32[13,8,128]{2,1,0:T(8,128)S(1)}, u32[]{:S(2)}, u32[]{:S(2)}) collective-permute-start(f32[13,8,128]{2,1,0:T(8,128)S(1)} %get-tuple-element.17), channel_id=1, source_target_pairs={{0,24},{8,0},{16,8},{24,16},{1,25},{9,1},{17,9},{25,17},{2,26},{10... | collective-permute-start | bytes 159752 | tf_op jit(solution)/shard_map/ppermute | solution.py:317
  17.0 0.5 %shard_map.42 = (f32[16,64,128]{2,1,0:T(8,128)S(1)}, f32[16,64,128]{2,1,0:T(8,128)S(1)}) custom-call(f32[4,64,128]{2,1,0:T(8,128)S(1)} %collective-permute-done.left, f32[4,64,128]{2,1,0:T(8,128)S(1)} %collective-permute-done.1.right), custom_call_target="tpu_custom_call" | custom-call | flops 100000 | bytes 100000 | tf_op jit(solution)/shard_map/pallas_call | solution.py:303
  17.6 1.7 %collective-permute-done.4.cabove = f32[13,8,128]{2,1,0:T(8,128)S(1)} collective-permute-done((f32[13,8,128]{2,1,0:T(8,128)S(1)}, f32[13,8,128]{2,1,0:T(8,128)S(1)}, u32[]{:S(2)}, u32[]{:S(2)}) %collective-permute-start.4) | collective-permute-done | bytes 53280 | tf_op jit(solution)/shard_map/ppermute | solution.py:317
  19.3 1.6 %collective-permute-done.5.cbelow = f32[13,8,128]{2,1,0:T(8,128)S(1)} collective-permute-done((f32[13,8,128]{2,1,0:T(8,128)S(1)}, f32[13,8,128]{2,1,0:T(8,128)S(1)}, u32[]{:S(2)}, u32[]{:S(2)}) %collective-permute-start.5) | collective-permute-done | bytes 53280 | tf_op jit(solution)/shard_map/ppermute | solution.py:317
  20.9 0.0 collective-permute-done.2.above
  20.9 0.0 collective-permute-done.3.below
  20.9 0.0 copy-done.3
  20.9 0.0 copy-done.1
  20.9 5.2 %shard_map.45 = (f32[16,64,128]{2,1,0:T(8,128)}, f32[16,64,128]{2,1,0:T(8,128)}) custom-call(f32[16,64,128]{2,1,0:T(8,128)S(1)} %copy-done.1, f32[16,64,128]{2,1,0:T(8,128)S(1)} %copy-done.3, f32[16,64,128]{2,1,0:T(8,128)S(1)} %get-tuple-element.12.dens_side, f32[16,64,128]{2,1,0:T(8,128)S(1)} %get-tuple-element.13.cot_side, ...), custom_call_target="tpu_custom_call" | custom-call | flops 10000000 | bytes 1000000 | tf_op jit(solution)/shard_map/pallas_call | solution.py:337
  (1 shorter events, 0.0 us)
Async XLA Ops:
  0.6 1.0 %copy-start = (f32[16,64,128]{2,1,0:T(8,128)S(1)}, f32[16,64,128]{2,1,0:T(8,128)}, u32[]{:S(2)}) copy-start(f32[16,64,128]{2,1,0:T(8,128)} %dens.5) | copy-start | bytes 1572868
  1.7 1.0 %copy-start.2 = (f32[16,64,128]{2,1,0:T(8,128)S(1)}, f32[16,64,128]{2,1,0:T(8,128)}, u32[]{:S(2)}) copy-start(f32[16,64,128]{2,1,0:T(8,128)} %cot.5) | copy-start | bytes 1572868
  2.8 18.1 %collective-permute-start.2 = (f32[496,128]{1,0:T(8,128)S(1)}, f32[496,128]{1,0:T(8,128)S(1)}, u32[]{:S(2)}, u32[]{:S(2)}) collective-permute-start(f32[496,128]{1,0:T(8,128)S(1)} %get-tuple-element.14), channel_id=1, source_target_pairs={{0,8},{8,16},{16,24},{24,0},{1,9},{9,17},{17,25},{25,1},{2,10},{10... | collective-permute-start | bytes 761864 | tf_op jit(solution)/shard_map/ppermute | solution.py:317
  5.8 15.1 %collective-permute-start.3 = (f32[496,128]{1,0:T(8,128)S(1)}, f32[496,128]{1,0:T(8,128)S(1)}, u32[]{:S(2)}, u32[]{:S(2)}) collective-permute-start(f32[496,128]{1,0:T(8,128)S(1)} %get-tuple-element.15), channel_id=1, source_target_pairs={{0,24},{8,0},{16,8},{24,16},{1,25},{9,1},{17,9},{25,17},{2,26},{10... | collective-permute-start | bytes 761864 | tf_op jit(solution)/shard_map/ppermute | solution.py:317
  6.8 14.1 %copy-start.3 = (f32[16,64,128]{2,1,0:T(8,128)S(1)}, f32[16,64,128]{2,1,0:T(8,128)}, u32[]{:S(2)}) copy-start(f32[16,64,128]{2,1,0:T(8,128)} %cot.5) | copy-start | bytes 1572868
  7.3 13.6 %copy-start.1 = (f32[16,64,128]{2,1,0:T(8,128)S(1)}, f32[16,64,128]{2,1,0:T(8,128)}, u32[]{:S(2)}) copy-start(f32[16,64,128]{2,1,0:T(8,128)} %dens.5) | copy-start | bytes 1572868
  7.3 6.3 %collective-permute-start = (f32[4,64,128]{2,1,0:T(8,128)S(1)}, f32[4,64,128]{2,1,0:T(8,128)S(1)}, u32[]{:S(2)}, u32[]{:S(2)}) collective-permute-start(f32[4,64,128]{2,1,0:T(8,128)S(1)} %get-tuple-element.10), channel_id=1, source_target_pairs={{0,1},{1,2},{2,3},{3,4},{4,5},{5,6},{6,7},{7,0},{8,9},{9,10},{10,1... | collective-permute-start | bytes 393224 | tf_op jit(solution)/shard_map/ppermute | solution.py:317
  7.4 6.3 %collective-permute-start.1 = (f32[4,64,128]{2,1,0:T(8,128)S(1)}, f32[4,64,128]{2,1,0:T(8,128)S(1)}, u32[]{:S(2)}, u32[]{:S(2)}) collective-permute-start(f32[4,64,128]{2,1,0:T(8,128)S(1)} %get-tuple-element.11), channel_id=1, source_target_pairs={{0,7},{1,0},{2,1},{3,2},{4,3},{5,4},{6,5},{7,6},{8,15},{9,8},{10,9... | collective-permute-start | bytes 393224 | tf_op jit(solution)/shard_map/ppermute | solution.py:317
  14.1 5.2 %collective-permute-start.4 = (f32[13,8,128]{2,1,0:T(8,128)S(1)}, f32[13,8,128]{2,1,0:T(8,128)S(1)}, u32[]{:S(2)}, u32[]{:S(2)}) collective-permute-start(f32[13,8,128]{2,1,0:T(8,128)S(1)} %get-tuple-element.16), channel_id=1, source_target_pairs={{0,8},{8,16},{16,24},{24,0},{1,9},{9,17},{17,25},{25,1},{2,10},{10... | collective-permute-start | bytes 159752 | tf_op jit(solution)/shard_map/ppermute | solution.py:317
  15.1 5.8 %collective-permute-start.5 = (f32[13,8,128]{2,1,0:T(8,128)S(1)}, f32[13,8,128]{2,1,0:T(8,128)S(1)}, u32[]{:S(2)}, u32[]{:S(2)}) collective-permute-start(f32[13,8,128]{2,1,0:T(8,128)S(1)} %get-tuple-element.17), channel_id=1, source_target_pairs={{0,24},{8,0},{16,8},{24,16},{1,25},{9,1},{17,9},{25,17},{2,26},{10... | collective-permute-start | bytes 159752 | tf_op jit(solution)/shard_map/ppermute | solution.py:317

commit v3 on v2

--- a/solution.py
+++ b/solution.py
@@ -63,16 +63,24 @@
     return lax.broadcasted_iota(jnp.int32, shape, 1)
 
 
-def pack_rows(plan, dens, cot, first, last):
-    for arr, z, d in plan.fields:
-        src = (dens, cot)[arr]
-        at = plan.row_at[arr, z]
-        first[at : at + d, :] = src[z, :d, :]
-        last[at : at + d, :] = src[z, plan.rows - d :, :]
+def fetch(plan, dens_in, cot_in, dens, cot, first, last, sems):
+    copies = [
+        pltpu.make_async_copy(src, dst, sems.at[i])
+        for i, (src, dst) in enumerate(((dens_in, dens), (cot_in, cot)))
+    ]
+    for copy in copies:
+        copy.start()
     end = plan.row_at[1, 1] + 1
     for ref in (first, last):
         ref[:SUB, :] = jnp.zeros((SUB, plan.cols), jnp.float32)
         ref[end:, :] = jnp.zeros((plan.row_len - end, plan.cols), jnp.float32)
+    for turn, copy in enumerate(copies):
+        copy.wait()
+        for arr, z, d in plan.fields:
+            if arr == turn:
+                src, at = (dens, cot)[arr], plan.row_at[arr, z]
+                first[at : at + d, :] = src[z, :d, :]
+                last[at : at + d, :] = src[z, plan.rows - d :, :]
 
 
 def pack_columns(plan, dens, cot, first, last):
@@ -322,7 +330,16 @@
     plan = Plan(nz, rows, cols)
     part = functools.partial
     block = (nz, rows, cols)
-    first, last = call(part(pack_rows, plan), [(plan.row_len, cols)] * 2, density, cotangent)
+    packed = (plan.row_len, cols)
+    density, cotangent, first, last = pl.pallas_call(
+        part(fetch, plan),
+        out_shape=[pltpu.VMEM(s, jnp.float32) for s in (block, block, packed, packed)],
+        in_specs=[pl.BlockSpec(memory_space=pltpu.HBM)] * 2,
+        out_specs=[VMEM] * 4,
+        scratch_shapes=[pltpu.SemaphoreType.DMA((2,))],
+        cost_estimate=pl.CostEstimate(flops=100000, bytes_accessed=1000000, transcendentals=0),
+        compiler_params=pltpu.CompilerParams(vmem_limit_bytes=4 << 20),
+    )(*[pltpu.with_memory_space_constraint(x, pltpu.HBM) for x in (density, cotangent)])
     above, below = swap("gx", first, last)
     first, last = call(part(pack_columns, plan), [(plan.col_tiles, rows, cols)] * 2, density, cotangent)
     left, right = swap("gy", first, last)

time: 26.3 us -> 25.3 us (0.962)
  local copies, waits for them, and re-layouts: 2.09 us -> 0 us
  Pallas kernels: 6.62 us -> 7.81 us
    unnamed x8 -> x0, local copies, waits for them, and re-layouts: 2.09 us -> none
    pallas_call x0 -> x1, Pallas kernels: none -> 1.23 us  [shards(): pl.pallas_call(part(fetch, plan), out_shape=[pltpu.VMEM(s, jnp.float32) f...]
    pallas_call x4 -> x3, Pallas kernels: 1.44 us -> 1.4 us  [call(): pl.pallas_call(body, out_shape=[pltpu.VMEM(s, jnp.float32) for s in outs]...]
  transfers between devices with their start and end apart: 6 -> 6, of which waited for: 3 -> 3; matrix products, arithmetic and copies ran while one was open for 0% -> 0% of each run, Pallas kernels for 5% -> 6%
where the time goes in v3:
time: 25.3 us; the launch traced here: 25.2 us
  starting transfers between devices  10.6 us (42%)
  Pallas kernels  7.81 us (31%)
  waiting for transfers between devices  6.06 us (24%)
  between operations  0.67 us (3%)
    ppermute x3, starting transfers between devices, swap(): lax.ppermute(first, axis, backward)  6.47 us
    pallas_call x1, Pallas kernels, shards(): pl.pallas_call(part(filter_body, plan), out_shape=[jax.ShapeDtypeStruct(b...  5.18 us
    ppermute x3, waiting for transfers between devices, swap(): lax.ppermute(last, axis, forward)  4.44 us
    ppermute x3, starting transfers between devices, swap(): lax.ppermute(last, axis, forward)  4.13 us
    ppermute x3, waiting for transfers between devices, swap(): lax.ppermute(first, axis, backward)  1.62 us
    pallas_call x3, Pallas kernels, call(): pl.pallas_call(body, out_shape=[pltpu.VMEM(s, jnp.float32) for s in outs]...  1.4 us
    pallas_call x1, Pallas kernels, shards(): pl.pallas_call(part(fetch, plan), out_shape=[pltpu.VMEM(s, jnp.float32) f...  1.23 us
  transfers between devices with their start and end apart: 6, of which 3 were waited for; matrix products, arithmetic and copies ran while one was open for 0% of the time, Pallas kernels for 6%

profile of v3, /device:TPU:0, one launch (start us, length us, event | category | flops | bytes accessed | tf_op | source)
XLA Modules:
  0.0 25.2 jit_solution(2831163047971908256)
XLA Ops:
  0.6 1.2 %shard_map.41 = (f32[16,64,128]{2,1,0:T(8,128)S(1)}, f32[16,64,128]{2,1,0:T(8,128)S(1)}, f32[496,128]{1,0:T(8,128)S(1)}, f32[496,128]{1,0:T(8,128)S(1)}) custom-call(f32[16,64,128]{2,1,0:T(8,128)} %dens_in.1, f32[16,64,128]{2,1,0:T(8,128)} %cot_in.1), custom_call_target="tpu_custom_call" | custom-call | flops 100000 | bytes 1000000 | tf_op jit(solution)/shard_map/pallas_call | solution.py:334
  1.9 3.0 %collective-permute-start.2 = (f32[496,128]{1,0:T(8,128)S(1)}, f32[496,128]{1,0:T(8,128)S(1)}, u32[]{:S(2)}, u32[]{:S(2)}) collective-permute-start(f32[496,128]{1,0:T(8,128)S(1)} %get-tuple-element.18), channel_id=1, source_target_pairs={{0,8},{8,16},{16,24},{24,0},{1,9},{9,17},{17,25},{25,1},{2,10},{10... | collective-permute-start | bytes 761864 | tf_op jit(solution)/shard_map/ppermute | solution.py:325
  4.9 1.0 %collective-permute-start.3 = (f32[496,128]{1,0:T(8,128)S(1)}, f32[496,128]{1,0:T(8,128)S(1)}, u32[]{:S(2)}, u32[]{:S(2)}) collective-permute-start(f32[496,128]{1,0:T(8,128)S(1)} %get-tuple-element.19), channel_id=1, source_target_pairs={{0,24},{8,0},{16,8},{24,16},{1,25},{9,1},{17,9},{25,17},{2,26},{10... | collective-permute-start | bytes 761864 | tf_op jit(solution)/shard_map/ppermute | solution.py:325
  5.9 0.5 %shard_map.42 = (f32[4,64,128]{2,1,0:T(8,128)S(1)}, f32[4,64,128]{2,1,0:T(8,128)S(1)}) custom-call(f32[16,64,128]{2,1,0:T(8,128)S(1)} %get-tuple-element.12.dens, f32[16,64,128]{2,1,0:T(8,128)S(1)} %get-tuple-element.13.cot), custom_call_target="tpu_custom_call" | custom-call | flops 100000 | bytes 100000 | tf_op jit(solution)/shard_map/pallas_call | solution.py:311
  6.4 0.1 collective-permute-start
  6.5 3.5 %collective-permute-start.1 = (f32[4,64,128]{2,1,0:T(8,128)S(1)}, f32[4,64,128]{2,1,0:T(8,128)S(1)}, u32[]{:S(2)}, u32[]{:S(2)}) collective-permute-start(f32[4,64,128]{2,1,0:T(8,128)S(1)} %get-tuple-element.15), channel_id=1, source_target_pairs={{0,7},{1,0},{2,1},{3,2},{4,3},{5,4},{6,5},{7,6},{8,15},{9,8},{10,9... | collective-permute-start | bytes 393224 | tf_op jit(solution)/shard_map/ppermute | solution.py:325
  10.0 2.7 %collective-permute-done.left = f32[4,64,128]{2,1,0:T(8,128)S(1)} collective-permute-done((f32[4,64,128]{2,1,0:T(8,128)S(1)}, f32[4,64,128]{2,1,0:T(8,128)S(1)}, u32[]{:S(2)}, u32[]{:S(2)}) %collective-permute-start) | collective-permute-done | bytes 131104 | tf_op jit(solution)/shard_map/ppermute | solution.py:325
  12.8 0.0 collective-permute-done.1.right
  12.8 0.4 %shard_map.44 = (f32[13,8,128]{2,1,0:T(8,128)S(1)}, f32[13,8,128]{2,1,0:T(8,128)S(1)}) custom-call(f32[4,64,128]{2,1,0:T(8,128)S(1)} %collective-permute-done.left, f32[4,64,128]{2,1,0:T(8,128)S(1)} %collective-permute-done.1.right), custom_call_target="tpu_custom_call" | custom-call | flops 100000 | bytes 100000 | tf_op jit(solution)/shard_map/pallas_call | solution.py:311
  13.1 1.1 %collective-permute-start.4 = (f32[13,8,128]{2,1,0:T(8,128)S(1)}, f32[13,8,128]{2,1,0:T(8,128)S(1)}, u32[]{:S(2)}, u32[]{:S(2)}) collective-permute-start(f32[13,8,128]{2,1,0:T(8,128)S(1)} %get-tuple-element.20), channel_id=1, source_target_pairs={{0,8},{8,16},{16,24},{24,0},{1,9},{9,17},{17,25},{25,1},{2,10},{10... | collective-permute-start | bytes 159752 | tf_op jit(solution)/shard_map/ppermute | solution.py:325
  14.2 1.9 %collective-permute-start.5 = (f32[13,8,128]{2,1,0:T(8,128)S(1)}, f32[13,8,128]{2,1,0:T(8,128)S(1)}, u32[]{:S(2)}, u32[]{:S(2)}) collective-permute-start(f32[13,8,128]{2,1,0:T(8,128)S(1)} %get-tuple-element.21), channel_id=1, source_target_pairs={{0,24},{8,0},{16,8},{24,16},{1,25},{9,1},{17,9},{25,17},{2,26},{10... | collective-permute-start | bytes 159752 | tf_op jit(solution)/shard_map/ppermute | solution.py:325
  16.1 0.5 %shard_map.43 = (f32[16,64,128]{2,1,0:T(8,128)S(1)}, f32[16,64,128]{2,1,0:T(8,128)S(1)}) custom-call(f32[4,64,128]{2,1,0:T(8,128)S(1)} %collective-permute-done.left, f32[4,64,128]{2,1,0:T(8,128)S(1)} %collective-permute-done.1.right), custom_call_target="tpu_custom_call" | custom-call | flops 100000 | bytes 100000 | tf_op jit(solution)/shard_map/pallas_call | solution.py:311
  16.7 1.7 %collective-permute-done.4.cabove = f32[13,8,128]{2,1,0:T(8,128)S(1)} collective-permute-done((f32[13,8,128]{2,1,0:T(8,128)S(1)}, f32[13,8,128]{2,1,0:T(8,128)S(1)}, u32[]{:S(2)}, u32[]{:S(2)}) %collective-permute-start.4) | collective-permute-done | bytes 53280 | tf_op jit(solution)/shard_map/ppermute | solution.py:325
  18.4 1.6 %collective-permute-done.5.cbelow = f32[13,8,128]{2,1,0:T(8,128)S(1)} collective-permute-done((f32[13,8,128]{2,1,0:T(8,128)S(1)}, f32[13,8,128]{2,1,0:T(8,128)S(1)}, u32[]{:S(2)}, u32[]{:S(2)}) %collective-permute-start.5) | collective-permute-done | bytes 53280 | tf_op jit(solution)/shard_map/ppermute | solution.py:325
  20.0 0.0 collective-permute-done.2.above
  20.0 0.0 collective-permute-done.3.below
  20.0 5.2 %shard_map.45 = (f32[16,64,128]{2,1,0:T(8,128)}, f32[16,64,128]{2,1,0:T(8,128)}) custom-call(f32[16,64,128]{2,1,0:T(8,128)S(1)} %get-tuple-element.12.dens, f32[16,64,128]{2,1,0:T(8,128)S(1)} %get-tuple-element.13.cot, f32[16,64,128]{2,1,0:T(8,128)S(1)} %get-tuple-element.16.dens_side, f32[16,64,128]{2,1,0:T(8,128)S(1)} %get-tuple-element.17.cot_side, ...), custom_call_target="tpu_custom_call" | custom-call | flops 10000000 | bytes 1000000 | tf_op jit(solution)/shard_map/pallas_call | solution.py:354
Async XLA Ops:
  1.9 18.1 %collective-permute-start.2 = (f32[496,128]{1,0:T(8,128)S(1)}, f32[496,128]{1,0:T(8,128)S(1)}, u32[]{:S(2)}, u32[]{:S(2)}) collective-permute-start(f32[496,128]{1,0:T(8,128)S(1)} %get-tuple-element.18), channel_id=1, source_target_pairs={{0,8},{8,16},{16,24},{24,0},{1,9},{9,17},{17,25},{25,1},{2,10},{10... | collective-permute-start | bytes 761864 | tf_op jit(solution)/shard_map/ppermute | solution.py:325
  4.9 15.1 %collective-permute-start.3 = (f32[496,128]{1,0:T(8,128)S(1)}, f32[496,128]{1,0:T(8,128)S(1)}, u32[]{:S(2)}, u32[]{:S(2)}) collective-permute-start(f32[496,128]{1,0:T(8,128)S(1)} %get-tuple-element.19), channel_id=1, source_target_pairs={{0,24},{8,0},{16,8},{24,16},{1,25},{9,1},{17,9},{25,17},{2,26},{10... | collective-permute-start | bytes 761864 | tf_op jit(solution)/shard_map/ppermute | solution.py:325
  6.4 6.3 %collective-permute-start = (f32[4,64,128]{2,1,0:T(8,128)S(1)}, f32[4,64,128]{2,1,0:T(8,128)S(1)}, u32[]{:S(2)}, u32[]{:S(2)}) collective-permute-start(f32[4,64,128]{2,1,0:T(8,128)S(1)} %get-tuple-element.14), channel_id=1, source_target_pairs={{0,1},{1,2},{2,3},{3,4},{4,5},{5,6},{6,7},{7,0},{8,9},{9,10},{10,1... | collective-permute-start | bytes 393224 | tf_op jit(solution)/shard_map/ppermute | solution.py:325
  6.5 6.3 %collective-permute-start.1 = (f32[4,64,128]{2,1,0:T(8,128)S(1)}, f32[4,64,128]{2,1,0:T(8,128)S(1)}, u32[]{:S(2)}, u32[]{:S(2)}) collective-permute-start(f32[4,64,128]{2,1,0:T(8,128)S(1)} %get-tuple-element.15), channel_id=1, source_target_pairs={{0,7},{1,0},{2,1},{3,2},{4,3},{5,4},{6,5},{7,6},{8,15},{9,8},{10,9... | collective-permute-start | bytes 393224 | tf_op jit(solution)/shard_map/ppermute | solution.py:325
  13.1 5.2 %collective-permute-start.4 = (f32[13,8,128]{2,1,0:T(8,128)S(1)}, f32[13,8,128]{2,1,0:T(8,128)S(1)}, u32[]{:S(2)}, u32[]{:S(2)}) collective-permute-start(f32[13,8,128]{2,1,0:T(8,128)S(1)} %get-tuple-element.20), channel_id=1, source_target_pairs={{0,8},{8,16},{16,24},{24,0},{1,9},{9,17},{17,25},{25,1},{2,10},{10... | collective-permute-start | bytes 159752 | tf_op jit(solution)/shard_map/ppermute | solution.py:325
  14.2 5.8 %collective-permute-start.5 = (f32[13,8,128]{2,1,0:T(8,128)S(1)}, f32[13,8,128]{2,1,0:T(8,128)S(1)}, u32[]{:S(2)}, u32[]{:S(2)}) collective-permute-start(f32[13,8,128]{2,1,0:T(8,128)S(1)} %get-tuple-element.21), channel_id=1, source_target_pairs={{0,24},{8,0},{16,8},{24,16},{1,25},{9,1},{17,9},{25,17},{2,26},{10... | collective-permute-start | bytes 159752 | tf_op jit(solution)/shard_map/ppermute | solution.py:325

commit v4 on v3

v4 whole, which is shorter than its diff:
```python
import functools
import math

import jax
import jax.numpy as jnp
from jax import lax
from jax.experimental import pallas as pl
from jax.experimental.pallas import tpu as pltpu
from jax.sharding import PartitionSpec as P

power_p = 20.0
root_q = 20.0 + math.log(5.0) / math.log(0.1)
smooth_eps = 0.0001
SUB = 8

VMEM = pl.BlockSpec(memory_space=pltpu.VMEM)


def up8(n):
    return -(-n // SUB) * SUB


class Plan:
    def __init__(self, layers, rows, cols):
        self.nz, self.rows, self.cols = layers, rows, cols
        self.fields = [(0, z, 2 * (layers - 1) - z) for z in range(layers)]
        self.fields += [(1, z, z) for z in range(layers - 1, 0, -1)]
        far = 2 * (layers - 1)
        self.halo = up8(far)
        self.row_at = {}
        at = SUB
        for arr, z, d in self.fields:
            self.row_at[arr, z] = at
            at += d
        self.row_len = up8(at) + SUB
        self.col_at, self.col_tiles = self.fit([((arr, z), d) for arr, z, d in self.fields])
        items = []
        for arr, z, d in self.fields:
            for k in range(-(-(d - 1) // SUB)):
                items.append(((arr, z, k), 2 * (d - 1 - SUB * k)))
        self.corner_at, self.corner_tiles = self.fit(items)

    def fit(self, items):
        room, where = [], {}
        for key, width in sorted(items, key=lambda item: -item[1]):
            for tile, used in enumerate(room):
                if used + width <= self.cols:
                    break
            else:
                tile = len(room)
                room.append(0)
            where[key] = (tile, room[tile])
            room[tile] += width
        return where, len(room)


def shift(x, amount):
    amount %= x.shape[1]
    return x if amount == 0 else pltpu.roll(x, amount, 1)


def lanes_of(shape):
    return lax.broadcasted_iota(jnp.int32, shape, 1)


def fetch(plan, dens_in, cot_in, dens, cot, first, last, sems):
    copies = [
        pltpu.make_async_copy(src, dst, sems.at[i])
        for i, (src, dst) in enumerate(((dens_in, dens), (cot_in, cot)))
    ]
    for copy in copies:
        copy.start()
    end = plan.row_at[1, 1] + 1
    for ref in (first, last):
        ref[:SUB, :] = jnp.zeros((SUB, plan.cols), jnp.float32)
        ref[end:, :] = jnp.zeros((plan.row_len - end, plan.cols), jnp.float32)
    for turn, copy in enumerate(copies):
        copy.wait()
        for arr, z, d in plan.fields:
            if arr == turn:
                src, at = (dens, cot)[arr], plan.row_at[arr, z]
                first[at : at + d, :] = src[z, :d, :]
                last[at : at + d, :] = src[z, plan.rows - d :, :]


def pack_columns(plan, dens, cot, first, last):
    n = plan.cols
    lane = lanes_of((SUB, n))
    for tile in range(plan.col_tiles):
        inside = [f for f in plan.fields if plan.col_at[f[0], f[1]][0] == tile]
        inside.sort(key=lambda f: plan.col_at[f[0], f[1]][1])
        for r in range(0, plan.rows, SUB):
            one, two = None, None
            for arr, z, d in inside:
                at = plan.col_at[arr, z][1]
                x = (dens, cot)[arr][z, r : r + SUB, :]
                a, b = shift(x, at), shift(x, at + d)
                if one is None:
                    one, two = a, b
                else:
                    here = lane >= at
                    one, two = jnp.where(here, a, one), jnp.where(here, b, two)
            first[tile, r : r + SUB, :] = one
            last[tile, r : r + SUB, :] = two


def pack_corners(plan, left, right, first, last):
    lane = lanes_of((SUB, plan.cols))
    out = [[None] * plan.corner_tiles, [None] * plan.corner_tiles]
    order = sorted(plan.corner_at.items(), key=lambda item: item[1][1])
    reach = {(arr, z): d for arr, z, d in plan.fields}
    for (arr, z, k), (tile, at) in order:
        d = reach[arr, z]
        w = d - 1 - SUB * k
        ctile, cat = plan.col_at[arr, z]
        for way in range(2):
            r = SUB * k if way == 0 else plan.rows - SUB * (k + 1)
            a = shift(left[ctile, r : r + SUB, :], at - (cat + d - w))
            b = shift(right[ctile, r : r + SUB, :], at + w - cat)
            both = jnp.where(lane >= at + w, b, a)
            prev = out[way][tile]
            out[way][tile] = both if prev is None else jnp.where(lane >= at, both, prev)
    for tile in range(plan.corner_tiles):
        first[tile] = out[0][tile]
        last[tile] = out[1][tile]


def cross(ref, z, r, lane):
    n = lane.shape[1]
    b = SUB + r
    m, s = ref[z, 0, b : b + SUB, :], ref[z, 1, b : b + SUB, :]
    m1, s1 = pltpu.roll(m, 1, 1), pltpu.roll(s, 1, 1)
    m2, s2 = pltpu.roll(m, n - 1, 1), pltpu.roll(s, n - 1, 1)
    vm = m + ref[z, 0, b - 1 : b + SUB - 1, :] + ref[z, 0, b + 1 : b + SUB + 1, :]
    vs = s + ref[z, 1, b - 1 : b + SUB - 1, :] + ref[z, 1, b + 1 : b + SUB + 1, :]
    start, end = lane == 0, lane == n - 1
    hm = jnp.where(start, s1, m1) + jnp.where(end, s2, m2)
    hs = jnp.where(start, m1, s1) + jnp.where(end, m2, s2)
    return vm + hm, vs + hs


def layer(plan, z, r, half, density, total, power, slope, weight, da, printed):
    top, rows, coef = plan.halo, plan.rows, up8(z)
    if total is None:
        level = jnp.ones_like(density)
    else:
        lg = jnp.log(total)
        level = jnp.exp2(lg * jnp.float32(1.0 / (root_q * math.log(2.0))))
    diff = density - level
    square = diff * diff + smooth_eps
    inv = lax.rsqrt(square)
    value = 0.5 * (density + level - square * inv + math.sqrt(smooth_eps))
    p2 = value * value
    p4 = p2 * p2
    p16 = (p4 * p4) * (p4 * p4)
    if z < plan.nz - 1:
        power[z, half, SUB + r : SUB + r + SUB, :] = p16 * p4
    if top - coef <= r < top + rows + coef:
        u = diff * inv
        if z > 0 or half == 0:
            slope[z, half, r : r + SUB, :] = jnp.float32(0.5 * power_p / root_q) * (p16 * (p2 * value))
        if z > 0:
            ratio = jnp.exp2(lg * jnp.float32((1.0 / root_q - 1.0) / math.log(2.0)))
            weight[z, half, r : r + SUB, :] = (1.0 + u) * ratio
        if half == 0 and top <= r < top + rows:
            printed[z, r - top : r - top + SUB, :] = value
            da[z, r - top : r - top + SUB, :] = 0.5 - 0.5 * u


def inner_body(plan, dens, left, right, dens_side, cot_side, power, slope, weight, da, printed):
    nz, rows, n, top = plan.nz, plan.rows, plan.cols, plan.halo
    lane = lanes_of((SUB, n))
    low = lane < n // 2
    sides = (dens_side, cot_side)
    for arr, z, d in plan.fields:
        tile, at = plan.col_at[arr, z]
        for r in range(0, rows, SUB):
            x = shift(left[tile, r : r + SUB, :], -(at + d))
            y = shift(right[tile, r : r + SUB, :], -at)
            sides[arr][z, r : r + SUB, :] = jnp.where(low, y, x)
    margin = jnp.ones((SUB, n), jnp.float32)
    out = (power, slope, weight, da, printed)
    for z in range(nz):
        if z < nz - 1:
            for half in range(2):
                for r in (0, top, SUB + top + rows, SUB + 2 * top + rows):
                    power[z, half, r : r + SUB, :] = margin
        skip = z // SUB * SUB
        for k in range(skip, rows - skip, SUB):
            total = (None, None) if z == 0 else cross(power, z - 1, top + k, lane)
            for half in range(2):
                density = (dens, dens_side)[half][z, k : k + SUB, :]
                layer(plan, z, top + k, half, density, total[half], *out)


def outer_body(
    plan, dens, cot, dens_side, cot_side, above, below, cabove, cbelow, power_in, slope_in, weight_in, da_in, printed_in,
    power, slope, weight, da, printed, gradient_out, printed_out, gradient, work, sems,
):
    nz, rows, n, top = plan.nz, plan.rows, plan.cols, plan.halo
    lane = lanes_of((SUB, n))
    full = top + rows + top
    reach = {(arr, z): d for arr, z, d in plan.fields}
    out = (power, slope, weight, da, printed)

    margin = jnp.ones((SUB, n), jnp.float32)
    for half in range(2):
        for now in range(2):
            work[now, half, :SUB, :] = margin
            work[now, half, SUB + full :, :] = margin

    def inside(r):
        return top <= r < top + rows

    def field(arr, z, r, half):
        if inside(r):
            blocks = ((dens, dens_side), (cot, cot_side))[arr]
            return blocks[half][z, r - top : r - top + SUB, :]
        d = reach[arr, z]
        before = r < top
        k = (top - r) // SUB - 1 if before else (r - top - rows) // SUB
        if half == 0:
            at = plan.row_at[arr, z]
            if before:
                return above[at + d - SUB * (k + 1) : at + d - SUB * k, :]
            return below[at + SUB * k : at + SUB * (k + 1), :]
        w = d - 1 - SUB * k
        if w <= 0:
            return jnp.ones((SUB, n), jnp.float32)
        tile, cor = plan.corner_at[arr, z, k]
        return shift((cabove if before else cbelow)[tile], -(cor + w))

    def tiles(depth):
        return range(top - up8(depth), top + rows + up8(depth), SUB)

    for z in range(nz):
        edge = up8(z)
        for r in tiles(2 * (nz - 1) - z):
            if top + edge <= r < top + rows - edge:
                continue
            total = (None, None) if z == 0 else cross(power, z - 1, r, lane)
            for half in range(2):
                layer(plan, z, r, half, field(0, z, r, half), total[half], *out)

    copies = [pltpu.make_async_copy(printed, printed_out, sems.at[nz])]
    copies[0].start()

    for z in range(nz - 1, -1, -1):
        for r in tiles(z):
            if z == nz - 1:
                spreads = (None, None)
            else:
                spreads = cross(work, (z + 1) % 2, r, lane)
            for half in range(2 if z > 0 else 1):
                adjoint = field(1, z, r, half) if z > 0 else cot[0, r - top : r - top + SUB, :]
                if spreads[half] is not None:
                    adjoint = adjoint + slope[z, half, r : r + SUB, :] * spreads[half]
                if z > 0:
                    work[z % 2, half, SUB + r : SUB + r + SUB, :] = adjoint * weight[z, half, r : r + SUB, :]
                if half == 0 and inside(r):
                    k = r - top
                    gradient[z, k : k + SUB, :] = adjoint * da[z, k : k + SUB, :]
        copies.append(pltpu.make_async_copy(gradient.at[z], gradient_out.at[z], sems.at[z]))
        copies[-1].start()
    for copy in copies:
        copy.wait()


def swap(axis, first, last):
    count = lax.axis_size(axis)
    forward = [(i, (i + 1) % count) for i in range(count)]
    backward = [(i, (i - 1) % count) for i in range(count)]
    return lax.ppermute(last, axis, forward), lax.ppermute(first, axis, backward)


def near(x):
    return pltpu.with_memory_space_constraint(x, pltpu.VMEM)


def call(body, outs, *args, flops=100000, limit=4):
    return pl.pallas_call(
        body,
        out_shape=[pltpu.VMEM(s, jnp.float32) for s in outs],
        in_specs=[VMEM] * len(args),
        out_specs=[VMEM] * len(outs),
        cost_estimate=pl.CostEstimate(flops=flops, bytes_accessed=flops, transcendentals=0),
        compiler_params=pltpu.CompilerParams(vmem_limit_bytes=limit << 20),
    )(*[near(x) for x in args])


def shards(density, cotangent):
    nz, rows, cols = density.shape
    plan = Plan(nz, rows, cols)
    part = functools.partial
    block = (nz, rows, cols)
    packed = (plan.row_len, cols)
    density, cotangent, first, last = pl.pallas_call(
        part(fetch, plan),
        out_shape=[pltpu.VMEM(s, jnp.float32) for s in (block, block, packed, packed)],
        in_specs=[pl.BlockSpec(memory_space=pltpu.HBM)] * 2,
        out_specs=[VMEM] * 4,
        scratch_shapes=[pltpu.SemaphoreType.DMA((2,))],
        cost_estimate=pl.CostEstimate(flops=100000, bytes_accessed=1000000, transcendentals=0),
        compiler_params=pltpu.CompilerParams(vmem_limit_bytes=4 << 20),
    )(*[pltpu.with_memory_space_constraint(x, pltpu.HBM) for x in (density, cotangent)])
    above, below = swap("gx", first, last)
    first, last = call(part(pack_columns, plan), [(plan.col_tiles, rows, cols)] * 2, density, cotangent)
    left, right = swap("gy", first, last)
    first, last = call(part(pack_corners, plan), [(plan.corner_tiles, SUB, cols)] * 2, left, right)
    cabove, cbelow = swap("gx", first, last)
    full = rows + 2 * plan.halo
    power = (nz - 1, 2, full + 2 * SUB, cols)
    coef = (nz, 2, full, cols)
    kept = [power, coef, coef, block, block]
    dens_side, cot_side, *state = call(part(inner_body, plan), [block] * 2 + kept, density, left, right, limit=8)
    args = (density, cotangent, dens_side, cot_side, above, below, cabove, cbelow, *state)
    *_, gradient, printed = pl.pallas_call(
        part(outer_body, plan),
        out_shape=[pltpu.VMEM(s, jnp.float32) for s in kept] + [jax.ShapeDtypeStruct(block, jnp.float32)] * 2,
        in_specs=[VMEM] * len(args),
        out_specs=[VMEM] * len(kept) + [pl.BlockSpec(memory_space=pltpu.HBM)] * 2,
        scratch_shapes=[
            pltpu.VMEM(block, jnp.float32),
            pltpu.VMEM((2, 2, full + 2 * SUB, cols), jnp.float32),
            pltpu.SemaphoreType.DMA((nz + 1,)),
        ],
        input_output_aliases={len(args) - len(kept) + i: i for i in range(len(kept))},
        cost_estimate=pl.CostEstimate(flops=10000000, bytes_accessed=1000000, transcendentals=0),
        compiler_params=pltpu.CompilerParams(vmem_limit_bytes=8 << 20),
    )(*[near(x) for x in args])
    return printed, gradient


def solution(mesh):
    placed = P(None, "gx", "gy")
    return jax.shard_map(
        shards,
        mesh=mesh,
        in_specs=(placed, placed),
        out_specs=(placed, placed),
        check_vma=False,
    )
```

time: 25.3 us -> 24 us (0.949)
  waiting for transfers between devices: 6.06 us -> 4.65 us
    pallas_call x3, Pallas kernels: 1.4 us -> 2.82 us  [call(): pl.pallas_call(body, out_shape=[pltpu.VMEM(s, jnp.float32) for s in outs]...]
    ppermute x3, waiting for transfers between devices: 4.44 us -> 3.03 us  [swap(): lax.ppermute(last, axis, forward)]
    pallas_call x1, Pallas kernels: 5.18 us -> 3.91 us  [shards(): pl.pallas_call(part(outer_body, plan), out_shape=[pltpu.VMEM(s, jnp.float...]
  transfers between devices with their start and end apart: 6 -> 6, of which waited for: 3 -> 3; matrix products, arithmetic and copies ran while one was open for 0% -> 0% of each run, Pallas kernels for 6% -> 12%
where the time goes in v4:
time: 24 us; the launch traced here: 23.9 us
  starting transfers between devices  10.6 us (44%)
  Pallas kernels  7.96 us (33%)
  waiting for transfers between devices  4.65 us (19%)
  between operations  0.67 us (3%)
    ppermute x3, starting transfers between devices, swap(): lax.ppermute(first, axis, backward)  6.47 us
    ppermute x3, starting transfers between devices, swap(): lax.ppermute(last, axis, forward)  4.13 us
    pallas_call x1, Pallas kernels, shards(): pl.pallas_call(part(outer_body, plan), out_shape=[pltpu.VMEM(s, jnp.float...  3.91 us
    ppermute x3, waiting for transfers between devices, swap(): lax.ppermute(last, axis, forward)  3.03 us
    pallas_call x3, Pallas kernels, call(): pl.pallas_call(body, out_shape=[pltpu.VMEM(s, jnp.float32) for s in outs]...  2.82 us
    ppermute x3, waiting for transfers between devices, swap(): lax.ppermute(first, axis, backward)  1.62 us
    pallas_call x1, Pallas kernels, shards(): pl.pallas_call(part(fetch, plan), out_shape=[pltpu.VMEM(s, jnp.float32) f...  1.23 us
  transfers between devices with their start and end apart: 6, of which 3 were waited for; matrix products, arithmetic and copies ran while one was open for 0% of the time, Pallas kernels for 12%

profile of v4, /device:TPU:0, one launch (start us, length us, event | category | flops | bytes accessed | tf_op | source)
XLA Modules:
  0.0 23.9 jit_solution(11490217040606611220)
XLA Ops:
  0.6 1.2 %shard_map.41 = (f32[16,64,128]{2,1,0:T(8,128)S(1)}, f32[16,64,128]{2,1,0:T(8,128)S(1)}, f32[496,128]{1,0:T(8,128)S(1)}, f32[496,128]{1,0:T(8,128)S(1)}) custom-call(f32[16,64,128]{2,1,0:T(8,128)} %dens_in.1, f32[16,64,128]{2,1,0:T(8,128)} %cot_in.1), custom_call_target="tpu_custom_call" | custom-call | flops 100000 | bytes 1000000 | tf_op jit(solution)/shard_map/pallas_call | solution.py:297
  1.9 3.0 %collective-permute-start.2 = (f32[496,128]{1,0:T(8,128)S(1)}, f32[496,128]{1,0:T(8,128)S(1)}, u32[]{:S(2)}, u32[]{:S(2)}) collective-permute-start(f32[496,128]{1,0:T(8,128)S(1)} %get-tuple-element.25), channel_id=1, source_target_pairs={{0,8},{8,16},{16,24},{24,0},{1,9},{9,17},{17,25},{25,1},{2,10},{10... | collective-permute-start | bytes 761864 | tf_op jit(solution)/shard_map/ppermute | solution.py:273
  4.9 1.0 %collective-permute-start.3 = (f32[496,128]{1,0:T(8,128)S(1)}, f32[496,128]{1,0:T(8,128)S(1)}, u32[]{:S(2)}, u32[]{:S(2)}) collective-permute-start(f32[496,128]{1,0:T(8,128)S(1)} %get-tuple-element.26), channel_id=1, source_target_pairs={{0,24},{8,0},{16,8},{24,16},{1,25},{9,1},{17,9},{25,17},{2,26},{10... | collective-permute-start | bytes 761864 | tf_op jit(solution)/shard_map/ppermute | solution.py:273
  5.9 0.5 %shard_map.42 = (f32[4,64,128]{2,1,0:T(8,128)S(1)}, f32[4,64,128]{2,1,0:T(8,128)S(1)}) custom-call(f32[16,64,128]{2,1,0:T(8,128)S(1)} %get-tuple-element.19.dens, f32[16,64,128]{2,1,0:T(8,128)S(1)} %get-tuple-element.20.cot), custom_call_target="tpu_custom_call" | custom-call | flops 100000 | bytes 100000 | tf_op jit(solution)/shard_map/pallas_call | solution.py:281
  6.4 0.1 collective-permute-start
  6.5 3.5 %collective-permute-start.1 = (f32[4,64,128]{2,1,0:T(8,128)S(1)}, f32[4,64,128]{2,1,0:T(8,128)S(1)}, u32[]{:S(2)}, u32[]{:S(2)}) collective-permute-start(f32[4,64,128]{2,1,0:T(8,128)S(1)} %get-tuple-element.22), channel_id=1, source_target_pairs={{0,7},{1,0},{2,1},{3,2},{4,3},{5,4},{6,5},{7,6},{8,15},{9,8},{10,9... | collective-permute-start | bytes 393224 | tf_op jit(solution)/shard_map/ppermute | solution.py:273
  10.0 2.7 %collective-permute-done.left = f32[4,64,128]{2,1,0:T(8,128)S(1)} collective-permute-done((f32[4,64,128]{2,1,0:T(8,128)S(1)}, f32[4,64,128]{2,1,0:T(8,128)S(1)}, u32[]{:S(2)}, u32[]{:S(2)}) %collective-permute-start) | collective-permute-done | bytes 131104 | tf_op jit(solution)/shard_map/ppermute | solution.py:273
  12.8 0.0 collective-permute-done.1.right
  12.8 0.4 %shard_map.44 = (f32[13,8,128]{2,1,0:T(8,128)S(1)}, f32[13,8,128]{2,1,0:T(8,128)S(1)}) custom-call(f32[4,64,128]{2,1,0:T(8,128)S(1)} %collective-permute-done.left, f32[4,64,128]{2,1,0:T(8,128)S(1)} %collective-permute-done.1.right), custom_call_target="tpu_custom_call" | custom-call | flops 100000 | bytes 100000 | tf_op jit(solution)/shard_map/pallas_call | solution.py:281
  13.1 1.1 %collective-permute-start.4 = (f32[13,8,128]{2,1,0:T(8,128)S(1)}, f32[13,8,128]{2,1,0:T(8,128)S(1)}, u32[]{:S(2)}, u32[]{:S(2)}) collective-permute-start(f32[13,8,128]{2,1,0:T(8,128)S(1)} %get-tuple-element.27), channel_id=1, source_target_pairs={{0,8},{8,16},{16,24},{24,0},{1,9},{9,17},{17,25},{25,1},{2,10},{10... | collective-permute-start | bytes 159752 | tf_op jit(solution)/shard_map/ppermute | solution.py:273
  14.2 1.9 %collective-permute-start.5 = (f32[13,8,128]{2,1,0:T(8,128)S(1)}, f32[13,8,128]{2,1,0:T(8,128)S(1)}, u32[]{:S(2)}, u32[]{:S(2)}) collective-permute-start(f32[13,8,128]{2,1,0:T(8,128)S(1)} %get-tuple-element.28), channel_id=1, source_target_pairs={{0,24},{8,0},{16,8},{24,16},{1,25},{9,1},{17,9},{25,17},{2,26},{10... | collective-permute-start | bytes 159752 | tf_op jit(solution)/shard_map/ppermute | solution.py:273
  16.1 1.9 %shard_map.43 = (f32[16,64,128]{2,1,0:T(8,128)S(1)}, f32[16,64,128]{2,1,0:T(8,128)S(1)}, f32[15,2,144,128]{3,2,1,0:T(8,128)S(1)}, f32[16,2,128,128]{3,2,1,0:T(8,...) custom-call(f32[16,64,128]{2,1,0:T(8,128)S(1)} %get-tuple-element.19.dens, ...), custom_call_target="tpu_custom_call" | custom-call | flops 100000 | bytes 100000 | tf_op jit(solution)/shard_map/pallas_call | solution.py:281
  18.1 0.3 %collective-permute-done.4.cabove = f32[13,8,128]{2,1,0:T(8,128)S(1)} collective-permute-done((f32[13,8,128]{2,1,0:T(8,128)S(1)}, f32[13,8,128]{2,1,0:T(8,128)S(1)}, u32[]{:S(2)}, u32[]{:S(2)}) %collective-permute-start.4) | collective-permute-done | bytes 53280 | tf_op jit(solution)/shard_map/ppermute | solution.py:273
  18.4 1.6 %collective-permute-done.5.cbelow = f32[13,8,128]{2,1,0:T(8,128)S(1)} collective-permute-done((f32[13,8,128]{2,1,0:T(8,128)S(1)}, f32[13,8,128]{2,1,0:T(8,128)S(1)}, u32[]{:S(2)}, u32[]{:S(2)}) %collective-permute-start.5) | collective-permute-done | bytes 53280 | tf_op jit(solution)/shard_map/ppermute | solution.py:273
  20.0 0.0 collective-permute-done.2.above
  20.0 0.0 collective-permute-done.3.below
  20.0 3.9 %shard_map.45 = (f32[15,2,144,128]{3,2,1,0:T(8,128)S(1)}, f32[16,2,128,128]{3,2,1,0:T(8,128)S(1)}, f32[16,2,128,128]{3,2,1,0:T(8,128)S(1)}, f32[16,64,128]{2,1,0...) custom-call(f32[16,64,128]{2,1,0:T(8,128)S(1)} %get-tuple-element.19, ...), custom_call_target="tpu_custom_call", output_to_operand_aliasing={{0}: (8, {}), {1}: (9, {}), {2}: (10, {}), {3}: (11, {}), {... | custom-call | flops 10000000 | bytes 1000000 | tf_op jit(solution)/shard_map/pallas_call | solution.py:317
Async XLA Ops:
  1.9 18.1 %collective-permute-start.2 = (f32[496,128]{1,0:T(8,128)S(1)}, f32[496,128]{1,0:T(8,128)S(1)}, u32[]{:S(2)}, u32[]{:S(2)}) collective-permute-start(f32[496,128]{1,0:T(8,128)S(1)} %get-tuple-element.25), channel_id=1, source_target_pairs={{0,8},{8,16},{16,24},{24,0},{1,9},{9,17},{17,25},{25,1},{2,10},{10... | collective-permute-start | bytes 761864 | tf_op jit(solution)/shard_map/ppermute | solution.py:273
  4.9 15.1 %collective-permute-start.3 = (f32[496,128]{1,0:T(8,128)S(1)}, f32[496,128]{1,0:T(8,128)S(1)}, u32[]{:S(2)}, u32[]{:S(2)}) collective-permute-start(f32[496,128]{1,0:T(8,128)S(1)} %get-tuple-element.26), channel_id=1, source_target_pairs={{0,24},{8,0},{16,8},{24,16},{1,25},{9,1},{17,9},{25,17},{2,26},{10... | collective-permute-start | bytes 761864 | tf_op jit(solution)/shard_map/ppermute | solution.py:273
  6.4 6.3 %collective-permute-start = (f32[4,64,128]{2,1,0:T(8,128)S(1)}, f32[4,64,128]{2,1,0:T(8,128)S(1)}, u32[]{:S(2)}, u32[]{:S(2)}) collective-permute-start(f32[4,64,128]{2,1,0:T(8,128)S(1)} %get-tuple-element.21), channel_id=1, source_target_pairs={{0,1},{1,2},{2,3},{3,4},{4,5},{5,6},{6,7},{7,0},{8,9},{9,10},{10,1... | collective-permute-start | bytes 393224 | tf_op jit(solution)/shard_map/ppermute | solution.py:273
  6.5 6.3 %collective-permute-start.1 = (f32[4,64,128]{2,1,0:T(8,128)S(1)}, f32[4,64,128]{2,1,0:T(8,128)S(1)}, u32[]{:S(2)}, u32[]{:S(2)}) collective-permute-start(f32[4,64,128]{2,1,0:T(8,128)S(1)} %get-tuple-element.22), channel_id=1, source_target_pairs={{0,7},{1,0},{2,1},{3,2},{4,3},{5,4},{6,5},{7,6},{8,15},{9,8},{10,9... | collective-permute-start | bytes 393224 | tf_op jit(solution)/shard_map/ppermute | solution.py:273
  13.1 5.2 %collective-permute-start.4 = (f32[13,8,128]{2,1,0:T(8,128)S(1)}, f32[13,8,128]{2,1,0:T(8,128)S(1)}, u32[]{:S(2)}, u32[]{:S(2)}) collective-permute-start(f32[13,8,128]{2,1,0:T(8,128)S(1)} %get-tuple-element.27), channel_id=1, source_target_pairs={{0,8},{8,16},{16,24},{24,0},{1,9},{9,17},{17,25},{25,1},{2,10},{10... | collective-permute-start | bytes 159752 | tf_op jit(solution)/shard_map/ppermute | solution.py:273
  14.2 5.8 %collective-permute-start.5 = (f32[13,8,128]{2,1,0:T(8,128)S(1)}, f32[13,8,128]{2,1,0:T(8,128)S(1)}, u32[]{:S(2)}, u32[]{:S(2)}) collective-permute-start(f32[13,8,128]{2,1,0:T(8,128)S(1)} %get-tuple-element.28), channel_id=1, source_target_pairs={{0,24},{8,0},{16,8},{24,16},{1,25},{9,1},{17,9},{25,17},{2,26},{10... | collective-permute-start | bytes 159752 | tf_op jit(solution)/shard_map/ppermute | solution.py:273

commit v5 on v4

--- a/solution.py
+++ b/solution.py
@@ -7,6 +7,7 @@
 from jax.experimental import pallas as pl
 from jax.experimental.pallas import tpu as pltpu
 from jax.sharding import PartitionSpec as P
+
 
 power_p = 20.0
 root_q = 20.0 + math.log(5.0) / math.log(0.1)
@@ -27,12 +28,18 @@
         self.fields += [(1, z, z) for z in range(layers - 1, 0, -1)]
         far = 2 * (layers - 1)
         self.halo = up8(far)
+        line = sorted(self.fields, key=lambda f: f[2] % SUB != 0)
+        even = sum(d % SUB == 0 for _, _, d in line)
+        line = line[1:] + line[:1]
+        line = line[even - 2 : even - 1] + line[: even - 2] + line[even - 1 :] if even >= 2 else line
+        self.margin = 0 if even >= 2 else SUB
         self.row_at = {}
-        at = SUB
-        for arr, z, d in self.fields:
+        at = self.margin
+        for arr, z, d in line:
             self.row_at[arr, z] = at
             at += d
-        self.row_len = up8(at) + SUB
+        self.row_end = at
+        self.row_len = up8(at) + self.margin
         self.col_at, self.col_tiles = self.fit([((arr, z), d) for arr, z, d in self.fields])
         items = []
         for arr, z, d in self.fields:
@@ -63,28 +70,36 @@
     return lax.broadcasted_iota(jnp.int32, shape, 1)
 
 
-def fetch(plan, dens_in, cot_in, dens, cot, first, last, sems):
+def odd_on(axis):
+    return lax.rem(lax.axis_index(axis), 2) == 1
+
+
+def fetch(plan, dens_in, cot_in, dens, cot, ours, theirs, sems):
     copies = [
         pltpu.make_async_copy(src, dst, sems.at[i])
         for i, (src, dst) in enumerate(((dens_in, dens), (cot_in, cot)))
     ]
     for copy in copies:
         copy.start()
-    end = plan.row_at[1, 1] + 1
-    for ref in (first, last):
-        ref[:SUB, :] = jnp.zeros((SUB, plan.cols), jnp.float32)
-        ref[end:, :] = jnp.zeros((plan.row_len - end, plan.cols), jnp.float32)
+    odd = odd_on("gx")
+    for ref in (ours, theirs):
+        if plan.margin > 0:
+            ref[: plan.margin, :] = jnp.zeros((plan.margin, plan.cols), jnp.float32)
+        if plan.row_len > plan.row_end:
+            ref[plan.row_end :, :] = jnp.zeros((plan.row_len - plan.row_end, plan.cols), jnp.float32)
     for turn, copy in enumerate(copies):
         copy.wait()
         for arr, z, d in plan.fields:
             if arr == turn:
                 src, at = (dens, cot)[arr], plan.row_at[arr, z]
-                first[at : at + d, :] = src[z, :d, :]
-                last[at : at + d, :] = src[z, plan.rows - d :, :]
-
-
-def pack_columns(plan, dens, cot, first, last):
+                one, two = src[z, :d, :], src[z, plan.rows - d :, :]
+                ours[at : at + d, :] = jnp.where(odd, one, two)
+                theirs[at : at + d, :] = jnp.where(odd, two, one)
+
+
+def pack_columns(plan, dens, cot, ours, theirs):
     n = plan.cols
+    odd = odd_on("gy")
     lane = lanes_of((SUB, n))
     for tile in range(plan.col_tiles):
         inside = [f for f in plan.fields if plan.col_at[f[0], f[1]][0] == tile]
@@ -100,12 +115,13 @@
                 else:
                     here = lane >= at
                     one, two = jnp.where(here, a, one), jnp.where(here, b, two)
-            first[tile, r : r + SUB, :] = one
-            last[tile, r : r + SUB, :] = two
-
-
-def pack_corners(plan, left, right, first, last):
+            ours[tile, r : r + SUB, :] = jnp.where(odd, one, two)
+            theirs[tile, r : r + SUB, :] = jnp.where(odd, two, one)
+
+
+def pack_corners(plan, mine, other, ours, theirs):
     lane = lanes_of((SUB, plan.cols))
+    odd_x, odd_y = odd_on("gx"), odd_on("gy")
     out = [[None] * plan.corner_tiles, [None] * plan.corner_tiles]
     order = sorted(plan.corner_at.items(), key=lambda item: item[1][1])
     reach = {(arr, z): d for arr, z, d in plan.fields}
@@ -115,14 +131,15 @@
         ctile, cat = plan.col_at[arr, z]
         for way in range(2):
             r = SUB * k if way == 0 else plan.rows - SUB * (k + 1)
-            a = shift(left[ctile, r : r + SUB, :], at - (cat + d - w))
-            b = shift(right[ctile, r : r + SUB, :], at + w - cat)
+            x, y = mine[ctile, r : r + SUB, :], other[ctile, r : r + SUB, :]
+            a = shift(jnp.where(odd_y, x, y), at - (cat + d - w))
+            b = shift(jnp.where(odd_y, y, x), at + w - cat)
             both = jnp.where(lane >= at + w, b, a)
             prev = out[way][tile]
             out[way][tile] = both if prev is None else jnp.where(lane >= at, both, prev)
     for tile in range(plan.corner_tiles):
-        first[tile] = out[0][tile]
-        last[tile] = out[1][tile]
+        ours[tile] = jnp.where(odd_x, out[0][tile], out[1][tile])
+        theirs[tile] = jnp.where(odd_x, out[1][tile], out[0][tile])
 
 
 def cross(ref, z, r, lane):
@@ -167,16 +184,17 @@
             da[z, r - top : r - top + SUB, :] = 0.5 - 0.5 * u
 
 
-def inner_body(plan, dens, left, right, dens_side, cot_side, power, slope, weight, da, printed):
+def inner_body(plan, dens, mine, other, dens_side, cot_side, power, slope, weight, da, printed):
     nz, rows, n, top = plan.nz, plan.rows, plan.cols, plan.halo
     lane = lanes_of((SUB, n))
     low = lane < n // 2
     sides = (dens_side, cot_side)
+    odd = odd_on("gy")
     for arr, z, d in plan.fields:
         tile, at = plan.col_at[arr, z]
         for r in range(0, rows, SUB):
-            x = shift(left[tile, r : r + SUB, :], -(at + d))
-            y = shift(right[tile, r : r + SUB, :], -at)
+            x, y = mine[tile, r : r + SUB, :], other[tile, r : r + SUB, :]
+            x, y = shift(jnp.where(odd, x, y), -(at + d)), shift(jnp.where(odd, y, x), -at)
             sides[arr][z, r : r + SUB, :] = jnp.where(low, y, x)
     margin = jnp.ones((SUB, n), jnp.float32)
     out = (power, slope, weight, da, printed)
@@ -194,13 +212,14 @@
 
 
 def outer_body(
-    plan, dens, cot, dens_side, cot_side, above, below, cabove, cbelow, power_in, slope_in, weight_in, da_in, printed_in,
+    plan, dens, cot, dens_side, cot_side, mine, other, cmine, cother, power_in, slope_in, weight_in, da_in, printed_in,
     power, slope, weight, da, printed, gradient_out, printed_out, gradient, work, sems,
 ):
     nz, rows, n, top = plan.nz, plan.rows, plan.cols, plan.halo
     lane = lanes_of((SUB, n))
     full = top + rows + top
     reach = {(arr, z): d for arr, z, d in plan.fields}
+    odd = odd_on("gx")
     out = (power, slope, weight, da, printed)
 
     margin = jnp.ones((SUB, n), jnp.float32)
@@ -221,14 +240,15 @@
         k = (top - r) // SUB - 1 if before else (r - top - rows) // SUB
         if half == 0:
             at = plan.row_at[arr, z]
-            if before:
-                return above[at + d - SUB * (k + 1) : at + d - SUB * k, :]
-            return below[at + SUB * k : at + SUB * (k + 1), :]
+            at = at + d - SUB * (k + 1) if before else at + SUB * k
+            x, y = mine[at : at + SUB, :], other[at : at + SUB, :]
+            return jnp.where(odd, x, y) if before else jnp.where(odd, y, x)
         w = d - 1 - SUB * k
         if w <= 0:
             return jnp.ones((SUB, n), jnp.float32)
         tile, cor = plan.corner_at[arr, z, k]
-        return shift((cabove if before else cbelow)[tile], -(cor + w))
+        x, y = cmine[tile], cother[tile]
+        return shift(jnp.where(odd, x, y) if before else jnp.where(odd, y, x), -(cor + w))
 
     def tiles(depth):
         return range(top - up8(depth), top + rows + up8(depth), SUB)
@@ -266,11 +286,14 @@
         copy.wait()
 
 
-def swap(axis, first, last):
+def swap(axis, ours, theirs):
     count = lax.axis_size(axis)
-    forward = [(i, (i + 1) % count) for i in range(count)]
-    backward = [(i, (i - 1) % count) for i in range(count)]
-    return lax.ppermute(last, axis, forward), lax.ppermute(first, axis, backward)
+    assert count % 2 == 0
+    results = []
+    for turn, x in enumerate((ours, theirs)):
+        ends = [((i + turn) % count, (i + turn + 1) % count) for i in range(0, count, 2)]
+        results.append(lax.ppermute(x, axis, [p for a, b in ends for p in ((a, b), (b, a))]))
+    return results
 
 
 def near(x):
@@ -294,7 +317,7 @@
     part = functools.partial
     block = (nz, rows, cols)
     packed = (plan.row_len, cols)
-    density, cotangent, first, last = pl.pallas_call(
+    density, cotangent, ours, theirs = pl.pallas_call(
         part(fetch, plan),
         out_shape=[pltpu.VMEM(s, jnp.float32) for s in (block, block, packed, packed)],
         in_specs=[pl.BlockSpec(memory_space=pltpu.HBM)] * 2,
@@ -303,17 +326,17 @@
         cost_estimate=pl.CostEstimate(flops=100000, bytes_accessed=1000000, transcendentals=0),
         compiler_params=pltpu.CompilerParams(vmem_limit_bytes=4 << 20),
     )(*[pltpu.with_memory_space_constraint(x, pltpu.HBM) for x in (density, cotangent)])
-    above, below = swap("gx", first, last)
-    first, last = call(part(pack_columns, plan), [(plan.col_tiles, rows, cols)] * 2, density, cotangent)
-    left, right = swap("gy", first, last)
-    first, last = call(part(pack_corners, plan), [(plan.corner_tiles, SUB, cols)] * 2, left, right)
-    cabove, cbelow = swap("gx", first, last)
+    near_rows = swap("gx", ours, theirs)
+    ours, theirs = call(part(pack_columns, plan), [(plan.col_tiles, rows, cols)] * 2, density, cotangent)
+    sides = swap("gy", ours, theirs)
+    ours, theirs = call(part(pack_corners, plan), [(plan.corner_tiles, SUB, cols)] * 2, *sides)
+    corners = swap("gx", ours, theirs)
     full = rows + 2 * plan.halo
     power = (nz - 1, 2, full + 2 * SUB, cols)
     coef = (nz, 2, full, cols)
     kept = [power, coef, coef, block, block]
-    dens_side, cot_side, *state = call(part(inner_body, plan), [block] * 2 + kept, density, left, right, limit=8)
-    args = (density, cotangent, dens_side, cot_side, above, below, cabove, cbelow, *state)
+    dens_side, cot_side, *state = call(part(inner_body, plan), [block] * 2 + kept, density, *sides, limit=8)
+    args = (density, cotangent, dens_side, cot_side, *near_rows, *corners, *state)
     *_, gradient, printed = pl.pallas_call(
         part(outer_body, plan),
         out_shape=[pltpu.VMEM(s, jnp.float32) for s in kept] + [jax.ShapeDtypeStruct(block, jnp.float32)] * 2,

time: 24 us -> 25.1 us (1.046)
  waiting for transfers between devices: 4.65 us -> 5.91 us
  starting transfers between devices: 10.6 us -> 10.3 us
    ppermute x6, waiting for transfers between devices: 4.65 us -> 5.91 us  [swap(): lax.ppermute(x, axis, [p for a, b in ends for p in ((a, b), (b, a))])]
    ppermute x6, starting transfers between devices: 10.6 us -> 10.3 us  [swap(): lax.ppermute(x, axis, [p for a, b in ends for p in ((a, b), (b, a))])]
  transfers between devices with their start and end apart: 6 -> 6, of which waited for: 3 -> 3; matrix products, arithmetic and copies ran while one was open for 0% -> 0% of each run, Pallas kernels for 12% -> 11%
where the time goes in v5:
time: 25.1 us; the launch traced here: 24.9 us
  starting transfers between devices  10.3 us (41%)
  Pallas kernels  8.01 us (32%)
  waiting for transfers between devices  5.91 us (24%)
  between operations  0.67 us (3%)
    ppermute x6, starting transfers between devices, swap(): lax.ppermute(x, axis, [p for a, b in ends for p in ((a, b), (b, a))])  10.3 us
    ppermute x6, waiting for transfers between devices, swap(): lax.ppermute(x, axis, [p for a, b in ends for p in ((a, b), (b, a))])  5.91 us
    pallas_call x1, Pallas kernels, shards(): pl.pallas_call(part(outer_body, plan), out_shape=[pltpu.VMEM(s, jnp.float...  3.94 us
    pallas_call x3, Pallas kernels, call(): pl.pallas_call(body, out_shape=[pltpu.VMEM(s, jnp.float32) for s in outs]...  2.84 us
    pallas_call x1, Pallas kernels, shards(): pl.pallas_call(part(fetch, plan), out_shape=[pltpu.VMEM(s, jnp.float32) f...  1.23 us
  transfers between devices with their start and end apart: 6, of which 3 were waited for; matrix products, arithmetic and copies ran while one was open for 0% of the time, Pallas kernels for 11%

profile of v5, /device:TPU:0, one launch (start us, length us, event | category | flops | bytes accessed | tf_op | source)
XLA Modules:
  0.0 24.9 jit_solution(14671144191170681235)
XLA Ops:
  0.6 1.2 %shard_map.41 = (f32[16,64,128]{2,1,0:T(8,128)S(1)}, f32[16,64,128]{2,1,0:T(8,128)S(1)}, f32[480,128]{1,0:T(8,128)S(1)}, f32[480,128]{1,0:T(8,128)S(1)}) custom-call(f32[16,64,128]{2,1,0:T(8,128)} %dens_in.1, f32[16,64,128]{2,1,0:T(8,128)} %cot_in.1), custom_call_target="tpu_custom_call" | custom-call | flops 100000 | bytes 1000000 | tf_op jit(solution)/shard_map/pallas_call | solution.py:320
  1.9 3.0 %collective-permute-start.2 = (f32[480,128]{1,0:T(8,128)S(1)}, f32[480,128]{1,0:T(8,128)S(1)}, u32[]{:S(2)}, u32[]{:S(2)}) collective-permute-start(f32[480,128]{1,0:T(8,128)S(1)} %get-tuple-element.25), channel_id=1, source_target_pairs={{0,8},{8,0},{16,24},{24,16},{1,9},{9,1},{17,25},{25,17},{2,10},{10... | collective-permute-start | bytes 737288 | tf_op jit(solution)/shard_map/ppermute | solution.py:295
  4.9 1.5 %collective-permute-start.3 = (f32[480,128]{1,0:T(8,128)S(1)}, f32[480,128]{1,0:T(8,128)S(1)}, u32[]{:S(2)}, u32[]{:S(2)}) collective-permute-start(f32[480,128]{1,0:T(8,128)S(1)} %get-tuple-element.26), channel_id=1, source_target_pairs={{8,16},{16,8},{24,0},{0,24},{9,17},{17,9},{25,1},{1,25},{10,18},{1... | collective-permute-start | bytes 737288 | tf_op jit(solution)/shard_map/ppermute | solution.py:295
  6.4 0.5 %shard_map.42 = (f32[4,64,128]{2,1,0:T(8,128)S(1)}, f32[4,64,128]{2,1,0:T(8,128)S(1)}) custom-call(f32[16,64,128]{2,1,0:T(8,128)S(1)} %get-tuple-element.19.dens, f32[16,64,128]{2,1,0:T(8,128)S(1)} %get-tuple-element.20.cot), custom_call_target="tpu_custom_call" | custom-call | flops 100000 | bytes 100000 | tf_op jit(solution)/shard_map/pallas_call | solution.py:304
  6.9 0.1 collective-permute-start
  7.0 3.7 %collective-permute-start.1 = (f32[4,64,128]{2,1,0:T(8,128)S(1)}, f32[4,64,128]{2,1,0:T(8,128)S(1)}, u32[]{:S(2)}, u32[]{:S(2)}) collective-permute-start(f32[4,64,128]{2,1,0:T(8,128)S(1)} %get-tuple-element.22), channel_id=1, source_target_pairs={{1,2},{2,1},{3,4},{4,3},{5,6},{6,5},{7,0},{0,7},{9,10},{10,9},{11,... | collective-permute-start | bytes 393224 | tf_op jit(solution)/shard_map/ppermute | solution.py:295
  10.7 0.0 collective-permute-done.mine
  10.7 3.3 %collective-permute-done.1.other = f32[4,64,128]{2,1,0:T(8,128)S(1)} collective-permute-done((f32[4,64,128]{2,1,0:T(8,128)S(1)}, f32[4,64,128]{2,1,0:T(8,128)S(1)}, u32[]{:S(2)}, u32[]{:S(2)}) %collective-permute-start.1) | collective-permute-done | bytes 131104 | tf_op jit(solution)/shard_map/ppermute | solution.py:295
  14.0 0.4 %shard_map.44 = (f32[13,8,128]{2,1,0:T(8,128)S(1)}, f32[13,8,128]{2,1,0:T(8,128)S(1)}) custom-call(f32[4,64,128]{2,1,0:T(8,128)S(1)} %collective-permute-done.mine, f32[4,64,128]{2,1,0:T(8,128)S(1)} %collective-permute-done.1.other), custom_call_target="tpu_custom_call" | custom-call | flops 100000 | bytes 100000 | tf_op jit(solution)/shard_map/pallas_call | solution.py:304
  14.4 1.6 %collective-permute-start.4 = (f32[13,8,128]{2,1,0:T(8,128)S(1)}, f32[13,8,128]{2,1,0:T(8,128)S(1)}, u32[]{:S(2)}, u32[]{:S(2)}) collective-permute-start(f32[13,8,128]{2,1,0:T(8,128)S(1)} %get-tuple-element.27), channel_id=1, source_target_pairs={{0,8},{8,0},{16,24},{24,16},{1,9},{9,1},{17,25},{25,17},{2,10},{10... | collective-permute-start | bytes 159752 | tf_op jit(solution)/shard_map/ppermute | solution.py:295
  15.9 0.5 %collective-permute-start.5 = (f32[13,8,128]{2,1,0:T(8,128)S(1)}, f32[13,8,128]{2,1,0:T(8,128)S(1)}, u32[]{:S(2)}, u32[]{:S(2)}) collective-permute-start(f32[13,8,128]{2,1,0:T(8,128)S(1)} %get-tuple-element.28), channel_id=1, source_target_pairs={{8,16},{16,8},{24,0},{0,24},{9,17},{17,9},{25,1},{1,25},{10,18},{1... | collective-permute-start | bytes 159752 | tf_op jit(solution)/shard_map/ppermute | solution.py:295
  16.4 2.0 %shard_map.43 = (f32[16,64,128]{2,1,0:T(8,128)S(1)}, f32[16,64,128]{2,1,0:T(8,128)S(1)}, f32[15,2,144,128]{3,2,1,0:T(8,128)S(1)}, f32[16,2,128,128]{3,2,1,0:T(8,...) custom-call(f32[16,64,128]{2,1,0:T(8,128)S(1)} %get-tuple-element.19.dens, ...), custom_call_target="tpu_custom_call" | custom-call | flops 100000 | bytes 100000 | tf_op jit(solution)/shard_map/pallas_call | solution.py:304
  18.4 0.2 collective-permute-done.4.cmine
  18.6 2.4 %collective-permute-done.5.cother = f32[13,8,128]{2,1,0:T(8,128)S(1)} collective-permute-done((f32[13,8,128]{2,1,0:T(8,128)S(1)}, f32[13,8,128]{2,1,0:T(8,128)S(1)}, u32[]{:S(2)}, u32[]{:S(2)}) %collective-permute-start.5) | collective-permute-done | bytes 53280 | tf_op jit(solution)/shard_map/ppermute | solution.py:295
  21.0 0.0 collective-permute-done.2.mine
  21.0 0.0 collective-permute-done.3.other
  21.0 3.9 %shard_map.45 = (f32[15,2,144,128]{3,2,1,0:T(8,128)S(1)}, f32[16,2,128,128]{3,2,1,0:T(8,128)S(1)}, f32[16,2,128,128]{3,2,1,0:T(8,128)S(1)}, f32[16,64,128]{2,1,0...) custom-call(f32[16,64,128]{2,1,0:T(8,128)S(1)} %get-tuple-element.19, ...), custom_call_target="tpu_custom_call", output_to_operand_aliasing={{0}: (8, {}), {1}: (9, {}), {2}: (10, {}), {3}: (11, {}), {... | custom-call | flops 10000000 | bytes 1000000 | tf_op jit(solution)/shard_map/pallas_call | solution.py:340
Async XLA Ops:
  1.9 19.1 %collective-permute-start.2 = (f32[480,128]{1,0:T(8,128)S(1)}, f32[480,128]{1,0:T(8,128)S(1)}, u32[]{:S(2)}, u32[]{:S(2)}) collective-permute-start(f32[480,128]{1,0:T(8,128)S(1)} %get-tuple-element.25), channel_id=1, source_target_pairs={{0,8},{8,0},{16,24},{24,16},{1,9},{9,1},{17,25},{25,17},{2,10},{10... | collective-permute-start | bytes 737288 | tf_op jit(solution)/shard_map/ppermute | solution.py:295
  4.9 16.1 %collective-permute-start.3 = (f32[480,128]{1,0:T(8,128)S(1)}, f32[480,128]{1,0:T(8,128)S(1)}, u32[]{:S(2)}, u32[]{:S(2)}) collective-permute-start(f32[480,128]{1,0:T(8,128)S(1)} %get-tuple-element.26), channel_id=1, source_target_pairs={{8,16},{16,8},{24,0},{0,24},{9,17},{17,9},{25,1},{1,25},{10,18},{1... | collective-permute-start | bytes 737288 | tf_op jit(solution)/shard_map/ppermute | solution.py:295
  6.9 3.8 %collective-permute-start = (f32[4,64,128]{2,1,0:T(8,128)S(1)}, f32[4,64,128]{2,1,0:T(8,128)S(1)}, u32[]{:S(2)}, u32[]{:S(2)}) collective-permute-start(f32[4,64,128]{2,1,0:T(8,128)S(1)} %get-tuple-element.21), channel_id=1, source_target_pairs={{0,1},{1,0},{2,3},{3,2},{4,5},{5,4},{6,7},{7,6},{8,9},{9,8},{10,11... | collective-permute-start | bytes 393224 | tf_op jit(solution)/shard_map/ppermute | solution.py:295
  7.0 7.0 %collective-permute-start.1 = (f32[4,64,128]{2,1,0:T(8,128)S(1)}, f32[4,64,128]{2,1,0:T(8,128)S(1)}, u32[]{:S(2)}, u32[]{:S(2)}) collective-permute-start(f32[4,64,128]{2,1,0:T(8,128)S(1)} %get-tuple-element.22), channel_id=1, source_target_pairs={{1,2},{2,1},{3,4},{4,3},{5,6},{6,5},{7,0},{0,7},{9,10},{10,9},{11,... | collective-permute-start | bytes 393224 | tf_op jit(solution)/shard_map/ppermute | solution.py:295
  14.4 4.2 %collective-permute-start.4 = (f32[13,8,128]{2,1,0:T(8,128)S(1)}, f32[13,8,128]{2,1,0:T(8,128)S(1)}, u32[]{:S(2)}, u32[]{:S(2)}) collective-permute-start(f32[13,8,128]{2,1,0:T(8,128)S(1)} %get-tuple-element.27), channel_id=1, source_target_pairs={{0,8},{8,0},{16,24},{24,16},{1,9},{9,1},{17,25},{25,17},{2,10},{10... | collective-permute-start | bytes 159752 | tf_op jit(solution)/shard_map/ppermute | solution.py:295
  15.9 5.0 %collective-permute-start.5 = (f32[13,8,128]{2,1,0:T(8,128)S(1)}, f32[13,8,128]{2,1,0:T(8,128)S(1)}, u32[]{:S(2)}, u32[]{:S(2)}) collective-permute-start(f32[13,8,128]{2,1,0:T(8,128)S(1)} %get-tuple-element.28), channel_id=1, source_target_pairs={{8,16},{16,8},{24,0},{0,24},{9,17},{17,9},{25,1},{1,25},{10,18},{1... | collective-permute-start | bytes 159752 | tf_op jit(solution)/shard_map/ppermute | solution.py:295

commit v6 on v5

--- a/solution.py
+++ b/solution.py
@@ -40,22 +40,24 @@
             at += d
         self.row_end = at
         self.row_len = up8(at) + self.margin
-        self.col_at, self.col_tiles = self.fit([((arr, z), d) for arr, z, d in self.fields])
+        items = [((arr, z, r), d) for arr, z, d in self.fields for r in range(0, rows, SUB)]
+        self.col_at, self.col_tiles = self.fit(items, both=True)
         items = []
         for arr, z, d in self.fields:
             for k in range(-(-(d - 1) // SUB)):
                 items.append(((arr, z, k), 2 * (d - 1 - SUB * k)))
         self.corner_at, self.corner_tiles = self.fit(items)
 
-    def fit(self, items):
-        room, where = [], {}
+    def fit(self, items, both=False):
+        room, widest, where = [], [], {}
         for key, width in sorted(items, key=lambda item: -item[1]):
             for tile, used in enumerate(room):
-                if used + width <= self.cols:
+                if used + (widest[tile] if both else width) <= self.cols:
                     break
             else:
                 tile = len(room)
                 room.append(0)
+                widest.append(width)
             where[key] = (tile, room[tile])
             room[tile] += width
         return where, len(room)
@@ -101,22 +103,24 @@
     n = plan.cols
     odd = odd_on("gy")
     lane = lanes_of((SUB, n))
+    reach = {(arr, z): d for arr, z, d in plan.fields}
     for tile in range(plan.col_tiles):
-        inside = [f for f in plan.fields if plan.col_at[f[0], f[1]][0] == tile]
-        inside.sort(key=lambda f: plan.col_at[f[0], f[1]][1])
-        for r in range(0, plan.rows, SUB):
-            one, two = None, None
-            for arr, z, d in inside:
-                at = plan.col_at[arr, z][1]
-                x = (dens, cot)[arr][z, r : r + SUB, :]
-                a, b = shift(x, at), shift(x, at + d)
-                if one is None:
-                    one, two = a, b
-                else:
-                    here = lane >= at
-                    one, two = jnp.where(here, a, one), jnp.where(here, b, two)
-            ours[tile, r : r + SUB, :] = jnp.where(odd, one, two)
-            theirs[tile, r : r + SUB, :] = jnp.where(odd, two, one)
+        inside = [(at, key) for key, (t, at) in plan.col_at.items() if t == tile]
+        one, two = None, None
+        for at, (arr, z, r) in sorted(inside):
+            d = reach[arr, z]
+            x = shift((dens, cot)[arr][z, r : r + SUB, :], at)
+            one = x if one is None else jnp.where(lane >= at, x, one)
+            two = x if two is None else jnp.where((lane >= at - d) & (lane < at), x, two)
+        ours[tile] = jnp.where(odd, one, two)
+        theirs[tile] = jnp.where(odd, two, one)
+
+
+def merge(odd, mine, other, at):
+    n = mine.shape[1]
+    lane = lanes_of(mine.shape)
+    after = (lane >= at) & (lane < at + n // 2) if at <= n // 2 else (lane >= at) | (lane < at - n // 2)
+    return jnp.where(after != odd, mine, other)
 
 
 def pack_corners(plan, mine, other, ours, theirs):
@@ -128,15 +132,13 @@
     for (arr, z, k), (tile, at) in order:
         d = reach[arr, z]
         w = d - 1 - SUB * k
-        ctile, cat = plan.col_at[arr, z]
         for way in range(2):
             r = SUB * k if way == 0 else plan.rows - SUB * (k + 1)
-            x, y = mine[ctile, r : r + SUB, :], other[ctile, r : r + SUB, :]
-            a = shift(jnp.where(odd_y, x, y), at - (cat + d - w))
-            b = shift(jnp.where(odd_y, y, x), at + w - cat)
-            both = jnp.where(lane >= at + w, b, a)
+            ctile, cat = plan.col_at[arr, z, r]
+            x = merge(odd_y, mine[ctile], other[ctile], cat)
+            x = shift(x, at + w - cat)
             prev = out[way][tile]
-            out[way][tile] = both if prev is None else jnp.where(lane >= at, both, prev)
+            out[way][tile] = x if prev is None else jnp.where(lane >= at, x, prev)
     for tile in range(plan.corner_tiles):
         ours[tile] = jnp.where(odd_x, out[0][tile], out[1][tile])
         theirs[tile] = jnp.where(odd_x, out[1][tile], out[0][tile])
@@ -187,15 +189,13 @@
 def inner_body(plan, dens, mine, other, dens_side, cot_side, power, slope, weight, da, printed):
     nz, rows, n, top = plan.nz, plan.rows, plan.cols, plan.halo
     lane = lanes_of((SUB, n))
-    low = lane < n // 2
     sides = (dens_side, cot_side)
     odd = odd_on("gy")
     for arr, z, d in plan.fields:
-        tile, at = plan.col_at[arr, z]
         for r in range(0, rows, SUB):
-            x, y = mine[tile, r : r + SUB, :], other[tile, r : r + SUB, :]
-            x, y = shift(jnp.where(odd, x, y), -(at + d)), shift(jnp.where(odd, y, x), -at)
-            sides[arr][z, r : r + SUB, :] = jnp.where(low, y, x)
+            tile, at = plan.col_at[arr, z, r]
+            x = merge(odd, mine[tile], other[tile], at)
+            sides[arr][z, r : r + SUB, :] = shift(x, -at)
     margin = jnp.ones((SUB, n), jnp.float32)
     out = (power, slope, weight, da, printed)
     for z in range(nz):
@@ -327,7 +327,7 @@
         compiler_params=pltpu.CompilerParams(vmem_limit_bytes=4 << 20),
     )(*[pltpu.with_memory_space_constraint(x, pltpu.HBM) for x in (density, cotangent)])
     near_rows = swap("gx", ours, theirs)
-    ours, theirs = call(part(pack_columns, plan), [(plan.col_tiles, rows, cols)] * 2, density, cotangent)
+    ours, theirs = call(part(pack_columns, plan), [(plan.col_tiles, SUB, cols)] * 2, density, cotangent)
     sides = swap("gy", ours, theirs)
     ours, theirs = call(part(pack_corners, plan), [(plan.corner_tiles, SUB, cols)] * 2, *sides)
     corners = swap("gx", ours, theirs)

time: 25.1 us -> 24.8 us (0.988)
  Pallas kernels: 8.01 us -> 7.67 us
    pallas_call x3, Pallas kernels: 2.84 us -> 2.5 us  [call(): pl.pallas_call(body, out_shape=[pltpu.VMEM(s, jnp.float32) for s in outs]...]
  transfers between devices with their start and end apart: 6 -> 6, of which waited for: 3 -> 3; matrix products, arithmetic and copies ran while one was open for 0% -> 0% of each run, Pallas kernels for 11% -> 10%
where the time goes in v6:
time: 24.8 us; the launch traced here: 24.6 us
  starting transfers between devices  10.3 us (42%)
  Pallas kernels  7.67 us (31%)
  waiting for transfers between devices  5.97 us (24%)
  between operations  0.67 us (3%)
    ppermute x6, starting transfers between devices, swap(): lax.ppermute(x, axis, [p for a, b in ends for p in ((a, b), (b, a))])  10.3 us
    ppermute x6, waiting for transfers between devices, swap(): lax.ppermute(x, axis, [p for a, b in ends for p in ((a, b), (b, a))])  5.97 us
    pallas_call x1, Pallas kernels, shards(): pl.pallas_call(part(outer_body, plan), out_shape=[pltpu.VMEM(s, jnp.float...  3.94 us
    pallas_call x3, Pallas kernels, call(): pl.pallas_call(body, out_shape=[pltpu.VMEM(s, jnp.float32) for s in outs]...  2.5 us
    pallas_call x1, Pallas kernels, shards(): pl.pallas_call(part(fetch, plan), out_shape=[pltpu.VMEM(s, jnp.float32) f...  1.23 us
  transfers between devices with their start and end apart: 6, of which 3 were waited for; matrix products, arithmetic and copies ran while one was open for 0% of the time, Pallas kernels for 10%

profile of v6, /device:TPU:0, one launch (start us, length us, event | category | flops | bytes accessed | tf_op | source)
XLA Modules:
  0.0 24.6 jit_solution(10136741022957245052)
XLA Ops:
  0.6 1.2 %shard_map.41 = (f32[16,64,128]{2,1,0:T(8,128)S(1)}, f32[16,64,128]{2,1,0:T(8,128)S(1)}, f32[480,128]{1,0:T(8,128)S(1)}, f32[480,128]{1,0:T(8,128)S(1)}) custom-call(f32[16,64,128]{2,1,0:T(8,128)} %dens_in.1, f32[16,64,128]{2,1,0:T(8,128)} %cot_in.1), custom_call_target="tpu_custom_call" | custom-call | flops 100000 | bytes 1000000 | tf_op jit(solution)/shard_map/pallas_call | solution.py:320
  1.9 3.0 %collective-permute-start.2 = (f32[480,128]{1,0:T(8,128)S(1)}, f32[480,128]{1,0:T(8,128)S(1)}, u32[]{:S(2)}, u32[]{:S(2)}) collective-permute-start(f32[480,128]{1,0:T(8,128)S(1)} %get-tuple-element.25), channel_id=1, source_target_pairs={{0,8},{8,0},{16,24},{24,16},{1,9},{9,1},{17,25},{25,17},{2,10},{10... | collective-permute-start | bytes 737288 | tf_op jit(solution)/shard_map/ppermute | solution.py:295
  4.9 1.5 %collective-permute-start.3 = (f32[480,128]{1,0:T(8,128)S(1)}, f32[480,128]{1,0:T(8,128)S(1)}, u32[]{:S(2)}, u32[]{:S(2)}) collective-permute-start(f32[480,128]{1,0:T(8,128)S(1)} %get-tuple-element.26), channel_id=1, source_target_pairs={{8,16},{16,8},{24,0},{0,24},{9,17},{17,9},{25,1},{1,25},{10,18},{1... | collective-permute-start | bytes 737288 | tf_op jit(solution)/shard_map/ppermute | solution.py:295
  6.4 0.3 %shard_map.42 = (f32[33,8,128]{2,1,0:T(8,128)S(1)}, f32[33,8,128]{2,1,0:T(8,128)S(1)}) custom-call(f32[16,64,128]{2,1,0:T(8,128)S(1)} %get-tuple-element.19.dens, f32[16,64,128]{2,1,0:T(8,128)S(1)} %get-tuple-element.20.cot), custom_call_target="tpu_custom_call" | custom-call | flops 100000 | bytes 100000 | tf_op jit(solution)/shard_map/pallas_call | solution.py:304
  6.7 0.1 collective-permute-start
  6.8 3.7 %collective-permute-start.1 = (f32[33,8,128]{2,1,0:T(8,128)S(1)}, f32[33,8,128]{2,1,0:T(8,128)S(1)}, u32[]{:S(2)}, u32[]{:S(2)}) collective-permute-start(f32[33,8,128]{2,1,0:T(8,128)S(1)} %get-tuple-element.22), channel_id=1, source_target_pairs={{1,2},{2,1},{3,4},{4,3},{5,6},{6,5},{7,0},{0,7},{9,10},{10,9},{11,... | collective-permute-start | bytes 405512 | tf_op jit(solution)/shard_map/ppermute | solution.py:295
  10.5 0.0 collective-permute-done.mine
  10.5 3.4 %collective-permute-done.1.other = f32[33,8,128]{2,1,0:T(8,128)S(1)} collective-permute-done((f32[33,8,128]{2,1,0:T(8,128)S(1)}, f32[33,8,128]{2,1,0:T(8,128)S(1)}, u32[]{:S(2)}, u32[]{:S(2)}) %collective-permute-start.1) | collective-permute-done | bytes 135200 | tf_op jit(solution)/shard_map/ppermute | solution.py:295
  13.9 0.2 shard_map.44
  14.1 1.6 %collective-permute-start.4 = (f32[13,8,128]{2,1,0:T(8,128)S(1)}, f32[13,8,128]{2,1,0:T(8,128)S(1)}, u32[]{:S(2)}, u32[]{:S(2)}) collective-permute-start(f32[13,8,128]{2,1,0:T(8,128)S(1)} %get-tuple-element.27), channel_id=1, source_target_pairs={{0,8},{8,0},{16,24},{24,16},{1,9},{9,1},{17,25},{25,17},{2,10},{10... | collective-permute-start | bytes 159752 | tf_op jit(solution)/shard_map/ppermute | solution.py:295
  15.7 0.5 %collective-permute-start.5 = (f32[13,8,128]{2,1,0:T(8,128)S(1)}, f32[13,8,128]{2,1,0:T(8,128)S(1)}, u32[]{:S(2)}, u32[]{:S(2)}) collective-permute-start(f32[13,8,128]{2,1,0:T(8,128)S(1)} %get-tuple-element.28), channel_id=1, source_target_pairs={{8,16},{16,8},{24,0},{0,24},{9,17},{17,9},{25,1},{1,25},{10,18},{1... | collective-permute-start | bytes 159752 | tf_op jit(solution)/shard_map/ppermute | solution.py:295
  16.1 2.0 %shard_map.43 = (f32[16,64,128]{2,1,0:T(8,128)S(1)}, f32[16,64,128]{2,1,0:T(8,128)S(1)}, f32[15,2,144,128]{3,2,1,0:T(8,128)S(1)}, f32[16,2,128,128]{3,2,1,0:T(8,...) custom-call(f32[16,64,128]{2,1,0:T(8,128)S(1)} %get-tuple-element.19.dens, ...), custom_call_target="tpu_custom_call" | custom-call | flops 100000 | bytes 100000 | tf_op jit(solution)/shard_map/pallas_call | solution.py:304
  18.1 0.2 collective-permute-done.4.cmine
  18.3 2.4 %collective-permute-done.5.cother = f32[13,8,128]{2,1,0:T(8,128)S(1)} collective-permute-done((f32[13,8,128]{2,1,0:T(8,128)S(1)}, f32[13,8,128]{2,1,0:T(8,128)S(1)}, u32[]{:S(2)}, u32[]{:S(2)}) %collective-permute-start.5) | collective-permute-done | bytes 53280 | tf_op jit(solution)/shard_map/ppermute | solution.py:295
  20.7 0.0 collective-permute-done.2.mine
  20.7 0.0 collective-permute-done.3.other
  20.7 3.9 %shard_map.45 = (f32[15,2,144,128]{3,2,1,0:T(8,128)S(1)}, f32[16,2,128,128]{3,2,1,0:T(8,128)S(1)}, f32[16,2,128,128]{3,2,1,0:T(8,128)S(1)}, f32[16,64,128]{2,1,0...) custom-call(f32[16,64,128]{2,1,0:T(8,128)S(1)} %get-tuple-element.19, ...), custom_call_target="tpu_custom_call", output_to_operand_aliasing={{0}: (8, {}), {1}: (9, {}), {2}: (10, {}), {3}: (11, {}), {... | custom-call | flops 10000000 | bytes 1000000 | tf_op jit(solution)/shard_map/pallas_call | solution.py:340
Async XLA Ops:
  1.9 18.8 %collective-permute-start.2 = (f32[480,128]{1,0:T(8,128)S(1)}, f32[480,128]{1,0:T(8,128)S(1)}, u32[]{:S(2)}, u32[]{:S(2)}) collective-permute-start(f32[480,128]{1,0:T(8,128)S(1)} %get-tuple-element.25), channel_id=1, source_target_pairs={{0,8},{8,0},{16,24},{24,16},{1,9},{9,1},{17,25},{25,17},{2,10},{10... | collective-permute-start | bytes 737288 | tf_op jit(solution)/shard_map/ppermute | solution.py:295
  4.9 15.8 %collective-permute-start.3 = (f32[480,128]{1,0:T(8,128)S(1)}, f32[480,128]{1,0:T(8,128)S(1)}, u32[]{:S(2)}, u32[]{:S(2)}) collective-permute-start(f32[480,128]{1,0:T(8,128)S(1)} %get-tuple-element.26), channel_id=1, source_target_pairs={{8,16},{16,8},{24,0},{0,24},{9,17},{17,9},{25,1},{1,25},{10,18},{1... | collective-permute-start | bytes 737288 | tf_op jit(solution)/shard_map/ppermute | solution.py:295
  6.7 3.8 %collective-permute-start = (f32[33,8,128]{2,1,0:T(8,128)S(1)}, f32[33,8,128]{2,1,0:T(8,128)S(1)}, u32[]{:S(2)}, u32[]{:S(2)}) collective-permute-start(f32[33,8,128]{2,1,0:T(8,128)S(1)} %get-tuple-element.21), channel_id=1, source_target_pairs={{0,1},{1,0},{2,3},{3,2},{4,5},{5,4},{6,7},{7,6},{8,9},{9,8},{10,11... | collective-permute-start | bytes 405512 | tf_op jit(solution)/shard_map/ppermute | solution.py:295
  6.8 7.1 %collective-permute-start.1 = (f32[33,8,128]{2,1,0:T(8,128)S(1)}, f32[33,8,128]{2,1,0:T(8,128)S(1)}, u32[]{:S(2)}, u32[]{:S(2)}) collective-permute-start(f32[33,8,128]{2,1,0:T(8,128)S(1)} %get-tuple-element.22), channel_id=1, source_target_pairs={{1,2},{2,1},{3,4},{4,3},{5,6},{6,5},{7,0},{0,7},{9,10},{10,9},{11,... | collective-permute-start | bytes 405512 | tf_op jit(solution)/shard_map/ppermute | solution.py:295
  14.1 4.2 %collective-permute-start.4 = (f32[13,8,128]{2,1,0:T(8,128)S(1)}, f32[13,8,128]{2,1,0:T(8,128)S(1)}, u32[]{:S(2)}, u32[]{:S(2)}) collective-permute-start(f32[13,8,128]{2,1,0:T(8,128)S(1)} %get-tuple-element.27), channel_id=1, source_target_pairs={{0,8},{8,0},{16,24},{24,16},{1,9},{9,1},{17,25},{25,17},{2,10},{10... | collective-permute-start | bytes 159752 | tf_op jit(solution)/shard_map/ppermute | solution.py:295
  15.7 5.0 %collective-permute-start.5 = (f32[13,8,128]{2,1,0:T(8,128)S(1)}, f32[13,8,128]{2,1,0:T(8,128)S(1)}, u32[]{:S(2)}, u32[]{:S(2)}) collective-permute-start(f32[13,8,128]{2,1,0:T(8,128)S(1)} %get-tuple-element.28), channel_id=1, source_target_pairs={{8,16},{16,8},{24,0},{0,24},{9,17},{17,9},{25,1},{1,25},{10,18},{1... | collective-permute-start | bytes 159752 | tf_op jit(solution)/shard_map/ppermute | solution.py:295

commit v7 on v6

--- a/solution.py
+++ b/solution.py
@@ -45,8 +45,14 @@
         items = []
         for arr, z, d in self.fields:
             for k in range(-(-(d - 1) // SUB)):
-                items.append(((arr, z, k), 2 * (d - 1 - SUB * k)))
-        self.corner_at, self.corner_tiles = self.fit(items)
+                for half in range(2):
+                    if (w := self.corner_width(d, k, half)) > 0:
+                        items.append(((arr, z, k, half), 2 * w))
+        self.corner_at, bins = self.fit(items)
+        self.corner_tiles = -(-bins // 2)
+
+    def corner_width(self, d, k, half):
+        return d - 1 - SUB * k - SUB // 2 * half
 
     def fit(self, items, both=False):
         room, widest, where = [], [], {}
@@ -126,22 +132,26 @@
 def pack_corners(plan, mine, other, ours, theirs):
     lane = lanes_of((SUB, plan.cols))
     odd_x, odd_y = odd_on("gx"), odd_on("gy")
-    out = [[None] * plan.corner_tiles, [None] * plan.corner_tiles]
-    order = sorted(plan.corner_at.items(), key=lambda item: item[1][1])
+    bins = 2 * plan.corner_tiles
+    out = [[jnp.zeros(lane.shape, jnp.float32)] * bins, [jnp.zeros(lane.shape, jnp.float32)] * bins]
     reach = {(arr, z): d for arr, z, d in plan.fields}
-    for (arr, z, k), (tile, at) in order:
-        d = reach[arr, z]
-        w = d - 1 - SUB * k
+    for (arr, z, k, half), (place, at) in sorted(plan.corner_at.items(), key=lambda item: item[1][1]):
+        w = plan.corner_width(reach[arr, z], k, half)
         for way in range(2):
             r = SUB * k if way == 0 else plan.rows - SUB * (k + 1)
             ctile, cat = plan.col_at[arr, z, r]
             x = merge(odd_y, mine[ctile], other[ctile], cat)
-            x = shift(x, at + w - cat)
-            prev = out[way][tile]
-            out[way][tile] = x if prev is None else jnp.where(lane >= at, x, prev)
+            x = turn(shift(x, at + w - cat), half != way, place % 2)
+            out[way][place] = x if at == 0 else jnp.where(lane >= at, x, out[way][place])
+    low = lax.broadcasted_iota(jnp.int32, lane.shape, 0) < SUB // 2
     for tile in range(plan.corner_tiles):
-        ours[tile] = jnp.where(odd_x, out[0][tile], out[1][tile])
-        theirs[tile] = jnp.where(odd_x, out[1][tile], out[0][tile])
+        one, two = [jnp.where(low, out[way][2 * tile], out[way][2 * tile + 1]) for way in range(2)]
+        ours[tile] = jnp.where(odd_x, one, two)
+        theirs[tile] = jnp.where(odd_x, two, one)
+
+
+def turn(x, src, dst):
+    return x if bool(src) == bool(dst) else pltpu.roll(x, SUB // 2, 0)
 
 
 def cross(ref, z, r, lane):
@@ -163,8 +173,8 @@
     if total is None:
         level = jnp.ones_like(density)
     else:
-        lg = jnp.log(total)
-        level = jnp.exp2(lg * jnp.float32(1.0 / (root_q * math.log(2.0))))
+        lg = lax.log2(total)
+        level = jnp.exp2(lg * jnp.float32(1.0 / root_q))
     diff = density - level
     square = diff * diff + smooth_eps
     inv = lax.rsqrt(square)
@@ -179,7 +189,7 @@
         if z > 0 or half == 0:
             slope[z, half, r : r + SUB, :] = jnp.float32(0.5 * power_p / root_q) * (p16 * (p2 * value))
         if z > 0:
-            ratio = jnp.exp2(lg * jnp.float32((1.0 / root_q - 1.0) / math.log(2.0)))
+            ratio = jnp.exp2(lg * jnp.float32(1.0 / root_q - 1.0))
             weight[z, half, r : r + SUB, :] = (1.0 + u) * ratio
         if half == 0 and top <= r < top + rows:
             printed[z, r - top : r - top + SUB, :] = value
@@ -217,6 +227,7 @@
 ):
     nz, rows, n, top = plan.nz, plan.rows, plan.cols, plan.halo
     lane = lanes_of((SUB, n))
+    low = lax.broadcasted_iota(jnp.int32, lane.shape, 0) < SUB // 2
     full = top + rows + top
     reach = {(arr, z): d for arr, z, d in plan.fields}
     odd = odd_on("gx")
@@ -243,12 +254,17 @@
             at = at + d - SUB * (k + 1) if before else at + SUB * k
             x, y = mine[at : at + SUB, :], other[at : at + SUB, :]
             return jnp.where(odd, x, y) if before else jnp.where(odd, y, x)
-        w = d - 1 - SUB * k
-        if w <= 0:
-            return jnp.ones((SUB, n), jnp.float32)
-        tile, cor = plan.corner_at[arr, z, k]
-        x, y = cmine[tile], cother[tile]
-        return shift(jnp.where(odd, x, y) if before else jnp.where(odd, y, x), -(cor + w))
+        found = []
+        for part in range(2):
+            w = plan.corner_width(d, k, part)
+            if w > 0:
+                place, cor = plan.corner_at[arr, z, k, part]
+                x, y = cmine[place // 2], cother[place // 2]
+                x = jnp.where(odd, x, y) if before else jnp.where(odd, y, x)
+                found.append(turn(shift(x, -(cor + w)), place % 2, part != before))
+        if len(found) < 2:
+            return found[0] if found else jnp.ones((SUB, n), jnp.float32)
+        return jnp.where(low != before, found[0], found[1])
 
     def tiles(depth):
         return range(top - up8(depth), top + rows + up8(depth), SUB)

time: 24.8 us -> 24.9 us (level)
  transfers between devices with their start and end apart: 6 -> 6, of which waited for: 3 -> 3; matrix products, arithmetic and copies ran while one was open for 0% -> 0% of each run, Pallas kernels for 10% -> 11%
where the time goes in v7:
time: 24.9 us; the launch traced here: 24.7 us
  starting transfers between devices  10.3 us (41%)
  Pallas kernels  7.85 us (32%)
  waiting for transfers between devices  5.89 us (24%)
  between operations  0.67 us (3%)
    ppermute x6, starting transfers between devices, swap(): lax.ppermute(x, axis, [p for a, b in ends for p in ((a, b), (b, a))])  10.3 us
    ppermute x6, waiting for transfers between devices, swap(): lax.ppermute(x, axis, [p for a, b in ends for p in ((a, b), (b, a))])  5.89 us
    pallas_call x1, Pallas kernels, shards(): pl.pallas_call(part(outer_body, plan), out_shape=[pltpu.VMEM(s, jnp.float...  4.01 us
    pallas_call x3, Pallas kernels, call(): pl.pallas_call(body, out_shape=[pltpu.VMEM(s, jnp.float32) for s in outs]...  2.61 us
    pallas_call x1, Pallas kernels, shards(): pl.pallas_call(part(fetch, plan), out_shape=[pltpu.VMEM(s, jnp.float32) f...  1.23 us
  transfers between devices with their start and end apart: 6, of which 3 were waited for; matrix products, arithmetic and copies ran while one was open for 0% of the time, Pallas kernels for 11%

profile of v7, /device:TPU:0, one launch (start us, length us, event | category | flops | bytes accessed | tf_op | source)
XLA Modules:
  0.0 24.7 jit_solution(2844141297754727291)
XLA Ops:
  0.6 1.2 %shard_map.41 = (f32[16,64,128]{2,1,0:T(8,128)S(1)}, f32[16,64,128]{2,1,0:T(8,128)S(1)}, f32[480,128]{1,0:T(8,128)S(1)}, f32[480,128]{1,0:T(8,128)S(1)}) custom-call(f32[16,64,128]{2,1,0:T(8,128)} %dens_in.1, f32[16,64,128]{2,1,0:T(8,128)} %cot_in.1), custom_call_target="tpu_custom_call" | custom-call | flops 100000 | bytes 1000000 | tf_op jit(solution)/shard_map/pallas_call | solution.py:336
  1.9 3.0 %collective-permute-start.2 = (f32[480,128]{1,0:T(8,128)S(1)}, f32[480,128]{1,0:T(8,128)S(1)}, u32[]{:S(2)}, u32[]{:S(2)}) collective-permute-start(f32[480,128]{1,0:T(8,128)S(1)} %get-tuple-element.25), channel_id=1, source_target_pairs={{0,8},{8,0},{16,24},{24,16},{1,9},{9,1},{17,25},{25,17},{2,10},{10... | collective-permute-start | bytes 737288 | tf_op jit(solution)/shard_map/ppermute | solution.py:311
  4.9 1.5 %collective-permute-start.3 = (f32[480,128]{1,0:T(8,128)S(1)}, f32[480,128]{1,0:T(8,128)S(1)}, u32[]{:S(2)}, u32[]{:S(2)}) collective-permute-start(f32[480,128]{1,0:T(8,128)S(1)} %get-tuple-element.26), channel_id=1, source_target_pairs={{8,16},{16,8},{24,0},{0,24},{9,17},{17,9},{25,1},{1,25},{10,18},{1... | collective-permute-start | bytes 737288 | tf_op jit(solution)/shard_map/ppermute | solution.py:311
  6.4 0.3 %shard_map.42 = (f32[33,8,128]{2,1,0:T(8,128)S(1)}, f32[33,8,128]{2,1,0:T(8,128)S(1)}) custom-call(f32[16,64,128]{2,1,0:T(8,128)S(1)} %get-tuple-element.19.dens, f32[16,64,128]{2,1,0:T(8,128)S(1)} %get-tuple-element.20.cot), custom_call_target="tpu_custom_call" | custom-call | flops 100000 | bytes 100000 | tf_op jit(solution)/shard_map/pallas_call | solution.py:320
  6.7 0.1 collective-permute-start
  6.8 3.7 %collective-permute-start.1 = (f32[33,8,128]{2,1,0:T(8,128)S(1)}, f32[33,8,128]{2,1,0:T(8,128)S(1)}, u32[]{:S(2)}, u32[]{:S(2)}) collective-permute-start(f32[33,8,128]{2,1,0:T(8,128)S(1)} %get-tuple-element.22), channel_id=1, source_target_pairs={{1,2},{2,1},{3,4},{4,3},{5,6},{6,5},{7,0},{0,7},{9,10},{10,9},{11,... | collective-permute-start | bytes 405512 | tf_op jit(solution)/shard_map/ppermute | solution.py:311
  10.5 0.0 collective-permute-done.mine
  10.5 3.4 %collective-permute-done.1.other = f32[33,8,128]{2,1,0:T(8,128)S(1)} collective-permute-done((f32[33,8,128]{2,1,0:T(8,128)S(1)}, f32[33,8,128]{2,1,0:T(8,128)S(1)}, u32[]{:S(2)}, u32[]{:S(2)}) %collective-permute-start.1) | collective-permute-done | bytes 135200 | tf_op jit(solution)/shard_map/ppermute | solution.py:311
  13.9 0.3 %shard_map.44 = (f32[11,8,128]{2,1,0:T(8,128)S(1)}, f32[11,8,128]{2,1,0:T(8,128)S(1)}) custom-call(f32[33,8,128]{2,1,0:T(8,128)S(1)} %collective-permute-done.mine, f32[33,8,128]{2,1,0:T(8,128)S(1)} %collective-permute-done.1.other), custom_call_target="tpu_custom_call" | custom-call | flops 100000 | bytes 100000 | tf_op jit(solution)/shard_map/pallas_call | solution.py:320
  14.2 1.6 %collective-permute-start.4 = (f32[11,8,128]{2,1,0:T(8,128)S(1)}, f32[11,8,128]{2,1,0:T(8,128)S(1)}, u32[]{:S(2)}, u32[]{:S(2)}) collective-permute-start(f32[11,8,128]{2,1,0:T(8,128)S(1)} %get-tuple-element.27), channel_id=1, source_target_pairs={{0,8},{8,0},{16,24},{24,16},{1,9},{9,1},{17,25},{25,17},{2,10},{10... | collective-permute-start | bytes 135176 | tf_op jit(solution)/shard_map/ppermute | solution.py:311
  15.8 0.5 %collective-permute-start.5 = (f32[11,8,128]{2,1,0:T(8,128)S(1)}, f32[11,8,128]{2,1,0:T(8,128)S(1)}, u32[]{:S(2)}, u32[]{:S(2)}) collective-permute-start(f32[11,8,128]{2,1,0:T(8,128)S(1)} %get-tuple-element.28), channel_id=1, source_target_pairs={{8,16},{16,8},{24,0},{0,24},{9,17},{17,9},{25,1},{1,25},{10,18},{1... | collective-permute-start | bytes 135176 | tf_op jit(solution)/shard_map/ppermute | solution.py:311
  16.3 2.0 %shard_map.43 = (f32[16,64,128]{2,1,0:T(8,128)S(1)}, f32[16,64,128]{2,1,0:T(8,128)S(1)}, f32[15,2,144,128]{3,2,1,0:T(8,128)S(1)}, f32[16,2,128,128]{3,2,1,0:T(8,...) custom-call(f32[16,64,128]{2,1,0:T(8,128)S(1)} %get-tuple-element.19.dens, ...), custom_call_target="tpu_custom_call" | custom-call | flops 100000 | bytes 100000 | tf_op jit(solution)/shard_map/pallas_call | solution.py:320
  18.2 0.1 collective-permute-done.4.cmine
  18.3 2.4 %collective-permute-done.5.cother = f32[11,8,128]{2,1,0:T(8,128)S(1)} collective-permute-done((f32[11,8,128]{2,1,0:T(8,128)S(1)}, f32[11,8,128]{2,1,0:T(8,128)S(1)}, u32[]{:S(2)}, u32[]{:S(2)}) %collective-permute-start.5) | collective-permute-done | bytes 45088 | tf_op jit(solution)/shard_map/ppermute | solution.py:311
  20.7 0.0 collective-permute-done.2.mine
  20.7 0.0 collective-permute-done.3.other
  20.7 4.0 %shard_map.45 = (f32[15,2,144,128]{3,2,1,0:T(8,128)S(1)}, f32[16,2,128,128]{3,2,1,0:T(8,128)S(1)}, f32[16,2,128,128]{3,2,1,0:T(8,128)S(1)}, f32[16,64,128]{2,1,0...) custom-call(f32[16,64,128]{2,1,0:T(8,128)S(1)} %get-tuple-element.19, ...), custom_call_target="tpu_custom_call", output_to_operand_aliasing={{0}: (8, {}), {1}: (9, {}), {2}: (10, {}), {3}: (11, {}), {... | custom-call | flops 10000000 | bytes 1000000 | tf_op jit(solution)/shard_map/pallas_call | solution.py:356
Async XLA Ops:
  1.9 18.9 %collective-permute-start.2 = (f32[480,128]{1,0:T(8,128)S(1)}, f32[480,128]{1,0:T(8,128)S(1)}, u32[]{:S(2)}, u32[]{:S(2)}) collective-permute-start(f32[480,128]{1,0:T(8,128)S(1)} %get-tuple-element.25), channel_id=1, source_target_pairs={{0,8},{8,0},{16,24},{24,16},{1,9},{9,1},{17,25},{25,17},{2,10},{10... | collective-permute-start | bytes 737288 | tf_op jit(solution)/shard_map/ppermute | solution.py:311
  4.9 15.8 %collective-permute-start.3 = (f32[480,128]{1,0:T(8,128)S(1)}, f32[480,128]{1,0:T(8,128)S(1)}, u32[]{:S(2)}, u32[]{:S(2)}) collective-permute-start(f32[480,128]{1,0:T(8,128)S(1)} %get-tuple-element.26), channel_id=1, source_target_pairs={{8,16},{16,8},{24,0},{0,24},{9,17},{17,9},{25,1},{1,25},{10,18},{1... | collective-permute-start | bytes 737288 | tf_op jit(solution)/shard_map/ppermute | solution.py:311
  6.7 3.8 %collective-permute-start = (f32[33,8,128]{2,1,0:T(8,128)S(1)}, f32[33,8,128]{2,1,0:T(8,128)S(1)}, u32[]{:S(2)}, u32[]{:S(2)}) collective-permute-start(f32[33,8,128]{2,1,0:T(8,128)S(1)} %get-tuple-element.21), channel_id=1, source_target_pairs={{0,1},{1,0},{2,3},{3,2},{4,5},{5,4},{6,7},{7,6},{8,9},{9,8},{10,11... | collective-permute-start | bytes 405512 | tf_op jit(solution)/shard_map/ppermute | solution.py:311
  6.8 7.1 %collective-permute-start.1 = (f32[33,8,128]{2,1,0:T(8,128)S(1)}, f32[33,8,128]{2,1,0:T(8,128)S(1)}, u32[]{:S(2)}, u32[]{:S(2)}) collective-permute-start(f32[33,8,128]{2,1,0:T(8,128)S(1)} %get-tuple-element.22), channel_id=1, source_target_pairs={{1,2},{2,1},{3,4},{4,3},{5,6},{6,5},{7,0},{0,7},{9,10},{10,9},{11,... | collective-permute-start | bytes 405512 | tf_op jit(solution)/shard_map/ppermute | solution.py:311
  14.2 4.1 %collective-permute-start.4 = (f32[11,8,128]{2,1,0:T(8,128)S(1)}, f32[11,8,128]{2,1,0:T(8,128)S(1)}, u32[]{:S(2)}, u32[]{:S(2)}) collective-permute-start(f32[11,8,128]{2,1,0:T(8,128)S(1)} %get-tuple-element.27), channel_id=1, source_target_pairs={{0,8},{8,0},{16,24},{24,16},{1,9},{9,1},{17,25},{25,17},{2,10},{10... | collective-permute-start | bytes 135176 | tf_op jit(solution)/shard_map/ppermute | solution.py:311
  15.8 4.9 %collective-permute-start.5 = (f32[11,8,128]{2,1,0:T(8,128)S(1)}, f32[11,8,128]{2,1,0:T(8,128)S(1)}, u32[]{:S(2)}, u32[]{:S(2)}) collective-permute-start(f32[11,8,128]{2,1,0:T(8,128)S(1)} %get-tuple-element.28), channel_id=1, source_target_pairs={{8,16},{16,8},{24,0},{0,24},{9,17},{17,9},{25,1},{1,25},{10,18},{1... | collective-permute-start | bytes 135176 | tf_op jit(solution)/shard_map/ppermute | solution.py:311

commit v8 on v7

--- a/solution.py
+++ b/solution.py
@@ -271,9 +271,9 @@
 
     for z in range(nz):
         edge = up8(z)
-        for r in tiles(2 * (nz - 1) - z):
-            if top + edge <= r < top + rows - edge:
-                continue
+        left = [r for r in tiles(2 * (nz - 1) - z) if not top + edge <= r < top + rows - edge]
+        m = len(left) // 2
+        for r in [r for pair in zip(left[:m], left[m:]) for r in pair] + left[2 * m :]:
             total = (None, None) if z == 0 else cross(power, z - 1, r, lane)
             for half in range(2):
                 layer(plan, z, r, half, field(0, z, r, half), total[half], *out)

time: 24.9 us -> 24.9 us (level)
  no operation moved by 1% of the time
where the time goes in v8:
time: 24.9 us; the launch traced here: 24.7 us
  starting transfers between devices  10.3 us (41%)
  Pallas kernels  7.82 us (31%)
  waiting for transfers between devices  5.89 us (24%)
  between operations  0.67 us (3%)
    ppermute x6, starting transfers between devices, swap(): lax.ppermute(x, axis, [p for a, b in ends for p in ((a, b), (b, a))])  10.3 us
    ppermute x6, waiting for transfers between devices, swap(): lax.ppermute(x, axis, [p for a, b in ends for p in ((a, b), (b, a))])  5.89 us
    pallas_call x1, Pallas kernels, shards(): pl.pallas_call(part(outer_body, plan), out_shape=[pltpu.VMEM(s, jnp.float...  3.98 us
    pallas_call x3, Pallas kernels, call(): pl.pallas_call(body, out_shape=[pltpu.VMEM(s, jnp.float32) for s in outs]...  2.61 us
    pallas_call x1, Pallas kernels, shards(): pl.pallas_call(part(fetch, plan), out_shape=[pltpu.VMEM(s, jnp.float32) f...  1.23 us
  transfers between devices with their start and end apart: 6, of which 3 were waited for; matrix products, arithmetic and copies ran while one was open for 0% of the time, Pallas kernels for 11%

profile of v8, /device:TPU:0, one launch (start us, length us, event | category | flops | bytes accessed | tf_op | source)
XLA Modules:
  0.0 24.7 jit_solution(4402767854661847078)
XLA Ops:
  0.6 1.2 %shard_map.41 = (f32[16,64,128]{2,1,0:T(8,128)S(1)}, f32[16,64,128]{2,1,0:T(8,128)S(1)}, f32[480,128]{1,0:T(8,128)S(1)}, f32[480,128]{1,0:T(8,128)S(1)}) custom-call(f32[16,64,128]{2,1,0:T(8,128)} %dens_in.1, f32[16,64,128]{2,1,0:T(8,128)} %cot_in.1), custom_call_target="tpu_custom_call" | custom-call | flops 100000 | bytes 1000000 | tf_op jit(solution)/shard_map/pallas_call | solution.py:336
  1.9 3.0 %collective-permute-start.2 = (f32[480,128]{1,0:T(8,128)S(1)}, f32[480,128]{1,0:T(8,128)S(1)}, u32[]{:S(2)}, u32[]{:S(2)}) collective-permute-start(f32[480,128]{1,0:T(8,128)S(1)} %get-tuple-element.25), channel_id=1, source_target_pairs={{0,8},{8,0},{16,24},{24,16},{1,9},{9,1},{17,25},{25,17},{2,10},{10... | collective-permute-start | bytes 737288 | tf_op jit(solution)/shard_map/ppermute | solution.py:311
  4.9 1.5 %collective-permute-start.3 = (f32[480,128]{1,0:T(8,128)S(1)}, f32[480,128]{1,0:T(8,128)S(1)}, u32[]{:S(2)}, u32[]{:S(2)}) collective-permute-start(f32[480,128]{1,0:T(8,128)S(1)} %get-tuple-element.26), channel_id=1, source_target_pairs={{8,16},{16,8},{24,0},{0,24},{9,17},{17,9},{25,1},{1,25},{10,18},{1... | collective-permute-start | bytes 737288 | tf_op jit(solution)/shard_map/ppermute | solution.py:311
  6.4 0.3 %shard_map.42 = (f32[33,8,128]{2,1,0:T(8,128)S(1)}, f32[33,8,128]{2,1,0:T(8,128)S(1)}) custom-call(f32[16,64,128]{2,1,0:T(8,128)S(1)} %get-tuple-element.19.dens, f32[16,64,128]{2,1,0:T(8,128)S(1)} %get-tuple-element.20.cot), custom_call_target="tpu_custom_call" | custom-call | flops 100000 | bytes 100000 | tf_op jit(solution)/shard_map/pallas_call | solution.py:320
  6.7 0.1 collective-permute-start
  6.8 3.7 %collective-permute-start.1 = (f32[33,8,128]{2,1,0:T(8,128)S(1)}, f32[33,8,128]{2,1,0:T(8,128)S(1)}, u32[]{:S(2)}, u32[]{:S(2)}) collective-permute-start(f32[33,8,128]{2,1,0:T(8,128)S(1)} %get-tuple-element.22), channel_id=1, source_target_pairs={{1,2},{2,1},{3,4},{4,3},{5,6},{6,5},{7,0},{0,7},{9,10},{10,9},{11,... | collective-permute-start | bytes 405512 | tf_op jit(solution)/shard_map/ppermute | solution.py:311
  10.5 0.0 collective-permute-done.mine
  10.5 3.4 %collective-permute-done.1.other = f32[33,8,128]{2,1,0:T(8,128)S(1)} collective-permute-done((f32[33,8,128]{2,1,0:T(8,128)S(1)}, f32[33,8,128]{2,1,0:T(8,128)S(1)}, u32[]{:S(2)}, u32[]{:S(2)}) %collective-permute-start.1) | collective-permute-done | bytes 135200 | tf_op jit(solution)/shard_map/ppermute | solution.py:311
  13.9 0.3 %shard_map.44 = (f32[11,8,128]{2,1,0:T(8,128)S(1)}, f32[11,8,128]{2,1,0:T(8,128)S(1)}) custom-call(f32[33,8,128]{2,1,0:T(8,128)S(1)} %collective-permute-done.mine, f32[33,8,128]{2,1,0:T(8,128)S(1)} %collective-permute-done.1.other), custom_call_target="tpu_custom_call" | custom-call | flops 100000 | bytes 100000 | tf_op jit(solution)/shard_map/pallas_call | solution.py:320
  14.2 1.6 %collective-permute-start.4 = (f32[11,8,128]{2,1,0:T(8,128)S(1)}, f32[11,8,128]{2,1,0:T(8,128)S(1)}, u32[]{:S(2)}, u32[]{:S(2)}) collective-permute-start(f32[11,8,128]{2,1,0:T(8,128)S(1)} %get-tuple-element.27), channel_id=1, source_target_pairs={{0,8},{8,0},{16,24},{24,16},{1,9},{9,1},{17,25},{25,17},{2,10},{10... | collective-permute-start | bytes 135176 | tf_op jit(solution)/shard_map/ppermute | solution.py:311
  15.8 0.5 %collective-permute-start.5 = (f32[11,8,128]{2,1,0:T(8,128)S(1)}, f32[11,8,128]{2,1,0:T(8,128)S(1)}, u32[]{:S(2)}, u32[]{:S(2)}) collective-permute-start(f32[11,8,128]{2,1,0:T(8,128)S(1)} %get-tuple-element.28), channel_id=1, source_target_pairs={{8,16},{16,8},{24,0},{0,24},{9,17},{17,9},{25,1},{1,25},{10,18},{1... | collective-permute-start | bytes 135176 | tf_op jit(solution)/shard_map/ppermute | solution.py:311
  16.3 2.0 %shard_map.43 = (f32[16,64,128]{2,1,0:T(8,128)S(1)}, f32[16,64,128]{2,1,0:T(8,128)S(1)}, f32[15,2,144,128]{3,2,1,0:T(8,128)S(1)}, f32[16,2,128,128]{3,2,1,0:T(8,...) custom-call(f32[16,64,128]{2,1,0:T(8,128)S(1)} %get-tuple-element.19.dens, ...), custom_call_target="tpu_custom_call" | custom-call | flops 100000 | bytes 100000 | tf_op jit(solution)/shard_map/pallas_call | solution.py:320
  18.2 0.1 collective-permute-done.4.cmine
  18.3 2.4 %collective-permute-done.5.cother = f32[11,8,128]{2,1,0:T(8,128)S(1)} collective-permute-done((f32[11,8,128]{2,1,0:T(8,128)S(1)}, f32[11,8,128]{2,1,0:T(8,128)S(1)}, u32[]{:S(2)}, u32[]{:S(2)}) %collective-permute-start.5) | collective-permute-done | bytes 45088 | tf_op jit(solution)/shard_map/ppermute | solution.py:311
  20.7 0.0 collective-permute-done.2.mine
  20.7 0.0 collective-permute-done.3.other
  20.7 4.0 %shard_map.45 = (f32[15,2,144,128]{3,2,1,0:T(8,128)S(1)}, f32[16,2,128,128]{3,2,1,0:T(8,128)S(1)}, f32[16,2,128,128]{3,2,1,0:T(8,128)S(1)}, f32[16,64,128]{2,1,0...) custom-call(f32[16,64,128]{2,1,0:T(8,128)S(1)} %get-tuple-element.19, ...), custom_call_target="tpu_custom_call", output_to_operand_aliasing={{0}: (8, {}), {1}: (9, {}), {2}: (10, {}), {3}: (11, {}), {... | custom-call | flops 10000000 | bytes 1000000 | tf_op jit(solution)/shard_map/pallas_call | solution.py:356
Async XLA Ops:
  1.9 18.9 %collective-permute-start.2 = (f32[480,128]{1,0:T(8,128)S(1)}, f32[480,128]{1,0:T(8,128)S(1)}, u32[]{:S(2)}, u32[]{:S(2)}) collective-permute-start(f32[480,128]{1,0:T(8,128)S(1)} %get-tuple-element.25), channel_id=1, source_target_pairs={{0,8},{8,0},{16,24},{24,16},{1,9},{9,1},{17,25},{25,17},{2,10},{10... | collective-permute-start | bytes 737288 | tf_op jit(solution)/shard_map/ppermute | solution.py:311
  4.9 15.8 %collective-permute-start.3 = (f32[480,128]{1,0:T(8,128)S(1)}, f32[480,128]{1,0:T(8,128)S(1)}, u32[]{:S(2)}, u32[]{:S(2)}) collective-permute-start(f32[480,128]{1,0:T(8,128)S(1)} %get-tuple-element.26), channel_id=1, source_target_pairs={{8,16},{16,8},{24,0},{0,24},{9,17},{17,9},{25,1},{1,25},{10,18},{1... | collective-permute-start | bytes 737288 | tf_op jit(solution)/shard_map/ppermute | solution.py:311
  6.7 3.8 %collective-permute-start = (f32[33,8,128]{2,1,0:T(8,128)S(1)}, f32[33,8,128]{2,1,0:T(8,128)S(1)}, u32[]{:S(2)}, u32[]{:S(2)}) collective-permute-start(f32[33,8,128]{2,1,0:T(8,128)S(1)} %get-tuple-element.21), channel_id=1, source_target_pairs={{0,1},{1,0},{2,3},{3,2},{4,5},{5,4},{6,7},{7,6},{8,9},{9,8},{10,11... | collective-permute-start | bytes 405512 | tf_op jit(solution)/shard_map/ppermute | solution.py:311
  6.8 7.1 %collective-permute-start.1 = (f32[33,8,128]{2,1,0:T(8,128)S(1)}, f32[33,8,128]{2,1,0:T(8,128)S(1)}, u32[]{:S(2)}, u32[]{:S(2)}) collective-permute-start(f32[33,8,128]{2,1,0:T(8,128)S(1)} %get-tuple-element.22), channel_id=1, source_target_pairs={{1,2},{2,1},{3,4},{4,3},{5,6},{6,5},{7,0},{0,7},{9,10},{10,9},{11,... | collective-permute-start | bytes 405512 | tf_op jit(solution)/shard_map/ppermute | solution.py:311
  14.2 4.1 %collective-permute-start.4 = (f32[11,8,128]{2,1,0:T(8,128)S(1)}, f32[11,8,128]{2,1,0:T(8,128)S(1)}, u32[]{:S(2)}, u32[]{:S(2)}) collective-permute-start(f32[11,8,128]{2,1,0:T(8,128)S(1)} %get-tuple-element.27), channel_id=1, source_target_pairs={{0,8},{8,0},{16,24},{24,16},{1,9},{9,1},{17,25},{25,17},{2,10},{10... | collective-permute-start | bytes 135176 | tf_op jit(solution)/shard_map/ppermute | solution.py:311
  15.8 4.9 %collective-permute-start.5 = (f32[11,8,128]{2,1,0:T(8,128)S(1)}, f32[11,8,128]{2,1,0:T(8,128)S(1)}, u32[]{:S(2)}, u32[]{:S(2)}) collective-permute-start(f32[11,8,128]{2,1,0:T(8,128)S(1)} %get-tuple-element.28), channel_id=1, source_target_pairs={{8,16},{16,8},{24,0},{0,24},{9,17},{17,9},{25,1},{1,25},{10,18},{1... | collective-permute-start | bytes 135176 | tf_op jit(solution)/shard_map/ppermute | solution.py:311
